TPU v7x, 512 devices: a whole 4x4x16 slice. The times are simulated.
512 devices in a mesh: uly: 8 (over y, core), blk: 64 (over x, z).
Axes of the slice: x: 4, y: 4, z: 16, core: 2. Of those that a mesh axis runs over, the one named last changes fastest.
Arguments:
- query_inputs: bfloat16 [65536, 2048], P(('blk', 'uly')), may hold values from -6 to 6
- key_inputs: bfloat16 [65536, 1024], P(('blk', 'uly')), may hold values from -6 to 6
- value_inputs: bfloat16 [65536, 1024], P(('blk', 'uly')), may hold values from -6 to 6
- forward_out: bfloat16 [65536, 2048], P(('blk', 'uly')), may hold values from -6 to 6
- output_gradient: bfloat16 [65536, 2048], P(('blk', 'uly')), may hold values from -4 to 4
- lse_parts: float32 [65536, 16, 2], P(('blk', 'uly')), may hold values from 3 to 247
- segment_ids: int32 [65536], P(('blk', 'uly')), may hold values from 0 to 127, never falling along the last dimension, each value on 1 to 2048 neighbouring positions
Outputs:
- query_grad: bfloat16 [65536, 2048], P(('blk', 'uly'))
- key_grad: bfloat16 [65536, 1024], P(('blk', 'uly'))
- value_grad: bfloat16 [65536, 1024], P(('blk', 'uly'))
Inputs may be any that keep to these rules, and one draw needn't show every extreme that they name: `segment_ids`: never falls along the sequence; every document holds 1 to 2048 tokens, and some document exactly 2048.
All inputs are finite; a program needn't handle non-finite values.
Results may differ from a plain program's by a relative error of at most 0.0051.
Values may be sent and summed in bfloat16 or wider, within the bound.
No kernel may reach another device: no remote copies, remote signals or barrier semaphores. Data moves between devices by JAX's collectives and lax.ppermute only.
A program may use at most 128 MiB of HBM per device.

v0:
```python
import math

import jax
import jax.numpy as jnp
from jax import lax
from jax.sharding import Mesh
from jax.sharding import PartitionSpec as P

HEAD_SIZE = 128
QUERY_HEADS = 16
KEY_VALUE_HEADS = 8
HOPS = 2
QBLOCK = 512
ULY = ("uly_0", "uly_1")
BLK_ULY = ("blk", "uly_0", "uly_1")


def cut_along(value, dim, count):
    before, after = (value.shape[:dim], value.shape[dim + 1 :])
    return jnp.moveaxis(value.reshape(*before, count, -1, *after), dim, 0)


def joined_along(pieces, dim):
    shape = list(pieces.shape[1:])
    shape[dim] *= pieces.shape[0]
    return jnp.moveaxis(pieces, 0, dim).reshape(shape)


def turned_blocks(pieces, axes, order):
    inside = pieces.shape[1:]
    whole = pieces.reshape(*(lax.axis_size(a) for a in axes), *inside)
    for k in order:
        whole = lax.all_to_all(whole, axes[k], k, k, tiled=True)
    return whole.reshape(-1, *inside)


def core_and_chips(value, groups, order, split_dim, concat_dim):
    count = lax.axis_size(groups[0]) * lax.axis_size(groups[1])
    pieces = cut_along(value, split_dim, count)
    return joined_along(turned_blocks(pieces, groups, order), concat_dim)


def sent_to_all(value, axis):
    count = lax.axis_size(axis)
    return lax.all_to_all(
        jnp.broadcast_to(value[None], (count, *value.shape)), axis, 0, 0, tiled=True
    )


def gathered_copies(value, axis, dim):
    return joined_along(sent_to_all(value, axis), dim)


def from_behind(block, axis, distance):
    devices = range(lax.axis_size(axis))
    route = [(i - distance, i) for i in devices if i - distance in devices]
    return lax.ppermute(block, axis, route)


def merge_parts(partials):
    highest = jnp.max(partials, axis=-1)
    return highest + jnp.log(jnp.sum(jnp.exp(partials - highest[..., None]), axis=-1))


def row_delta(grad_rows, out_rows):
    row_total = grad_rows.shape[0]
    products = grad_rows.astype(jnp.float32) * out_rows.astype(jnp.float32)
    return jnp.sum(products.reshape(row_total, -1, HEAD_SIZE), axis=-1)


def tile_grads(query_blk, grad_blk, lse_blk, delta_blk, key_blk, value_blk, allowed):
    score_scale = 1.0 / math.sqrt(HEAD_SIZE)
    scores = (
        jnp.einsum("mhgd,nhd->hgmn", query_blk, key_blk, preferred_element_type=jnp.float32)
        * score_scale
    )
    weights = jnp.where(allowed, jnp.exp(scores - lse_blk), 0.0)
    value_portion = jnp.einsum(
        "hgmn,mhgd->nhd", weights.astype(jnp.bfloat16), grad_blk, preferred_element_type=jnp.float32
    )
    prob_grad = jnp.einsum(
        "mhgd,nhd->hgmn", grad_blk, value_blk, preferred_element_type=jnp.float32
    )
    score_grad = (weights * (prob_grad - delta_blk)).astype(jnp.bfloat16)
    query_part = (
        jnp.einsum("hgmn,nhd->mhgd", score_grad, key_blk, preferred_element_type=jnp.float32)
        * score_scale
    )
    key_portion = (
        jnp.einsum("hgmn,mhgd->nhd", score_grad, query_blk, preferred_element_type=jnp.float32)
        * score_scale
    )
    return (query_part, key_portion, value_portion)


def per_device(
    query_inputs, key_inputs, value_inputs, forward_out, output_gradient, lse_parts, segment_ids
):
    uly_count = lax.axis_size(ULY)
    blk_place = lax.axis_index("blk")
    tok_local = query_inputs.shape[0]
    row_count = tok_local * uly_count
    group_width = QUERY_HEADS // KEY_VALUE_HEADS
    logsumexp_rows = merge_parts(lse_parts)
    row_deltas = row_delta(output_gradient, forward_out)
    query_loc, grad_loc, key_loc, value_loc = (
        core_and_chips(query_inputs, ("uly_0", "uly_1"), (1, 0), 1, 0),
        core_and_chips(output_gradient, ("uly_0", "uly_1"), (1, 0), 1, 0),
        core_and_chips(key_inputs, ("uly_0", "uly_1"), (1, 0), 1, 0),
        core_and_chips(value_inputs, ("uly_0", "uly_1"), (1, 0), 1, 0),
    )
    lse_loc, delta_loc = (
        lax.all_to_all(logsumexp_rows, ULY, split_axis=1, concat_axis=0, tiled=True),
        lax.all_to_all(row_deltas, ULY, split_axis=1, concat_axis=0, tiled=True),
    )
    ids_loc = gathered_copies(segment_ids, ULY, 0)
    kv_heads = key_loc.shape[1] // HEAD_SIZE
    query_quad = query_loc.reshape(row_count, kv_heads, group_width, HEAD_SIZE)
    gradient_quad = grad_loc.reshape(row_count, kv_heads, group_width, HEAD_SIZE)
    logsumexp_cube = lse_loc.reshape(row_count, kv_heads, group_width).transpose(1, 2, 0)[..., None]
    delta_cube = delta_loc.reshape(row_count, kv_heads, group_width).transpose(1, 2, 0)[..., None]
    key_cube = key_loc.reshape(row_count, kv_heads, HEAD_SIZE)
    value_cube = value_loc.reshape(row_count, kv_heads, HEAD_SIZE)
    rows_per_block = min(QBLOCK, row_count)
    block_total = row_count // rows_per_block
    position = jnp.arange(row_count, dtype=jnp.int32)
    query_parts = []
    key_gradient_running = jnp.zeros((row_count, kv_heads, HEAD_SIZE), jnp.float32)
    value_gradient_running = jnp.zeros((row_count, kv_heads, HEAD_SIZE), jnp.float32)
    for block_index in range(block_total):
        leading_row = block_index * rows_per_block
        finish = leading_row + rows_per_block
        allowed = (position[None, :finish] <= position[leading_row:finish, None]) & (
            ids_loc[None, :finish] == ids_loc[leading_row:finish, None]
        )
        tile_out = tile_grads(
            query_quad[leading_row:finish],
            gradient_quad[leading_row:finish],
            logsumexp_cube[:, :, leading_row:finish],
            delta_cube[:, :, leading_row:finish],
            key_cube[:finish],
            value_cube[:finish],
            allowed,
        )
        query_parts.append(tile_out[0])
        padding = ((0, row_count - finish), (0, 0), (0, 0))
        key_gradient_running = key_gradient_running + jnp.pad(tile_out[1], padding)
        value_gradient_running = value_gradient_running + jnp.pad(tile_out[2], padding)
    query_acc = jnp.concatenate(query_parts, axis=0)
    stacked_kv = jnp.stack([key_loc, value_loc])
    moved_kv = stacked_kv
    moved_ids = ids_loc
    key_parts = []
    for hop_index in range(1, HOPS + 1):
        moved_kv = from_behind(moved_kv, "blk", 1)
        moved_ids = from_behind(moved_ids, "blk", 1)
        live = (blk_place >= hop_index) & (moved_ids[-1] == ids_loc[0])
        moved_key = moved_kv[0].reshape(row_count, kv_heads, HEAD_SIZE)
        moved_value = moved_kv[1].reshape(row_count, kv_heads, HEAD_SIZE)

        def compute_tile(unused):
            query_pieces = []
            key_sum = jnp.zeros((row_count, kv_heads, HEAD_SIZE), jnp.float32)
            value_sum = jnp.zeros((row_count, kv_heads, HEAD_SIZE), jnp.float32)
            for block_index in range(block_total):
                leading_row = block_index * rows_per_block
                finish = leading_row + rows_per_block
                allowed = moved_ids[None, :] == ids_loc[leading_row:finish, None]
                tile_out = tile_grads(
                    query_quad[leading_row:finish],
                    gradient_quad[leading_row:finish],
                    logsumexp_cube[:, :, leading_row:finish],
                    delta_cube[:, :, leading_row:finish],
                    moved_key,
                    moved_value,
                    allowed,
                )
                query_pieces.append(tile_out[0])
                key_sum = key_sum + tile_out[1]
                value_sum = value_sum + tile_out[2]
            stacked = jnp.stack([key_sum.reshape(row_count, -1), value_sum.reshape(row_count, -1)])
            return (jnp.concatenate(query_pieces, axis=0), stacked)

        def skip_tile(unused):
            return (
                jnp.zeros((row_count, kv_heads, group_width, HEAD_SIZE), jnp.float32),
                jnp.zeros((2, row_count, kv_heads * HEAD_SIZE), jnp.float32),
            )

        query_more, key_more = lax.cond(live, compute_tile, skip_tile, 0)
        query_acc = query_acc + query_more
        key_parts.append(key_more)
    carried = jnp.zeros((2, row_count, kv_heads * HEAD_SIZE), jnp.float32)
    for hop_index in range(HOPS, 0, -1):
        carried = from_behind(carried + key_parts[hop_index - 1], "blk", -1)
    key_total = (key_gradient_running.reshape(row_count, -1) + carried[0]).astype(jnp.bfloat16)
    value_total = (value_gradient_running.reshape(row_count, -1) + carried[1]).astype(jnp.bfloat16)
    query_total = query_acc.reshape(row_count, -1).astype(jnp.bfloat16)
    query_grad, key_grad, value_grad = (
        lax.all_to_all(query_total, ULY, split_axis=0, concat_axis=1, tiled=True),
        lax.all_to_all(key_total, ULY, split_axis=0, concat_axis=1, tiled=True),
        lax.all_to_all(value_total, ULY, split_axis=0, concat_axis=1, tiled=True),
    )
    return (query_grad, key_grad, value_grad)


def solution(mesh):
    torus = Mesh(mesh.devices.reshape(4, 2, mesh.shape["blk"]), ("uly_0", "uly_1", "blk"))
    in_specs = (
        P(BLK_ULY, None),
        P(BLK_ULY, None),
        P(BLK_ULY, None),
        P(BLK_ULY, None),
        P(BLK_ULY, None),
        P(BLK_ULY, None, None),
        P(BLK_ULY),
    )
    out_specs = (P(BLK_ULY, None), P(BLK_ULY, None), P(BLK_ULY, None))
    return jax.shard_map(
        per_device, mesh=torus, in_specs=in_specs, out_specs=out_specs, check_vma=False
    )
```

profile of v0, /device:TPU:4, one launch (start us, length us, event | category | flops | bytes accessed | tf_op | source)
XLA Modules:
  0.0 218.7 jit_solution(10454374987237805808)
XLA Ops:
  2.7 3.6 %all-to-all-start.1 = ((bf16[4,2,128,128]{3,2,0,1:T(8,128)(2,1)}), bf16[4,2,128,128]{3,2,0,1:T(8,128)(2,1)S(1)}, u32[]{:S(2)}, u32[]{:S(2)}) async-start(bf16[4,2,128,128]{3,2,0,1:T(8,128)(2,1)} %copy.192), calls=%async_computation.1 | async-start | bytes 524288 | tf_op jit(solution)/shard_map/all_to_all | solution.py:33
  11.1 3.9 %all_to_all.123 = bf16[4,2,128,128]{3,2,0,1:T(8,128)(2,1)S(1)} all-to-all(bf16[4,2,128,128]{3,2,0,1:T(8,128)(2,1)S(1)} %copy.201), channel_id=1, replica_groups=mesh['uly_0'=4,'uly_1'=2,'blk'=64] {'uly_1'}, dimensions={1} | all-to-all | bytes 524288 | tf_op jit(solution)/shard_map/all_to_all | solution.py:33
  15.1 4.1 %all_to_all.124 = bf16[4,2,128,256]{3,2,0,1:T(8,128)(2,1)S(1)} all-to-all(bf16[4,2,128,256]{3,2,0,1:T(8,128)(2,1)S(1)} %copy.196), channel_id=1, replica_groups=mesh['uly_0'=4,'uly_1'=2,'blk'=64] {'uly_1'}, dimensions={1} | all-to-all | bytes 1048576 | tf_op jit(solution)/shard_map/all_to_all | solution.py:33
  19.2 4.1 %all_to_all.125 = bf16[4,2,128,256]{3,2,0,1:T(8,128)(2,1)S(1)} all-to-all(bf16[4,2,128,256]{3,2,0,1:T(8,128)(2,1)S(1)} %copy.205), channel_id=1, replica_groups=mesh['uly_0'=4,'uly_1'=2,'blk'=64] {'uly_1'}, dimensions={1} | all-to-all | bytes 1048576 | tf_op jit(solution)/shard_map/all_to_all | solution.py:33
  24.0 4.5 %all-to-all-start = ((s32[8,1,128]{2,1,0:T(1,128)}), s32[8,1,128]{2,1,0:T(1,128)S(1)}, u32[]{:S(2)}, u32[]{:S(2)}) async-start(s32[8,1,128]{2,1,0:T(1,128)} %broadcast_in_dim.64), calls=%async_computation | async-start | bytes 8192 | tf_op jit(solution)/shard_map/all_to_all | solution.py:45
  29.0 4.6 %all-to-all-done = s32[8,1,128]{2,1,0:T(1,128)S(1)} async-done(((s32[8,1,128]{2,1,0:T(1,128)}), s32[8,1,128]{2,1,0:T(1,128)S(1)}, u32[]{:S(2)}, u32[]{:S(2)}) %all-to-all-start) | async-done | bytes 4128 | tf_op jit(solution)/shard_map/all_to_all | solution.py:45
  33.7 3.3 %all-to-all-start.5 = ((f32[128,8,2]{0,2,1:T(2,128)}), f32[128,8,2]{0,2,1:T(2,128)S(1)}, u32[]{:S(2)}, u32[]{:S(2)}) async-start(f32[128,8,2]{0,2,1:T(2,128)} %bitcast.95), calls=%async_computation.5 | async-start | bytes 16384 | tf_op jit(solution)/shard_map/all_to_all | solution.py:113
  39.4 2.9 %all-to-all-done.5 = f32[128,8,2]{0,2,1:T(2,128)S(1)} async-done(((f32[128,8,2]{0,2,1:T(2,128)}), f32[128,8,2]{0,2,1:T(2,128)S(1)}, u32[]{:S(2)}, u32[]{:S(2)}) %all-to-all-start.5) | async-done | bytes 8224 | tf_op jit(solution)/shard_map/all_to_all | solution.py:113
  42.2 3.3 %all-to-all-start.10 = ((f32[128,8,2]{0,2,1:T(2,128)}), f32[128,8,2]{0,2,1:T(2,128)S(1)}, u32[]{:S(2)}, u32[]{:S(2)}) async-start(f32[128,8,2]{0,2,1:T(2,128)} %bitcast.111), calls=%async_computation.10 | async-start | bytes 16384 | tf_op jit(solution)/shard_map/all_to_all | solution.py:114
  49.3 3.8 %collective-permute-start = (s32[1024]{0:T(1024)S(1)}, s32[1024]{0:T(1024)S(1)}, u32[]{:S(2)}, u32[]{:S(2)}) collective-permute-start(s32[1024]{0:T(1024)S(1)} %bitcast.634), channel_id=1, source_target_pairs={{0,1},{1,2},{2,3},{3,4},{4,5},{5,6},{6,7},{7,8},{8,9},{9,10},{10,1... | collective-permute-start | bytes 12296 | tf_op jit(solution)/shard_map/ppermute | solution.py:57
  53.1 4.7 %all-to-all-start.2 = ((bf16[4,2,128,128]{3,2,1,0:T(8,128)(2,1)}), bf16[4,2,128,128]{3,2,1,0:T(8,128)(2,1)S(1)}, u32[]{:S(2)}, u32[]{:S(2)}) async-start(bf16[4,2,128,128]{3,2,1,0:T(8,128)(2,1)} %copy.193), calls=%async_computation.2 | async-start | bytes 524288 | tf_op jit(solution)/shard_map/all_to_all | solution.py:33
  57.8 6.7 %all-to-all-done.2 = bf16[4,2,128,128]{3,2,1,0:T(8,128)(2,1)S(1)} async-done(((bf16[4,2,128,128]{3,2,1,0:T(8,128)(2,1)}), bf16[4,2,128,128]{3,2,1,0:T(8,128)(2,1)S(1)}, u32[]{:S(2)}, u32[]{:S(2)}) %all-to-all-start.2) | async-done | bytes 262176 | tf_op jit(solution)/shard_map/all_to_all | solution.py:33
  64.5 3.4 %all-to-all-start.7 = ((bf16[4,2,128,128]{3,2,1,0:T(8,128)(2,1)}), bf16[4,2,128,128]{3,2,1,0:T(8,128)(2,1)S(1)}, u32[]{:S(2)}, u32[]{:S(2)}) async-start(bf16[4,2,128,128]{3,2,1,0:T(8,128)(2,1)} %copy.202), calls=%async_computation.7 | async-start | bytes 524288 | tf_op jit(solution)/shard_map/all_to_all | solution.py:33
  69.3 5.3 %all-to-all-done.7 = bf16[4,2,128,128]{3,2,1,0:T(8,128)(2,1)S(1)} async-done(((bf16[4,2,128,128]{3,2,1,0:T(8,128)(2,1)}), bf16[4,2,128,128]{3,2,1,0:T(8,128)(2,1)S(1)}, u32[]{:S(2)}, u32[]{:S(2)}) %all-to-all-start.7) | async-done | bytes 262176 | tf_op jit(solution)/shard_map/all_to_all | solution.py:33
  74.6 3.5 %all-to-all-start.4 = ((bf16[4,2,128,256]{3,2,1,0:T(8,128)(2,1)}), bf16[4,2,128,256]{3,2,1,0:T(8,128)(2,1)S(1)}, u32[]{:S(2)}, u32[]{:S(2)}) async-start(bf16[4,2,128,256]{3,2,1,0:T(8,128)(2,1)} %copy.197), calls=%async_computation.4 | async-start | bytes 1048576 | tf_op jit(solution)/shard_map/all_to_all | solution.py:33
  79.6 3.8 %collective-permute-start.2 = (s32[1024]{0:T(1024)S(1)}, s32[1024]{0:T(1024)S(1)}, u32[]{:S(2)}, u32[]{:S(2)}) collective-permute-start(s32[1024]{0:T(1024)S(1)} %collective-permute-done), channel_id=1, source_target_pairs={{0,1},{1,2},{2,3},{3,4},{4,5},{5,6},{6,7},{7,8},{8,9},{9,10},{10,1... | collective-permute-start | bytes 12296 | tf_op jit(solution)/shard_map/ppermute | solution.py:57
  83.5 2.6 %all-to-all-done.4 = bf16[4,2,128,256]{3,2,1,0:T(8,128)(2,1)S(1)} async-done(((bf16[4,2,128,256]{3,2,1,0:T(8,128)(2,1)}), bf16[4,2,128,256]{3,2,1,0:T(8,128)(2,1)S(1)}, u32[]{:S(2)}, u32[]{:S(2)}) %all-to-all-start.4) | async-done | bytes 524320 | tf_op jit(solution)/shard_map/all_to_all | solution.py:33
  86.1 3.5 %all-to-all-start.9 = ((bf16[4,2,128,256]{3,2,1,0:T(8,128)(2,1)}), bf16[4,2,128,256]{3,2,1,0:T(8,128)(2,1)S(1)}, u32[]{:S(2)}, u32[]{:S(2)}) async-start(bf16[4,2,128,256]{3,2,1,0:T(8,128)(2,1)} %copy.206), calls=%async_computation.9 | async-start | bytes 1048576 | tf_op jit(solution)/shard_map/all_to_all | solution.py:33
  94.9 3.8 %collective-permute-start.1 = (bf16[2,1024,128]{2,1,0:T(8,128)(2,1)}, bf16[2,1024,128]{2,1,0:T(8,128)(2,1)}, u32[]{:S(2)}, u32[]{:S(2)}) collective-permute-start(bf16[2,1024,128]{2,1,0:T(8,128)(2,1)} %pad_maximum_fusion.4), channel_id=1, source_target_pairs={{0,1},{1,2},{2,3},{3,4},{4,5},{5,6},{6,7},{7,8},{8,9},{9,10},{10,1... | collective-permute-start | bytes 1572872 | tf_op jit(solution)/shard_map/ppermute | solution.py:57
  104.3 1.8 fusion.175
  106.2 7.2 %collective-permute-done.1 = bf16[2,1024,128]{2,1,0:T(8,128)(2,1)} collective-permute-done((bf16[2,1024,128]{2,1,0:T(8,128)(2,1)}, bf16[2,1024,128]{2,1,0:T(8,128)(2,1)}, u32[]{:S(2)}, u32[]{:S(2)}) %collective-permute-start.1) | collective-permute-done | bytes 524320 | tf_op jit(solution)/shard_map/ppermute | solution.py:57
  113.4 1.9 collective-permute-start.3
  116.7 2.7 %fusion.219 = f32[1024,512,2]{1,0,2:T(8,128)} fusion(bf16[1024,128,1]{1,0,2:T(8,128)(2,1)S(1)} %bitcast.608, bf16[512,2,128]{2,1,0:T(2,128)(2,1)S(1)} %copy-done.4), kind=kOutput, calls=%fused_computation.194 | convolution fusion | flops 268435456 | bytes 4718592 | tf_op jit(solution)/shard_map/mhgd,nhd->hgmn/dot_general | solution.py:74
  119.4 7.8 %collective-permute-done.3 = bf16[2,1024,128]{2,1,0:T(8,128)(2,1)S(1)} collective-permute-done((bf16[2,1024,128]{2,1,0:T(8,128)(2,1)}, bf16[2,1024,128]{2,1,0:T(8,128)(2,1)S(1)}, u32[]{:S(2)}, u32[]{:S(2)}) %collective-permute-start.3) | collective-permute-done | bytes 524320 | tf_op jit(solution)/shard_map/ppermute | solution.py:57
  127.3 12.5 %conditional.3 = (f32[1024,1,2,128]{3,0,2,1:T(8,128)}, f32[2,1024,128]{2,1,0:T(8,128)}) conditional(s32[]{:T(128)} %convert_element_type.71, () %tuple.26, (s32[1024]{0:T(1024)S(1)}, s32[1024]{0:T(1024)S(1)}, bf16[2,1024,128]{2,1,0:T(8,128)(2,1)S(1)}, bf16[1024,1,2,128]{3,2,0,1:T(2,128)(2,1)S(1)}, f32[1,2,1024,1]{2,1,3,0:T(2,128)S(1)}, ...), branch_computations={%region_5.6_spmd, %region_6.7_spmd} | conditional | flops 2707554304 | bytes 55123984 | solution.py:190
  129.0 1.5 fusion.88
  139.8 1.9 collective-permute-start.4
  141.8 2.1 fusion.211
  143.8 1.7 reshape.381
  145.6 3.9 %fusion.167 = bf16[1,2,512,1024]{2,3,1,0:T(8,128)(2,1)S(1)} fusion(f32[1024,512,2]{1,0,2:T(8,128)} %fusion.219, bf16[1024,128,1]{1,0,2:T(8,128)(2,1)} %bitcast.620, f32[2,512]{1,0:T(2,128)S(1)} %copy-done.22, f32[2,512]{1,0:T(2,128)S(1)} %copy-done.21, pred[512,1024]{0,1:T(8,128)(4,1)} %fusion.182, bf16[512,2,128]{2,1,0:T(2,128)(2,1)} %reshape.381), kind=kOutput, calls=%fused_computation.144 | convolution fusion | flops 274726912 | bytes 7348224 | tf_op jit(solution)/shard_map/mhgd,nhd->hgmn/dot_general | solution.py:81
  149.5 1.5 fusion.195
  151.1 1.5 fusion.207
  152.6 16.3 %conditional.2 = (f32[1024,1,2,128]{3,0,2,1:T(8,128)S(1)}, f32[2,1024,128]{2,1,0:T(8,128)S(1)}) conditional(s32[]{:T(128)} %convert_element_type.70, () %tuple.24, (s32[1024]{0:T(1024)S(1)}, s32[1024]{0:T(1024)S(1)}, bf16[2,1024,128]{2,1,0:T(8,128)(2,1)}, bf16[1024,1,2,128]{3,2,0,1:T(2,128)(2,1)S(1)}, f32[1,2,1024,1]{2,1,3,0:T(2,128)S(1)}, ...), branch_computations={%region_3.4_spmd, %region_4.5_spmd} | conditional | flops 2707554304 | bytes 55123984 | solution.py:190
  153.7 1.7 fusion.71
  155.4 2.4 %fusion.5 = bf16[1,2,512,1024]{2,3,1,0:T(8,128)(2,1)S(1)} fusion(f32[1024,512,2]{1,0,2:T(8,128)S(1)} %fusion.71, f32[2,512]{1,0:T(2,128)S(1)} %get-tuple-element.164, f32[2,512]{1,0:T(2,128)S(1)} %get-tuple-element.171, pred[512,1024]{0,1:T(8,128)(4,1)S(1)} %get-tuple-element.166, bf16[1024,1,2,128]{3,0,2,1:T(8,128)(2,1)S(1)} %copy.214, ...), kind=kOutput, calls=%fused_computation.8 | convolution fusion | flops 274726912 | bytes 7348224 | tf_op jit(solution)/shard_map/cond/branch_1_fun/mhgd,nhd->hgmn/dot_general | solution.py:81
  158.5 1.7 fusion.41
  160.2 1.7 fusion.68
  164.0 2.4 %fusion.1 = bf16[1,2,512,1024]{2,3,1,0:T(8,128)(2,1)S(1)} fusion(f32[1024,512,2]{1,0,2:T(8,128)S(1)} %fusion.68, f32[2,512]{1,0:T(2,128)S(1)} %get-tuple-element.165, f32[2,512]{1,0:T(2,128)S(1)} %get-tuple-element.170, pred[512,1024]{0,1:T(8,128)(4,1)S(1)} %get-tuple-element.167, bf16[1024,1,2,128]{3,0,2,1:T(8,128)(2,1)S(1)} %copy.214, ...), kind=kOutput, calls=%fused_computation.2 | convolution fusion | flops 274726912 | bytes 7348224 | tf_op jit(solution)/shard_map/cond/branch_1_fun/mhgd,nhd->hgmn/dot_general | solution.py:81
  167.1 1.7 fusion.47
  169.0 2.4 %add.87 = f32[2,1024,128]{2,1,0:T(8,128)} add(f32[2,1024,128]{2,1,0:T(8,128)} %collective-permute-done.4, f32[2,1024,128]{2,1,0:T(8,128)S(1)} %get-tuple-element.62) | non-fusion elementwise | flops 262144 | bytes 3145728 | tf_op jit(solution)/shard_map/add | solution.py:195
  171.4 1.9 collective-permute-start.5
  178.3 4.2 %all-to-all-start.11 = ((bf16[8,128,256]{1,2,0:T(8,128)(2,1)}), bf16[8,128,256]{1,2,0:T(8,128)(2,1)S(1)}, u32[]{:S(2)}, u32[]{:S(2)}) async-start(bf16[8,128,256]{1,2,0:T(8,128)(2,1)} %copy.218), calls=%async_computation.11 | async-start | bytes 1048576 | tf_op jit(solution)/shard_map/all_to_all | solution.py:200
  183.0 3.3 %fusion.198 = f32[1024,1,128]{2,0,1:T(8,128)S(1)} fusion(f32[1024,512,2]{1,0,2:T(8,128)} %fusion.219, f32[2,512]{1,0:T(2,128)S(1)} %copy-done.21, pred[512,1024]{0,1:T(8,128)(4,1)} %fusion.182, f32[512,1,128]{2,0,1:T(8,128)S(1)} %convolution_bitcast_fusion, bf16[512,2,128]{2,1,0:T(2,128)(2,1)S(1)} %copy-done.13), kind=kOutput, calls=%fused_computation.171 | convolution fusion | flops 272760832 | bytes 5771264 | tf_op jit(solution)/shard_map/hgmn,mhgd->nhd/dot_general | solution.py:78
  186.3 6.6 %all-to-all-done.11 = bf16[8,128,256]{1,2,0:T(8,128)(2,1)S(1)} async-done(((bf16[8,128,256]{1,2,0:T(8,128)(2,1)}), bf16[8,128,256]{1,2,0:T(8,128)(2,1)S(1)}, u32[]{:S(2)}, u32[]{:S(2)}) %all-to-all-start.11) | async-done | bytes 524320 | tf_op jit(solution)/shard_map/all_to_all | solution.py:200
  195.9 3.7 %all-to-all-start.13 = ((bf16[8,128,128]{2,1,0:T(8,128)(2,1)}), bf16[8,128,128]{2,1,0:T(8,128)(2,1)S(1)}, u32[]{:S(2)}, u32[]{:S(2)}) async-start(bf16[8,128,128]{2,1,0:T(8,128)(2,1)} %add_convert_fusion), calls=%async_computation.13 | async-start | bytes 524288 | tf_op jit(solution)/shard_map/all_to_all | solution.py:202
  200.4 6.7 %all-to-all-done.13 = bf16[8,128,128]{2,1,0:T(8,128)(2,1)S(1)} async-done(((bf16[8,128,128]{2,1,0:T(8,128)(2,1)}), bf16[8,128,128]{2,1,0:T(8,128)(2,1)S(1)}, u32[]{:S(2)}, u32[]{:S(2)}) %all-to-all-start.13) | async-done | bytes 262176 | tf_op jit(solution)/shard_map/all_to_all | solution.py:202
  207.1 3.4 %all-to-all-start.12 = ((bf16[8,128,128]{2,1,0:T(8,128)(2,1)}), bf16[8,128,128]{2,1,0:T(8,128)(2,1)S(1)}, u32[]{:S(2)}, u32[]{:S(2)}) async-start(bf16[8,128,128]{2,1,0:T(8,128)(2,1)} %add_convert_fusion.1), calls=%async_computation.12 | async-start | bytes 524288 | tf_op jit(solution)/shard_map/all_to_all | solution.py:201
  211.3 6.7 %all-to-all-done.12 = bf16[8,128,128]{2,1,0:T(8,128)(2,1)S(1)} async-done(((bf16[8,128,128]{2,1,0:T(8,128)(2,1)}), bf16[8,128,128]{2,1,0:T(8,128)(2,1)S(1)}, u32[]{:S(2)}, u32[]{:S(2)}) %all-to-all-start.12) | async-done | bytes 262176 | tf_op jit(solution)/shard_map/all_to_all | solution.py:201
  (137 shorter events, 52.6 us)
Async XLA Ops:
  0.6 10.0 %copy-start.8 = (bf16[128,2048]{1,0:T(8,128)(2,1)S(1)}, bf16[128,2048]{1,0:T(8,128)(2,1)}, u32[]{:S(2)}) copy-start(bf16[128,2048]{1,0:T(8,128)(2,1)} %param.15) | copy-start | bytes 1572868
  2.7 20.7 %copy-start.23 = (s32[128]{0:T(128)S(1)}, s32[128]{0:T(128)}, u32[]{:S(2)}) copy-start(s32[128]{0:T(128)} %param.17) | copy-start | bytes 1540
  2.7 8.5 %all-to-all-start.1 = ((bf16[4,2,128,128]{3,2,0,1:T(8,128)(2,1)}), bf16[4,2,128,128]{3,2,0,1:T(8,128)(2,1)S(1)}, u32[]{:S(2)}, u32[]{:S(2)}) async-start(bf16[4,2,128,128]{3,2,0,1:T(8,128)(2,1)} %copy.192), calls=%async_computation.1 | async-start | bytes 524288 | tf_op jit(solution)/shard_map/all_to_all | solution.py:33
  24.0 9.7 %all-to-all-start = ((s32[8,1,128]{2,1,0:T(1,128)}), s32[8,1,128]{2,1,0:T(1,128)S(1)}, u32[]{:S(2)}, u32[]{:S(2)}) async-start(s32[8,1,128]{2,1,0:T(1,128)} %broadcast_in_dim.64), calls=%async_computation | async-start | bytes 8192 | tf_op jit(solution)/shard_map/all_to_all | solution.py:45
  33.7 34.3 %copy-start.14 = (s32[8,1,128]{2,1,0:T(1,128)}, s32[8,1,128]{2,1,0:T(1,128)S(1)}, u32[]{:S(2)}) copy-start(s32[8,1,128]{2,1,0:T(1,128)S(1)} %all-to-all-done) | copy-start | bytes 12292
  33.7 8.6 %all-to-all-start.5 = ((f32[128,8,2]{0,2,1:T(2,128)}), f32[128,8,2]{0,2,1:T(2,128)S(1)}, u32[]{:S(2)}, u32[]{:S(2)}) async-start(f32[128,8,2]{0,2,1:T(2,128)} %bitcast.95), calls=%async_computation.5 | async-start | bytes 16384 | tf_op jit(solution)/shard_map/all_to_all | solution.py:113
  42.2 10.9 %all-to-all-start.10 = ((f32[128,8,2]{0,2,1:T(2,128)}), f32[128,8,2]{0,2,1:T(2,128)S(1)}, u32[]{:S(2)}, u32[]{:S(2)}) async-start(f32[128,8,2]{0,2,1:T(2,128)} %bitcast.111), calls=%async_computation.10 | async-start | bytes 16384 | tf_op jit(solution)/shard_map/all_to_all | solution.py:114
  49.3 30.3 %collective-permute-start = (s32[1024]{0:T(1024)S(1)}, s32[1024]{0:T(1024)S(1)}, u32[]{:S(2)}, u32[]{:S(2)}) collective-permute-start(s32[1024]{0:T(1024)S(1)} %bitcast.634), channel_id=1, source_target_pairs={{0,1},{1,2},{2,3},{3,4},{4,5},{5,6},{6,7},{7,8},{8,9},{9,10},{10,1... | collective-permute-start | bytes 12296 | tf_op jit(solution)/shard_map/ppermute | solution.py:57
  53.1 11.4 %all-to-all-start.2 = ((bf16[4,2,128,128]{3,2,1,0:T(8,128)(2,1)}), bf16[4,2,128,128]{3,2,1,0:T(8,128)(2,1)S(1)}, u32[]{:S(2)}, u32[]{:S(2)}) async-start(bf16[4,2,128,128]{3,2,1,0:T(8,128)(2,1)} %copy.193), calls=%async_computation.2 | async-start | bytes 524288 | tf_op jit(solution)/shard_map/all_to_all | solution.py:33
  64.5 10.1 %all-to-all-start.7 = ((bf16[4,2,128,128]{3,2,1,0:T(8,128)(2,1)}), bf16[4,2,128,128]{3,2,1,0:T(8,128)(2,1)S(1)}, u32[]{:S(2)}, u32[]{:S(2)}) async-start(bf16[4,2,128,128]{3,2,1,0:T(8,128)(2,1)} %copy.202), calls=%async_computation.7 | async-start | bytes 524288 | tf_op jit(solution)/shard_map/all_to_all | solution.py:33
  74.6 28.8 %copy-start.10 = (bf16[4,2,128,128]{3,2,1,0:T(8,128)(2,1)}, bf16[4,2,128,128]{3,2,1,0:T(8,128)(2,1)S(1)}, u32[]{:S(2)}) copy-start(bf16[4,2,128,128]{3,2,1,0:T(8,128)(2,1)S(1)} %all-to-all-done.7) | copy-start | bytes 786436
  74.6 11.5 %all-to-all-start.4 = ((bf16[4,2,128,256]{3,2,1,0:T(8,128)(2,1)}), bf16[4,2,128,256]{3,2,1,0:T(8,128)(2,1)S(1)}, u32[]{:S(2)}, u32[]{:S(2)}) async-start(bf16[4,2,128,256]{3,2,1,0:T(8,128)(2,1)} %copy.197), calls=%async_computation.4 | async-start | bytes 1048576 | tf_op jit(solution)/shard_map/all_to_all | solution.py:33
  79.6 19.1 %copy-start.17 = (s32[1024]{0:T(1024)}, s32[1024]{0:T(1024)S(1)}, u32[]{:S(2)}) copy-start(s32[1024]{0:T(1024)S(1)} %collective-permute-done) | copy-start | bytes 12292
  79.6 12.5 %collective-permute-start.2 = (s32[1024]{0:T(1024)S(1)}, s32[1024]{0:T(1024)S(1)}, u32[]{:S(2)}, u32[]{:S(2)}) collective-permute-start(s32[1024]{0:T(1024)S(1)} %collective-permute-done), channel_id=1, source_target_pairs={{0,1},{1,2},{2,3},{3,4},{4,5},{5,6},{6,7},{7,8},{8,9},{9,10},{10,1... | collective-permute-start | bytes 12296 | tf_op jit(solution)/shard_map/ppermute | solution.py:57
  86.1 14.9 %all-to-all-start.9 = ((bf16[4,2,128,256]{3,2,1,0:T(8,128)(2,1)}), bf16[4,2,128,256]{3,2,1,0:T(8,128)(2,1)S(1)}, u32[]{:S(2)}, u32[]{:S(2)}) async-start(bf16[4,2,128,256]{3,2,1,0:T(8,128)(2,1)} %copy.206), calls=%async_computation.9 | async-start | bytes 1048576 | tf_op jit(solution)/shard_map/all_to_all | solution.py:33
  92.1 6.6 %copy-start.19 = (s32[1024]{0:T(1024)}, s32[1024]{0:T(1024)S(1)}, u32[]{:S(2)}) copy-start(s32[1024]{0:T(1024)S(1)} %collective-permute-done.2) | copy-start | bytes 12292
  94.9 18.5 %collective-permute-start.1 = (bf16[2,1024,128]{2,1,0:T(8,128)(2,1)}, bf16[2,1024,128]{2,1,0:T(8,128)(2,1)}, u32[]{:S(2)}, u32[]{:S(2)}) collective-permute-start(bf16[2,1024,128]{2,1,0:T(8,128)(2,1)} %pad_maximum_fusion.4), channel_id=1, source_target_pairs={{0,1},{1,2},{2,3},{3,4},{4,5},{5,6},{6,7},{7,8},{8,9},{9,10},{10,1... | collective-permute-start | bytes 1572872 | tf_op jit(solution)/shard_map/ppermute | solution.py:57
  104.3 12.4 %copy-start.4 = (bf16[512,2,128]{2,1,0:T(2,128)(2,1)S(1)}, bf16[512,2,128]{2,1,0:T(2,128)(2,1)}, u32[]{:S(2)}) copy-start(bf16[512,2,128]{2,1,0:T(2,128)(2,1)} %reshape.379) | copy-start | bytes 786436
  106.2 21.1 %copy-start = (bf16[1024,1,2,128]{3,2,0,1:T(2,128)(2,1)S(1)}, bf16[1024,1,2,128]{3,2,0,1:T(2,128)(2,1)}, u32[]{:S(2)}) copy-start(bf16[1024,1,2,128]{3,2,0,1:T(2,128)(2,1)} %reshape_reshape_reshape.8) | copy-start | bytes 1572868
  106.2 21.1 %copy-start.2 = (bf16[1024,1,2,128]{3,2,0,1:T(2,128)(2,1)S(1)}, bf16[1024,1,2,128]{3,2,0,1:T(2,128)(2,1)}, u32[]{:S(2)}) copy-start(bf16[1024,1,2,128]{3,2,0,1:T(2,128)(2,1)} %reshape_reshape_reshape.9) | copy-start | bytes 1572868
  106.2 21.1 %copy-start.15 = (s32[8,1,128]{2,1,0:T(1,128)S(1)}, s32[8,1,128]{2,1,0:T(1,128)}, u32[]{:S(2)}) copy-start(s32[8,1,128]{2,1,0:T(1,128)} %copy-done.14) | copy-start | bytes 12292
  106.2 21.1 %copy-start.20 = (s32[1024]{0:T(1024)S(1)}, s32[1024]{0:T(1024)}, u32[]{:S(2)}) copy-start(s32[1024]{0:T(1024)} %copy-done.19) | copy-start | bytes 12292
  113.4 13.8 %collective-permute-start.3 = (bf16[2,1024,128]{2,1,0:T(8,128)(2,1)}, bf16[2,1024,128]{2,1,0:T(8,128)(2,1)S(1)}, u32[]{:S(2)}, u32[]{:S(2)}) collective-permute-start(bf16[2,1024,128]{2,1,0:T(8,128)(2,1)} %collective-permute-done.1), channel_id=1, source_target_pairs={{0,1},{1,2},{2,3},{3,4},{4,5},{5,6},{6,7},{7,8},{8,9},{9,10},{10,1... | collective-permute-start | bytes 1572872 | tf_op jit(solution)/shard_map/ppermute | solution.py:57
  127.3 18.3 %copy-start.21 = (f32[2,512]{1,0:T(2,128)S(1)}, f32[2,512]{1,0:T(2,128)}, u32[]{:S(2)}) copy-start(f32[2,512]{1,0:T(2,128)} %get-tuple-element.191) | copy-start | bytes 12292
  127.3 18.3 %copy-start.22 = (f32[2,512]{1,0:T(2,128)S(1)}, f32[2,512]{1,0:T(2,128)}, u32[]{:S(2)}) copy-start(f32[2,512]{1,0:T(2,128)} %get-tuple-element.189) | copy-start | bytes 12292
  139.8 29.2 %collective-permute-start.4 = (f32[2,1024,128]{2,1,0:T(8,128)}, f32[2,1024,128]{2,1,0:T(8,128)}, u32[]{:S(2)}, u32[]{:S(2)}) collective-permute-start(f32[2,1024,128]{2,1,0:T(8,128)} %get-tuple-element.61), channel_id=1, source_target_pairs={{1,0},{2,1},{3,2},{4,3},{5,4},{6,5},{7,6},{8,7},{9,8},{10,9},{11,1... | collective-permute-start | bytes 3145736 | tf_op jit(solution)/shard_map/ppermute | solution.py:57
  145.6 5.5 %copy-start.5 = (bf16[512,2,128]{2,1,0:T(2,128)(2,1)S(1)}, bf16[512,2,128]{2,1,0:T(2,128)(2,1)}, u32[]{:S(2)}) copy-start(bf16[512,2,128]{2,1,0:T(2,128)(2,1)} %reshape.379) | copy-start | bytes 786436
  145.6 5.5 %copy-start.11 = (f32[512,1,128]{2,0,1:T(8,128)S(1)}, f32[512,1,128]{2,0,1:T(8,128)}, u32[]{:S(2)}) copy-start(f32[512,1,128]{2,0,1:T(8,128)} %fusion.211) | copy-start | bytes 786436
  149.5 3.1 %copy-start.1 = (bf16[1024,1,2,128]{3,2,0,1:T(2,128)(2,1)S(1)}, bf16[1024,1,2,128]{3,2,0,1:T(2,128)(2,1)}, u32[]{:S(2)}) copy-start(bf16[1024,1,2,128]{3,2,0,1:T(2,128)(2,1)} %reshape_reshape_reshape.8) | copy-start | bytes 1572868
  149.5 3.1 %copy-start.3 = (bf16[1024,1,2,128]{3,2,0,1:T(2,128)(2,1)S(1)}, bf16[1024,1,2,128]{3,2,0,1:T(2,128)(2,1)}, u32[]{:S(2)}) copy-start(bf16[1024,1,2,128]{3,2,0,1:T(2,128)(2,1)} %reshape_reshape_reshape.9) | copy-start | bytes 1572868
  149.5 3.1 %copy-start.16 = (s32[8,1,128]{2,1,0:T(1,128)S(1)}, s32[8,1,128]{2,1,0:T(1,128)}, u32[]{:S(2)}) copy-start(s32[8,1,128]{2,1,0:T(1,128)} %copy-done.14) | copy-start | bytes 12292
  149.5 3.1 %copy-start.18 = (s32[1024]{0:T(1024)S(1)}, s32[1024]{0:T(1024)}, u32[]{:S(2)}) copy-start(s32[1024]{0:T(1024)} %copy-done.17) | copy-start | bytes 12292
  152.6 20.7 %copy-start.12 = (bf16[2,2,128,128]{3,2,1,0:T(8,128)(2,1)S(1)}, bf16[2,2,128,128]{3,2,1,0:T(8,128)(2,1)}, u32[]{:S(2)}) copy-start(bf16[2,2,128,128]{3,2,1,0:T(8,128)(2,1)} %slice.174) | copy-start | bytes 393220
  169.0 4.9 %copy-start.7 = (f32[512,1,2,128]{3,0,2,1:T(8,128)S(1)}, f32[512,1,2,128]{3,0,2,1:T(8,128)}, u32[]{:S(2)}) copy-start(f32[512,1,2,128]{3,0,2,1:T(8,128)} %fusion.195) | copy-start | bytes 1572868
  171.4 22.4 %collective-permute-start.5 = (f32[2,1024,128]{2,1,0:T(8,128)}, f32[2,1024,128]{2,1,0:T(8,128)}, u32[]{:S(2)}, u32[]{:S(2)}) collective-permute-start(f32[2,1024,128]{2,1,0:T(8,128)} %add.87), channel_id=1, source_target_pairs={{1,0},{2,1},{3,2},{4,3},{5,4},{6,5},{7,6},{8,7},{9,8},{10,9},{11,1... | collective-permute-start | bytes 3145736 | tf_op jit(solution)/shard_map/ppermute | solution.py:57
  173.8 8.7 %copy-start.6 = (bf16[512,2,128]{2,1,0:T(2,128)(2,1)S(1)}, bf16[512,2,128]{2,1,0:T(2,128)(2,1)}, u32[]{:S(2)}) copy-start(bf16[512,2,128]{2,1,0:T(2,128)(2,1)} %reshape.374) | copy-start | bytes 786436
  175.3 7.7 %copy-start.13 = (bf16[512,2,128]{2,1,0:T(2,128)(2,1)S(1)}, bf16[512,2,128]{2,1,0:T(2,128)(2,1)}, u32[]{:S(2)}) copy-start(bf16[512,2,128]{2,1,0:T(2,128)(2,1)} %reshape.381) | copy-start | bytes 786436
  178.3 14.5 %all-to-all-start.11 = ((bf16[8,128,256]{1,2,0:T(8,128)(2,1)}), bf16[8,128,256]{1,2,0:T(8,128)(2,1)S(1)}, u32[]{:S(2)}, u32[]{:S(2)}) async-start(bf16[8,128,256]{1,2,0:T(8,128)(2,1)} %copy.218), calls=%async_computation.11 | async-start | bytes 1048576 | tf_op jit(solution)/shard_map/all_to_all | solution.py:200
  186.3 13.3 %copy-start.9 = (f32[1024,1,128]{2,0,1:T(8,128)S(1)}, f32[1024,1,128]{2,0,1:T(8,128)}, u32[]{:S(2)}) copy-start(f32[1024,1,128]{2,0,1:T(8,128)} %fusion.207) | copy-start | bytes 1572868
  195.9 11.2 %all-to-all-start.13 = ((bf16[8,128,128]{2,1,0:T(8,128)(2,1)}), bf16[8,128,128]{2,1,0:T(8,128)(2,1)S(1)}, u32[]{:S(2)}, u32[]{:S(2)}) async-start(bf16[8,128,128]{2,1,0:T(8,128)(2,1)} %add_convert_fusion), calls=%async_computation.13 | async-start | bytes 524288 | tf_op jit(solution)/shard_map/all_to_all | solution.py:202
  207.1 10.9 %all-to-all-start.12 = ((bf16[8,128,128]{2,1,0:T(8,128)(2,1)}), bf16[8,128,128]{2,1,0:T(8,128)(2,1)S(1)}, u32[]{:S(2)}, u32[]{:S(2)}) async-start(bf16[8,128,128]{2,1,0:T(8,128)(2,1)} %add_convert_fusion.1), calls=%async_computation.12 | async-start | bytes 524288 | tf_op jit(solution)/shard_map/all_to_all | solution.py:201
where the time goes:
time: 221 us; the launch traced here: 219 us
  starting transfers between devices  58.3 us (26%)
  waiting for transfers between devices  57.1 us (26%)
  matrix products  43.6 us (20%)
  local copies, waits for them, and re-layouts  27.4 us (12%)
  other arithmetic  15.7 us (7%)
  blocking collectives  12.2 us (6%)
  between operations  3.88 us (2%)
    all_to_all x5, starting transfers between devices, turned_blocks(): whole = lax.all_to_all(whole, axes[k], k, k, tiled=True)  18.6 us
    ppermute x6, starting transfers between devices, from_behind(): return lax.ppermute(block, axis, route)  17.2 us
    ppermute x6, waiting for transfers between devices, from_behind(): return lax.ppermute(block, axis, route)  15 us
    all_to_all x5, waiting for transfers between devices, turned_blocks(): whole = lax.all_to_all(whole, axes[k], k, k, tiled=True)  14.6 us
    dot_general x6, matrix products, tile_grads(): jnp.einsum('mhgd,nhd->hgmn', grad_blk, value_blk, preferred_element_type=...  13 us
    all_to_all x3, blocking collectives, turned_blocks(): whole = lax.all_to_all(whole, axes[k], k, k, tiled=True)  12.2 us
    dot_general x6, matrix products, tile_grads(): jnp.einsum('mhgd,nhd->hgmn', query_blk, key_blk, preferred_element_type=j...  9.25 us
    dot_general x6, matrix products, tile_grads(): jnp.einsum('hgmn,mhgd->nhd', weights.astype(jnp.bfloat16), grad_blk, pref...  7.93 us
  transfers between devices with their start and end apart: 17, of which 10 were waited for; matrix products, arithmetic and copies ran while one was open for 30% of the time, Pallas kernels for 0%

commit v1 on v0

v1 whole, which is shorter than its diff:
```python
import functools
import math

import jax
import jax.numpy as jnp
from jax import lax
from jax.experimental import pallas as pl
from jax.experimental.pallas import tpu as pltpu
from jax.sharding import Mesh
from jax.sharding import PartitionSpec as P

D = 128
T = 128
U = 8
KB = 256
QP = 2
STAT = 16
KROWS = 2 * T + STAT
QROWS = 4 * T + STAT
SCALE = 1.0 / math.sqrt(D)
LOG2E = 1.4426950408889634
ULY = ("uly_0", "uly_1")
BLK_ULY = ("blk", "uly_0", "uly_1")
F32 = jnp.float32
BF16 = jnp.bfloat16
VM = pl.BlockSpec(memory_space=pltpu.VMEM)


def dot(a, b, ca, cb):
    return lax.dot_general(a, b, (((ca,), (cb,)), ((), ())), preferred_element_type=F32)


def pack_kv_kernel(k_ref, v_ref, id_ref, out_ref):
    ids = jnp.broadcast_to(id_ref[...].astype(F32), (STAT, T)).astype(BF16)
    for j in range(U):
        out_ref[j, 0:T, :] = k_ref[:, j * D : (j + 1) * D]
        out_ref[j, T : 2 * T, :] = v_ref[:, j * D : (j + 1) * D]
        out_ref[j, 2 * T :, :] = ids


def three(x):
    hi = x.astype(BF16).astype(F32)
    rest = x - hi
    mid = rest.astype(BF16).astype(F32)
    return hi, mid, (rest - mid).astype(BF16).astype(F32)


def pack_q_kernel(q_ref, g_ref, o_ref, lse_ref, out_ref):
    first, second = lse_ref[:, 0, :], lse_ref[:, 1, :]
    top = jnp.maximum(first, second)
    lse = top + jnp.log(jnp.exp(first - top) + jnp.exp(second - top))
    lane = lax.broadcasted_iota(jnp.int32, (T, D), 1)
    deltas = jnp.zeros((T, D), F32)
    for h in range(2 * U):
        cols = slice(h * D, (h + 1) * D)
        prod = g_ref[:, cols].astype(F32) * o_ref[:, cols].astype(F32)
        deltas = jnp.where(lane == h, jnp.sum(prod, axis=1, keepdims=True), deltas)
        j, g = divmod(h, 2)
        out_ref[j, g * T : (g + 1) * T, :] = q_ref[:, cols]
        out_ref[j, (2 + g) * T : (3 + g) * T, :] = g_ref[:, cols]
    parts = three(lse) + three(deltas.T)
    for j in range(U):
        rows = [p[2 * j : 2 * j + 2, :] for p in parts] + [jnp.zeros((4, T), F32)]
        out_ref[j, 4 * T :, :] = jnp.concatenate(rows, axis=0).astype(BF16)


def fill_rows(q_ref, own_ref, lse_s, del_s, qid_s):
    for u in range(U):
        st = q_ref[u, 4 * T :, :].astype(F32)
        two = st[0:2] + st[2:4] + st[4:6]
        dlt = st[6:8] + st[8:10] + st[10:12]
        ids = own_ref[u, 2 * T : 2 * T + 1, :].astype(F32)
        for g in range(2):
            lse_s[u, 0:1, g * T : (g + 1) * T] = two[g : g + 1] * LOG2E
            del_s[u, 0:1, g * T : (g + 1) * T] = dlt[g : g + 1]
        qid_s[u, 0:1, :] = ids


def fill_keys(kv_refs, k_s, v_s, kid_s):
    pick = (lax.broadcasted_iota(jnp.int32, (STAT, D), 0) == 0).astype(F32).astype(BF16)
    for w, ref in enumerate(kv_refs):
        for u in range(U):
            b, r = divmod(w * U + u, KB // T)
            rows = slice(r * T, (r + 1) * T)
            k_s[b, rows, :] = ref[u, 0:T, :]
            v_s[b, rows, :] = ref[u, T : 2 * T, :]
            kid_s[b, rows, :] = dot(ref[u, 2 * T :, :], pick, 0, 0)


def matching(kv_ref, qid, upto):
    total = jnp.zeros((1, T), F32)
    for u in range(upto):
        ids = kv_ref[u, 2 * T : 2 * T + 1, :].astype(F32)
        total = total + jnp.where(ids == qid, 1.0, 0.0)
    return total


def tile(q_ref, k_s, v_s, kid_s, lse_s, del_s, qid_s, dq_s, dkv_ref, qb, kb, causal, key_base):
    k, v = k_s[kb], v_s[kb]
    us = [qb * QP + i for i in range(QP)]
    q = jnp.concatenate([q_ref[u, 0 : 2 * T, :] for u in us], axis=0)
    g = jnp.concatenate([q_ref[u, 2 * T : 4 * T, :] for u in us], axis=0)
    st = dot(k, q, 1, 1)
    dpt = dot(v, g, 1, 1)
    kid = kid_s[kb]
    if causal:
        kpos = lax.broadcasted_iota(jnp.int32, (KB, T), 0) + (kb * KB - key_base)
        qpos = lax.broadcasted_iota(jnp.int32, (KB, T), 1)
    ps, dss = [], []
    for i, u in enumerate(us):
        okay = kid == qid_s[u, 0:1, :]
        if causal:
            okay = okay & (kpos <= qpos + u * T)
        for h in range(2):
            c = slice((2 * i + h) * T, (2 * i + h + 1) * T)
            r = slice(h * T, (h + 1) * T)
            p = jnp.where(okay, jnp.exp2(st[:, c] * (SCALE * LOG2E) - lse_s[u, 0:1, r]), 0.0)
            ps.append(p.astype(BF16))
            dss.append((p * (dpt[:, c] - del_s[u, 0:1, r])).astype(BF16))
    p = jnp.concatenate(ps, axis=1)
    ds = jnp.concatenate(dss, axis=1)
    dv = dot(p, g, 1, 0)
    dk = dot(ds, q, 1, 0)
    dq = dot(k, ds, 0, 0)
    for r in range(KB // T):
        piece = kb * (KB // T) + r
        rows = slice(r * T, (r + 1) * T)
        dkv_ref[piece, 0:T, :] += dk[rows]
        dkv_ref[piece, T : 2 * T, :] += dv[rows]
    for i, u in enumerate(us):
        dq_s[u] += dq[:, i * 2 * T : (i + 1) * 2 * T]


def near_kernel(q_ref, own_ref, prev_ref, dq_ref, dkv_ref, k_s, v_s, kid_s, lse_s, del_s, qid_s):
    fill_rows(q_ref, own_ref, lse_s, del_s, qid_s)
    fill_keys((prev_ref, own_ref), k_s, v_s, kid_s)
    dq_ref[...] = jnp.zeros_like(dq_ref)
    dkv_ref[...] = jnp.zeros_like(dkv_ref)
    for qb in range(U // QP):
        head = qid_s[qb * QP, 0:1, 0:1]
        live = jnp.sum(matching(prev_ref, head, U) + matching(own_ref, head, qb * QP))
        start = U * T + qb * QP * T - live.astype(jnp.int32)

        @pl.loop(start // KB, (U * T + (qb + 1) * QP * T) // KB)
        def _(kb, qb=qb):
            tile(q_ref, k_s, v_s, kid_s, lse_s, del_s, qid_s, dq_ref, dkv_ref, qb, kb, True, U * T)


def far_kernel(
    q_ref, own_ref, far_ref, dqin_ref, dq_ref, dkv_ref, acc_s, dkv_s, k_s, v_s, kid_s, lse_s, del_s, qid_s
):
    fill_rows(q_ref, own_ref, lse_s, del_s, qid_s)
    fill_keys((far_ref,), k_s, v_s, kid_s)
    acc_s[...] = dqin_ref[...]
    dkv_s[...] = jnp.zeros_like(dkv_s)
    for qb in range(U // QP):
        head = qid_s[qb * QP, 0:1, 0:1]
        live = jnp.sum(matching(far_ref, head, U)).astype(jnp.int32)

        @pl.loop((U * T - live) // KB, U * T // KB)
        def _(kb, qb=qb):
            tile(q_ref, k_s, v_s, kid_s, lse_s, del_s, qid_s, acc_s, dkv_s, qb, kb, False, 0)

    for u in range(U):
        dkv_ref[u, 0:T, :] = (dkv_s[u, 0:T, :] * SCALE).astype(BF16)
        dkv_ref[u, T : 2 * T, :] = dkv_s[u, T : 2 * T, :].astype(BF16)
        for h in range(2):
            c = slice(h * T, (h + 1) * T)
            dq_ref[u, c, :] = (acc_s[u, :, c].T * SCALE).astype(BF16)


def add_kernel(base, part_ref, more_ref, out_ref):
    for u in range(U):
        dk = part_ref[base + u, 0:T, :] * SCALE
        out_ref[u, 0:T, :] = (dk + more_ref[u, 0:T, :].astype(F32)).astype(BF16)
        dv = part_ref[base + u, T : 2 * T, :]
        out_ref[u, T : 2 * T, :] = (dv + more_ref[u, T : 2 * T, :].astype(F32)).astype(BF16)


def unpack_q_kernel(in_ref, out_ref):
    for h in range(2 * U):
        j, g = divmod(h, 2)
        out_ref[:, h * D : (h + 1) * D] = in_ref[j, g * T : (g + 1) * T, :]


def unpack_kv_kernel(in_ref, k_ref, v_ref):
    for j in range(U):
        k_ref[:, j * D : (j + 1) * D] = in_ref[j, 0:T, :]
        v_ref[:, j * D : (j + 1) * D] = in_ref[j, T : 2 * T, :]


def call(kernel, outs, scratch=(), flops=0, name=None):
    many = isinstance(outs, tuple)
    return pl.pallas_call(
        kernel,
        out_shape=outs,
        out_specs=(VM,) * len(outs) if many else VM,
        scratch_shapes=scratch,
        cost_estimate=pl.CostEstimate(flops=flops, bytes_accessed=1 << 20, transcendentals=0),
        name=name,
    )


def key_scratch(windows):
    blocks = windows * U * T // KB
    return [
        pltpu.VMEM((blocks, KB, D), BF16),
        pltpu.VMEM((blocks, KB, D), BF16),
        pltpu.VMEM((blocks, KB, D), F32),
        pltpu.VMEM((U, 8, 2 * T), F32),
        pltpu.VMEM((U, 8, 2 * T), F32),
        pltpu.VMEM((U, 8, T), F32),
    ]


def shape(*dims, dtype=BF16):
    return jax.ShapeDtypeStruct(dims, dtype)


def exchanged(message):
    return lax.all_to_all(message, ULY, 0, 0, tiled=True)


def moved(block, distance):
    count = lax.axis_size("blk")
    return lax.ppermute(block, "blk", [(i, (i + distance) % count) for i in range(count)])


def per_device(query, key, value, forward_out, out_grad, lse_parts, ids):
    kv_msg = call(pack_kv_kernel, shape(U, KROWS, D), flops=1 << 20, name="pack_kv")(
        key, value, ids.reshape(1, T)
    )
    own = exchanged(kv_msg)
    q_msg = call(pack_q_kernel, shape(U, QROWS, D), flops=1 << 20, name="pack_q")(
        query, out_grad, forward_out, lse_parts.transpose(1, 2, 0)
    )
    prev = moved(own, 1)
    rows = exchanged(q_msg)
    far = moved(prev, 1)
    dq, dkv = call(
        near_kernel,
        (shape(U, D, 2 * T, dtype=F32), shape(2 * U, 2 * T, D, dtype=F32)),
        key_scratch(2),
        flops=8 << 30,
        name="near",
    )(rows, own, prev)
    dq_msg, far_msg = call(
        far_kernel,
        (shape(U, 2 * T, D), shape(U, 2 * T, D)),
        [pltpu.VMEM((U, D, 2 * T), F32), pltpu.VMEM((U, 2 * T, D), F32)] + key_scratch(1),
        flops=2 << 30,
        name="far",
    )(rows, own, far, dq)
    back = moved(far_msg, -1)
    dq_rows = exchanged(dq_msg)
    prev_msg = call(functools.partial(add_kernel, 0), shape(U, 2 * T, D), flops=1 << 20, name="add_prev")(
        dkv, back
    )
    back = moved(prev_msg, -1)
    query_grad = call(unpack_q_kernel, shape(T, 2 * U * D), flops=1 << 20, name="unpack_q")(dq_rows)
    own_msg = call(functools.partial(add_kernel, U), shape(U, 2 * T, D), flops=1 << 20, name="add_own")(
        dkv, back
    )
    key_grad, value_grad = call(
        unpack_kv_kernel, (shape(T, U * D), shape(T, U * D)), flops=1 << 20, name="unpack_kv"
    )(exchanged(own_msg))
    return query_grad, key_grad, value_grad


def solution(mesh):
    torus = Mesh(mesh.devices.reshape(4, 2, mesh.shape["blk"]), ("uly_0", "uly_1", "blk"))
    flat, cube, line = P(BLK_ULY, None), P(BLK_ULY, None, None), P(BLK_ULY)
    return jax.shard_map(
        per_device,
        mesh=torus,
        in_specs=(flat, flat, flat, flat, flat, cube, line),
        out_specs=(flat, flat, flat),
        check_vma=False,
    )
```

time: 221 us -> 130 us (0.59)
  the two profiles are of different devices: /device:TPU:4 before, /device:TPU:1 now
where the time goes in v1:
time: 130 us; the launch traced here: 128 us
  waiting for transfers between devices  58.2 us (45%)
  starting transfers between devices  36.6 us (28%)
  Pallas kernels  28 us (22%)
  local copies, waits for them, and re-layouts  4.21 us (3%)
    ppermute x4, waiting for transfers between devices, moved(): lax.ppermute(block, 'blk', [(i, (i + distance) % count) for i in range(co...  41 us
    all_to_all x4, starting transfers between devices, exchanged(): return lax.all_to_all(message, ULY, 0, 0, tiled=True)  25.4 us
    all_to_all x4, waiting for transfers between devices, exchanged(): return lax.all_to_all(message, ULY, 0, 0, tiled=True)  17.1 us
    ppermute x4, starting transfers between devices, moved(): lax.ppermute(block, 'blk', [(i, (i + distance) % count) for i in range(co...  11.2 us
    pallas_call x1, Pallas kernels, per_device(): call(near_kernel, (shape(U, D, 2 * T, dtype=F32), shape(2 * U, 2 * T, D,...  9.84 us
    pallas_call x1, Pallas kernels, per_device(): call(far_kernel, (shape(U, 2 * T, D), shape(U, 2 * T, D)), [pltpu.VMEM((U...  4.28 us
    unnamed x16, local copies, waits for them, and re-layouts  4.21 us
    pallas_call x1, Pallas kernels, per_device(): call(pack_q_kernel, shape(U, QROWS, D), flops=1 << 20, name='pack_q')  2.88 us
  transfers between devices with their start and end apart: 8, of which 7 were waited for; matrix products, arithmetic and copies ran while one was open for 0% of the time, Pallas kernels for 13%

profile of v1, /device:TPU:1, one launch (start us, length us, event | category | flops | bytes accessed | tf_op | source)
XLA Modules:
  0.0 127.8 jit_solution(10564352447092261900)
XLA Ops:
  0.6 2.0 %pack_kv.1 = bf16[8,272,128]{2,1,0:T(8,128)(2,1)} custom-call(bf16[128,1024]{1,0:T(8,128)(2,1)} %k_ref.1, bf16[128,1024]{1,0:T(8,128)(2,1)} %v_ref.1, s32[1,128]{1,0:T(1,128)} %bitcast.3), custom_call_target="tpu_custom_call" | custom-call | flops 1048576 | bytes 1048576 | tf_op jit(solution)/shard_map/pack_kv/pallas_call | solution.py:230
  2.6 10.3 %all-to-all-start.1 = ((bf16[8,272,128]{2,1,0:T(8,128)(2,1)}), bf16[8,272,128]{2,1,0:T(8,128)(2,1)S(1)}, u32[]{:S(2)}, u32[]{:S(2)}) async-start(bf16[8,272,128]{2,1,0:T(8,128)(2,1)} %pack_kv.1), calls=%async_computation.1 | async-start | bytes 1114112 | tf_op jit(solution)/shard_map/all_to_all | solution.py:221
  12.9 2.9 %pack_q.1 = bf16[8,528,128]{2,1,0:T(8,128)(2,1)} custom-call(bf16[128,2048]{1,0:T(8,128)(2,1)} %q_ref.1, bf16[128,2048]{1,0:T(8,128)(2,1)} %g_ref.1, bf16[128,2048]{1,0:T(8,128)(2,1)} %o_ref.1, f32[16,2,128]{2,1,0:T(2,128)} %bitcast.2), custom_call_target="tpu_custom_call" | custom-call | flops 1048576 | bytes 1048576 | tf_op jit(solution)/shard_map/pack_q/pallas_call | solution.py:234
  15.7 6.9 %all-to-all-done.1.own_ref = bf16[8,272,128]{2,1,0:T(8,128)(2,1)S(1)} async-done(((bf16[8,272,128]{2,1,0:T(8,128)(2,1)}), bf16[8,272,128]{2,1,0:T(8,128)(2,1)S(1)}, u32[]{:S(2)}, u32[]{:S(2)}) %all-to-all-start.1) | async-done | bytes 557088 | tf_op jit(solution)/shard_map/all_to_all | solution.py:221
  22.6 0.0 copy-start.3
  22.6 4.4 %all-to-all-start = ((bf16[8,528,128]{2,1,0:T(8,128)(2,1)}), bf16[8,528,128]{2,1,0:T(8,128)(2,1)S(1)}, u32[]{:S(2)}, u32[]{:S(2)}) async-start(bf16[8,528,128]{2,1,0:T(8,128)(2,1)} %pack_q.1), calls=%async_computation | async-start | bytes 2162688 | tf_op jit(solution)/shard_map/all_to_all | solution.py:221
  27.0 1.9 %collective-permute-start = (bf16[8,272,128]{2,1,0:T(8,128)(2,1)S(1)}, bf16[8,272,128]{2,1,0:T(8,128)(2,1)S(1)}, u32[]{:S(2)}, u32[]{:S(2)}) collective-permute-start(bf16[8,272,128]{2,1,0:T(8,128)(2,1)S(1)} %all-to-all-done.1.own_ref), channel_id=1, source_target_pairs={{0,1},{1,2},{2,3},{3,4},{4,5},{5,6},{6,7},{7,8},{8,9},{9,10},{10,1... | collective-permute-start | bytes 1671176 | tf_op jit(solution)/shard_map/ppermute | solution.py:226
  28.9 19.9 %collective-permute-done.prev_ref = bf16[8,272,128]{2,1,0:T(8,128)(2,1)S(1)} collective-permute-done((bf16[8,272,128]{2,1,0:T(8,128)(2,1)S(1)}, bf16[8,272,128]{2,1,0:T(8,128)(2,1)S(1)}, u32[]{:S(2)}, u32[]{:S(2)}) %collective-permute-start) | collective-permute-done | bytes 557088 | tf_op jit(solution)/shard_map/ppermute | solution.py:226
  48.9 0.0 copy-start.7
  48.9 1.9 %collective-permute-start.1 = (bf16[8,272,128]{2,1,0:T(8,128)(2,1)S(1)}, bf16[8,272,128]{2,1,0:T(8,128)(2,1)S(1)}, u32[]{:S(2)}, u32[]{:S(2)}) collective-permute-start(bf16[8,272,128]{2,1,0:T(8,128)(2,1)S(1)} %collective-permute-done.prev_ref), channel_id=1, source_target_pairs={{0,1},{1,2},{2,3},{3,4},{4,5},{5,6},{6,7},{7,8},{8,9},{9,10},{10,1... | collective-permute-start | bytes 1671176 | tf_op jit(solution)/shard_map/ppermute | solution.py:226
  50.8 0.0 all-to-all-done.q_ref
  50.8 0.0 copy-done.3
  50.8 0.0 copy-done.7
  50.8 0.0 copy-start.2
  50.8 1.0 copy-done.2
  51.8 9.8 %near.1 = (f32[8,128,256]{2,1,0:T(8,128)}, f32[16,256,128]{2,1,0:T(8,128)}) custom-call(bf16[8,528,128]{2,1,0:T(8,128)(2,1)} %copy-done.2, bf16[8,272,128]{2,1,0:T(8,128)(2,1)} %copy-done.3, bf16[8,272,128]{2,1,0:T(8,128)(2,1)} %copy-done.7), custom_call_target="tpu_custom_call" | custom-call | flops 8589934592 | bytes 1048576 | tf_op jit(solution)/shard_map/near/pallas_call | solution.py:240
  61.7 5.9 %collective-permute-done.1.far_ref = bf16[8,272,128]{2,1,0:T(8,128)(2,1)S(1)} collective-permute-done((bf16[8,272,128]{2,1,0:T(8,128)(2,1)S(1)}, bf16[8,272,128]{2,1,0:T(8,128)(2,1)S(1)}, u32[]{:S(2)}, u32[]{:S(2)}) %collective-permute-start.1) | collective-permute-done | bytes 557088 | tf_op jit(solution)/shard_map/ppermute | solution.py:226
  67.6 0.0 copy-start.6
  67.6 0.8 copy-done.6
  68.4 4.3 %far.1 = (bf16[8,256,128]{2,1,0:T(8,128)(2,1)}, bf16[8,256,128]{2,1,0:T(8,128)(2,1)}) custom-call(bf16[8,528,128]{2,1,0:T(8,128)(2,1)} %copy-done.2, bf16[8,272,128]{2,1,0:T(8,128)(2,1)} %copy-done.3, bf16[8,272,128]{2,1,0:T(8,128)(2,1)} %copy-done.6, f32[8,128,256]{2,1,0:T(8,128)} %get-tuple-element.9.dqin_ref), custom_call_target="tpu_custom_call" | custom-call | flops 2147483648 | bytes 1048576 | tf_op jit(solution)/shard_map/far/pallas_call | solution.py:247
  72.7 1.9 %collective-permute-start.2 = (bf16[8,256,128]{2,1,0:T(8,128)(2,1)}, bf16[8,256,128]{2,1,0:T(8,128)(2,1)S(1)}, u32[]{:S(2)}, u32[]{:S(2)}) collective-permute-start(bf16[8,256,128]{2,1,0:T(8,128)(2,1)} %get-tuple-element.12), channel_id=1, source_target_pairs={{0,63},{1,0},{2,1},{3,2},{4,3},{5,4},{6,5},{7,6},{8,7},{9,8},{10,9... | collective-permute-start | bytes 1572872 | tf_op jit(solution)/shard_map/ppermute | solution.py:226
  74.6 12.1 %collective-permute-done.2.more_ref = bf16[8,256,128]{2,1,0:T(8,128)(2,1)S(1)} collective-permute-done((bf16[8,256,128]{2,1,0:T(8,128)(2,1)}, bf16[8,256,128]{2,1,0:T(8,128)(2,1)S(1)}, u32[]{:S(2)}, u32[]{:S(2)}) %collective-permute-start.2) | collective-permute-done | bytes 524320 | tf_op jit(solution)/shard_map/ppermute | solution.py:226
  86.7 0.0 copy-start.5
  86.7 0.8 copy-done.5
  87.5 2.6 %add_prev.1 = bf16[8,256,128]{2,1,0:T(8,128)(2,1)} custom-call(f32[16,256,128]{2,1,0:T(8,128)} %get-tuple-element.11.part_ref, bf16[8,256,128]{2,1,0:T(8,128)(2,1)} %copy-done.5), custom_call_target="tpu_custom_call" | custom-call | flops 1048576 | bytes 1048576 | tf_op jit(solution)/shard_map/add_prev/pallas_call | solution.py:256
  90.0 5.5 %collective-permute-start.3 = (bf16[8,256,128]{2,1,0:T(8,128)(2,1)}, bf16[8,256,128]{2,1,0:T(8,128)(2,1)S(1)}, u32[]{:S(2)}, u32[]{:S(2)}) collective-permute-start(bf16[8,256,128]{2,1,0:T(8,128)(2,1)} %add_prev.1), channel_id=1, source_target_pairs={{0,63},{1,0},{2,1},{3,2},{4,3},{5,4},{6,5},{7,6},{8,7},{9,8},{10,9... | collective-permute-start | bytes 1572872 | tf_op jit(solution)/shard_map/ppermute | solution.py:226
  95.5 6.3 %all-to-all-start.2 = ((bf16[8,256,128]{2,1,0:T(8,128)(2,1)}), bf16[8,256,128]{2,1,0:T(8,128)(2,1)S(1)}, u32[]{:S(2)}, u32[]{:S(2)}) async-start(bf16[8,256,128]{2,1,0:T(8,128)(2,1)} %get-tuple-element.10), calls=%async_computation.2 | async-start | bytes 1048576 | tf_op jit(solution)/shard_map/all_to_all | solution.py:221
  101.9 3.1 %collective-permute-done.3.more_ref = bf16[8,256,128]{2,1,0:T(8,128)(2,1)S(1)} collective-permute-done((bf16[8,256,128]{2,1,0:T(8,128)(2,1)}, bf16[8,256,128]{2,1,0:T(8,128)(2,1)S(1)}, u32[]{:S(2)}, u32[]{:S(2)}) %collective-permute-start.3) | collective-permute-done | bytes 524320 | tf_op jit(solution)/shard_map/ppermute | solution.py:226
  105.0 0.0 copy-start.4
  105.0 0.8 copy-done.4
  105.8 2.6 %add_own.1 = bf16[8,256,128]{2,1,0:T(8,128)(2,1)} custom-call(f32[16,256,128]{2,1,0:T(8,128)} %get-tuple-element.11.part_ref, bf16[8,256,128]{2,1,0:T(8,128)(2,1)} %copy-done.4), custom_call_target="tpu_custom_call" | custom-call | flops 1048576 | bytes 1048576 | tf_op jit(solution)/shard_map/add_own/pallas_call | solution.py:261
  108.4 2.9 %all-to-all-done.2.in_ref = bf16[8,256,128]{2,1,0:T(8,128)(2,1)S(1)} async-done(((bf16[8,256,128]{2,1,0:T(8,128)(2,1)}), bf16[8,256,128]{2,1,0:T(8,128)(2,1)S(1)}, u32[]{:S(2)}, u32[]{:S(2)}) %all-to-all-start.2) | async-done | bytes 524320 | tf_op jit(solution)/shard_map/all_to_all | solution.py:221
  111.2 0.0 copy-start
  111.2 4.4 %all-to-all-start.3 = ((bf16[8,256,128]{2,1,0:T(8,128)(2,1)}), bf16[8,256,128]{2,1,0:T(8,128)(2,1)S(1)}, u32[]{:S(2)}, u32[]{:S(2)}) async-start(bf16[8,256,128]{2,1,0:T(8,128)(2,1)} %add_own.1), calls=%async_computation.3 | async-start | bytes 1048576 | tf_op jit(solution)/shard_map/all_to_all | solution.py:221
  115.6 0.0 copy-done
  115.6 2.0 %unpack_q.1 = bf16[128,2048]{1,0:T(8,128)(2,1)} custom-call(bf16[8,256,128]{2,1,0:T(8,128)(2,1)} %copy-done), custom_call_target="tpu_custom_call" | custom-call | flops 1048576 | bytes 1048576 | tf_op jit(solution)/shard_map/unpack_q/pallas_call | solution.py:260
  117.6 7.4 %all-to-all-done.3.in_ref = bf16[8,256,128]{2,1,0:T(8,128)(2,1)S(1)} async-done(((bf16[8,256,128]{2,1,0:T(8,128)(2,1)}), bf16[8,256,128]{2,1,0:T(8,128)(2,1)S(1)}, u32[]{:S(2)}, u32[]{:S(2)}) %all-to-all-start.3) | async-done | bytes 524320 | tf_op jit(solution)/shard_map/all_to_all | solution.py:221
  125.0 0.0 copy-start.1
  125.0 0.8 copy-done.1
  125.8 2.0 %unpack_kv.1 = (bf16[128,1024]{1,0:T(8,128)(2,1)}, bf16[128,1024]{1,0:T(8,128)(2,1)}) custom-call(bf16[8,256,128]{2,1,0:T(8,128)(2,1)} %copy-done.1), custom_call_target="tpu_custom_call" | custom-call | flops 1048576 | bytes 1048576 | tf_op jit(solution)/shard_map/unpack_kv/pallas_call | solution.py:264
Async XLA Ops:
  2.6 20.0 %all-to-all-start.1 = ((bf16[8,272,128]{2,1,0:T(8,128)(2,1)}), bf16[8,272,128]{2,1,0:T(8,128)(2,1)S(1)}, u32[]{:S(2)}, u32[]{:S(2)}) async-start(bf16[8,272,128]{2,1,0:T(8,128)(2,1)} %pack_kv.1), calls=%async_computation.1 | async-start | bytes 1114112 | tf_op jit(solution)/shard_map/all_to_all | solution.py:221
  22.6 28.2 %copy-start.3 = (bf16[8,272,128]{2,1,0:T(8,128)(2,1)}, bf16[8,272,128]{2,1,0:T(8,128)(2,1)S(1)}, u32[]{:S(2)}) copy-start(bf16[8,272,128]{2,1,0:T(8,128)(2,1)S(1)} %all-to-all-done.1.own_ref) | copy-start | bytes 1671172
  22.6 28.2 %all-to-all-start = ((bf16[8,528,128]{2,1,0:T(8,128)(2,1)}), bf16[8,528,128]{2,1,0:T(8,128)(2,1)S(1)}, u32[]{:S(2)}, u32[]{:S(2)}) async-start(bf16[8,528,128]{2,1,0:T(8,128)(2,1)} %pack_q.1), calls=%async_computation | async-start | bytes 2162688 | tf_op jit(solution)/shard_map/all_to_all | solution.py:221
  27.0 21.8 %collective-permute-start = (bf16[8,272,128]{2,1,0:T(8,128)(2,1)S(1)}, bf16[8,272,128]{2,1,0:T(8,128)(2,1)S(1)}, u32[]{:S(2)}, u32[]{:S(2)}) collective-permute-start(bf16[8,272,128]{2,1,0:T(8,128)(2,1)S(1)} %all-to-all-done.1.own_ref), channel_id=1, source_target_pairs={{0,1},{1,2},{2,3},{3,4},{4,5},{5,6},{6,7},{7,8},{8,9},{9,10},{10,1... | collective-permute-start | bytes 1671176 | tf_op jit(solution)/shard_map/ppermute | solution.py:226
  48.9 1.9 %copy-start.7 = (bf16[8,272,128]{2,1,0:T(8,128)(2,1)}, bf16[8,272,128]{2,1,0:T(8,128)(2,1)S(1)}, u32[]{:S(2)}) copy-start(bf16[8,272,128]{2,1,0:T(8,128)(2,1)S(1)} %collective-permute-done.prev_ref) | copy-start | bytes 1671172
  48.9 18.7 %collective-permute-start.1 = (bf16[8,272,128]{2,1,0:T(8,128)(2,1)S(1)}, bf16[8,272,128]{2,1,0:T(8,128)(2,1)S(1)}, u32[]{:S(2)}, u32[]{:S(2)}) collective-permute-start(bf16[8,272,128]{2,1,0:T(8,128)(2,1)S(1)} %collective-permute-done.prev_ref), channel_id=1, source_target_pairs={{0,1},{1,2},{2,3},{3,4},{4,5},{5,6},{6,7},{7,8},{8,9},{9,10},{10,1... | collective-permute-start | bytes 1671176 | tf_op jit(solution)/shard_map/ppermute | solution.py:226
  50.8 1.0 copy-start.2
  67.6 0.8 copy-start.6
  72.7 14.0 %collective-permute-start.2 = (bf16[8,256,128]{2,1,0:T(8,128)(2,1)}, bf16[8,256,128]{2,1,0:T(8,128)(2,1)S(1)}, u32[]{:S(2)}, u32[]{:S(2)}) collective-permute-start(bf16[8,256,128]{2,1,0:T(8,128)(2,1)} %get-tuple-element.12), channel_id=1, source_target_pairs={{0,63},{1,0},{2,1},{3,2},{4,3},{5,4},{6,5},{7,6},{8,7},{9,8},{10,9... | collective-permute-start | bytes 1572872 | tf_op jit(solution)/shard_map/ppermute | solution.py:226
  86.7 0.8 copy-start.5
  90.0 15.0 %collective-permute-start.3 = (bf16[8,256,128]{2,1,0:T(8,128)(2,1)}, bf16[8,256,128]{2,1,0:T(8,128)(2,1)S(1)}, u32[]{:S(2)}, u32[]{:S(2)}) collective-permute-start(bf16[8,256,128]{2,1,0:T(8,128)(2,1)} %add_prev.1), channel_id=1, source_target_pairs={{0,63},{1,0},{2,1},{3,2},{4,3},{5,4},{6,5},{7,6},{8,7},{9,8},{10,9... | collective-permute-start | bytes 1572872 | tf_op jit(solution)/shard_map/ppermute | solution.py:226
  95.5 15.7 %all-to-all-start.2 = ((bf16[8,256,128]{2,1,0:T(8,128)(2,1)}), bf16[8,256,128]{2,1,0:T(8,128)(2,1)S(1)}, u32[]{:S(2)}, u32[]{:S(2)}) async-start(bf16[8,256,128]{2,1,0:T(8,128)(2,1)} %get-tuple-element.10), calls=%async_computation.2 | async-start | bytes 1048576 | tf_op jit(solution)/shard_map/all_to_all | solution.py:221
  105.0 0.8 copy-start.4
  111.2 4.4 %copy-start = (bf16[8,256,128]{2,1,0:T(8,128)(2,1)}, bf16[8,256,128]{2,1,0:T(8,128)(2,1)S(1)}, u32[]{:S(2)}) copy-start(bf16[8,256,128]{2,1,0:T(8,128)(2,1)S(1)} %all-to-all-done.2.in_ref) | copy-start | bytes 1572868
  111.2 13.7 %all-to-all-start.3 = ((bf16[8,256,128]{2,1,0:T(8,128)(2,1)}), bf16[8,256,128]{2,1,0:T(8,128)(2,1)S(1)}, u32[]{:S(2)}, u32[]{:S(2)}) async-start(bf16[8,256,128]{2,1,0:T(8,128)(2,1)} %add_own.1), calls=%async_computation.3 | async-start | bytes 1048576 | tf_op jit(solution)/shard_map/all_to_all | solution.py:221
  125.0 0.8 copy-start.1

commit v2 on v1

v2 whole, which is shorter than its diff:
```python
import math

import jax
import jax.numpy as jnp
from jax import lax
from jax.experimental import pallas as pl
from jax.experimental.pallas import tpu as pltpu
from jax.sharding import Mesh
from jax.sharding import PartitionSpec as P


D = 128
T = 128
U = 8
KB = 256
QP = 2
STAT = 16
KROWS = 2 * T + STAT
QROWS = 4 * T + STAT
SCALE = 1.0 / math.sqrt(D)
LOG2E = 1.4426950408889634
ULY = ("uly_0", "uly_1")
BLK_ULY = ("blk", "uly_0", "uly_1")
F32 = jnp.float32
BF16 = jnp.bfloat16
VM = pl.BlockSpec(memory_space=pltpu.VMEM)


def dot(a, b, ca, cb):
    return lax.dot_general(a, b, (((ca,), (cb,)), ((), ())), preferred_element_type=F32)


def pack_kv_kernel(k_ref, v_ref, id_ref, out_ref):
    ids = jnp.broadcast_to(id_ref[...].astype(F32), (STAT, T)).astype(BF16)
    for j in range(U):
        out_ref[j, 0:T, :] = k_ref[:, j * D : (j + 1) * D]
        out_ref[j, T : 2 * T, :] = v_ref[:, j * D : (j + 1) * D]
        out_ref[j, 2 * T :, :] = ids


def three(x):
    hi = x.astype(BF16).astype(F32)
    rest = x - hi
    mid = rest.astype(BF16).astype(F32)
    return hi, mid, (rest - mid).astype(BF16).astype(F32)


def pack_all_kernel(q_ref, g_ref, o_ref, lse_ref, id_ref, kv_ref, out_ref):
    first, second = lse_ref[:, 0, :], lse_ref[:, 1, :]
    top = jnp.maximum(first, second)
    lse = top + jnp.log(jnp.exp(first - top) + jnp.exp(second - top))
    lane = lax.broadcasted_iota(jnp.int32, (T, D), 1)
    deltas = jnp.zeros((T, D), F32)
    for h in range(2 * U):
        cols = slice(h * D, (h + 1) * D)
        prod = g_ref[:, cols].astype(F32) * o_ref[:, cols].astype(F32)
        deltas = jnp.where(lane == h, jnp.sum(prod, axis=1, keepdims=True), deltas)
        j, g = divmod(h, 2)
        out_ref[j, g * T : (g + 1) * T, :] = q_ref[:, cols]
        out_ref[j, (2 + g) * T : (3 + g) * T, :] = g_ref[:, cols]
    parts = three(lse) + three(deltas.T)
    ids = jnp.broadcast_to(id_ref[...].astype(F32), (4, T))
    for j in range(U):
        rows = [p[2 * j : 2 * j + 2, :] for p in parts] + [ids]
        out_ref[j, 4 * T : QROWS, :] = jnp.concatenate(rows, axis=0).astype(BF16)
        out_ref[j, QROWS:, :] = kv_ref[j]


def fill_rows(q_ref, lse_s, del_s, qid_s):
    for u in range(U):
        st = q_ref[u, 4 * T : QROWS, :].astype(F32)
        two = st[0:2] + st[2:4] + st[4:6]
        dlt = st[6:8] + st[8:10] + st[10:12]
        for g in range(2):
            lse_s[u, 0:1, g * T : (g + 1) * T] = two[g : g + 1] * LOG2E
            del_s[u, 0:1, g * T : (g + 1) * T] = dlt[g : g + 1]
        qid_s[u, 0:1, :] = st[12:13]


def fill_keys(kv_ref, first, k_s, v_s, kid_s):
    pick = (lax.broadcasted_iota(jnp.int32, (STAT, D), 0) == 0).astype(F32).astype(BF16)
    for u in range(U):
        b, r = divmod(u, KB // T)
        rows = slice(r * T, (r + 1) * T)
        k_s[b, rows, :] = kv_ref[u, first : first + T, :]
        v_s[b, rows, :] = kv_ref[u, first + T : first + 2 * T, :]
        kid_s[b, rows, :] = dot(kv_ref[u, first + 2 * T : first + KROWS, :], pick, 0, 0)


def matching(kv_ref, first, qid, upto):
    total = jnp.zeros((1, T), F32)
    for u in range(upto):
        ids = kv_ref[u, first + 2 * T : first + 2 * T + 1, :].astype(F32)
        total = total + jnp.where(ids == qid, 1.0, 0.0)
    return jnp.sum(total).astype(jnp.int32)


def tile(q_ref, k_s, v_s, kid_s, lse_s, del_s, qid_s, dq_s, dkv_ref, qb, kb, causal):
    k, v = k_s[kb], v_s[kb]
    us = [qb * QP + i for i in range(QP)]
    q = jnp.concatenate([q_ref[u, 0 : 2 * T, :] for u in us], axis=0)
    g = jnp.concatenate([q_ref[u, 2 * T : 4 * T, :] for u in us], axis=0)
    st = dot(k, q, 1, 1)
    dpt = dot(v, g, 1, 1)
    kid = kid_s[kb]
    if causal:
        kpos = lax.broadcasted_iota(jnp.int32, (KB, T), 0) + kb * KB
        qpos = lax.broadcasted_iota(jnp.int32, (KB, T), 1)
    ps, dss = [], []
    for i, u in enumerate(us):
        okay = kid == qid_s[u, 0:1, :]
        if causal:
            okay = okay & (kpos <= qpos + u * T)
        for h in range(2):
            c = slice((2 * i + h) * T, (2 * i + h + 1) * T)
            r = slice(h * T, (h + 1) * T)
            p = jnp.where(okay, jnp.exp2(st[:, c] * (SCALE * LOG2E) - lse_s[u, 0:1, r]), 0.0)
            ps.append(p.astype(BF16))
            dss.append((p * (dpt[:, c] - del_s[u, 0:1, r])).astype(BF16))
    p = jnp.concatenate(ps, axis=1)
    ds = jnp.concatenate(dss, axis=1)
    dv = dot(p, g, 1, 0)
    dk = dot(ds, q, 1, 0)
    dq = dot(k, ds, 0, 0)
    for r in range(KB // T):
        piece = kb * (KB // T) + r
        rows = slice(r * T, (r + 1) * T)
        dkv_ref[piece, 0:T, :] += dk[rows]
        dkv_ref[piece, T : 2 * T, :] += dv[rows]
    for i, u in enumerate(us):
        dq_s[u] += dq[:, i * 2 * T : (i + 1) * 2 * T]


def turned(acc, u, h):
    return acc[u, :, h * T : (h + 1) * T].T * SCALE


def start_sums(dq_s, dkv_s):
    dq_s[...] = jnp.zeros_like(dq_s)
    dkv_s[...] = jnp.zeros_like(dkv_s)


def walk(q_ref, kv_ref, first, causal, dq_s, dkv_s, k_s, v_s, kid_s, lse_s, del_s, qid_s):
    fill_rows(q_ref, lse_s, del_s, qid_s)
    fill_keys(kv_ref, first, k_s, v_s, kid_s)
    for qb in range(U // QP):
        head = qid_s[qb * QP, 0:1, 0:1]
        before = qb * QP if causal else U
        upto = (qb + 1) * QP if causal else U
        live = matching(kv_ref, first, head, before)

        @pl.loop((before * T - live) // KB, upto * T // KB)
        def _(kb, qb=qb):
            tile(q_ref, k_s, v_s, kid_s, lse_s, del_s, qid_s, dq_s, dkv_s, qb, kb, causal)


def own_kernel(all_ref, dq_ref, dkv_ref, *scratch):
    start_sums(dq_ref, dkv_ref)
    walk(all_ref, all_ref, QROWS, True, dq_ref, dkv_ref, *scratch)
    for u in range(U):
        dkv_ref[u, 0:T, :] = dkv_ref[u, 0:T, :] * SCALE


def prev_kernel(all_ref, prev_ref, sum_ref, dq_ref, dkv_ref, dq_s, *scratch):
    dq_s[...] = sum_ref[...]
    dkv_ref[...] = jnp.zeros_like(dkv_ref)
    walk(all_ref, prev_ref, 0, False, dq_s, dkv_ref, *scratch)
    for u in range(U):
        for h in range(2):
            dq_ref[u, h * T : (h + 1) * T, :] = turned(dq_s, u, h)


def far_kernel(q_ref, prev_ref, sum_ref, dq_ref, dkv_ref, dq_s, dkv_s, *scratch):
    dq_s[...] = jnp.zeros_like(dq_s)
    dkv_s[...] = sum_ref[...]
    walk(q_ref, prev_ref, 0, False, dq_s, dkv_s, *scratch)
    for u in range(U):
        dkv_ref[u, 0:T, :] = (dkv_s[u, 0:T, :] * SCALE).astype(BF16)
        dkv_ref[u, T : 2 * T, :] = dkv_s[u, T : 2 * T, :].astype(BF16)
        for h in range(2):
            dq_ref[u, h * T : (h + 1) * T, :] = turned(dq_s, u, h).astype(BF16)


def total_kernel(dq_ref, more_q_ref, dkv_ref, more_kv_ref, out_ref):
    for u in range(U):
        out_ref[u, 0 : 2 * T, :] = (dq_ref[u] + more_q_ref[u].astype(F32)).astype(BF16)
        out_ref[u, 2 * T :, :] = (dkv_ref[u] + more_kv_ref[u].astype(F32)).astype(BF16)


def unpack_kernel(in_ref, q_ref, k_ref, v_ref):
    for j in range(U):
        for g in range(2):
            h = 2 * j + g
            q_ref[:, h * D : (h + 1) * D] = in_ref[j, g * T : (g + 1) * T, :]
        k_ref[:, j * D : (j + 1) * D] = in_ref[j, 2 * T : 3 * T, :]
        v_ref[:, j * D : (j + 1) * D] = in_ref[j, 3 * T : 4 * T, :]


def call(kernel, outs, scratch=(), flops=0, limit=16):
    many = isinstance(outs, tuple)
    return pl.pallas_call(
        kernel,
        out_shape=outs,
        out_specs=(VM,) * len(outs) if many else VM,
        scratch_shapes=scratch,
        cost_estimate=pl.CostEstimate(flops=flops, bytes_accessed=1 << 20, transcendentals=0),
        compiler_params=pltpu.CompilerParams(vmem_limit_bytes=limit << 20),
    )


KEYS = (
    pltpu.VMEM((U * T // KB, KB, D), BF16),
    pltpu.VMEM((U * T // KB, KB, D), BF16),
    pltpu.VMEM((U * T // KB, KB, D), F32),
    pltpu.VMEM((U, 8, 2 * T), F32),
    pltpu.VMEM((U, 8, 2 * T), F32),
    pltpu.VMEM((U, 8, T), F32),
)
SUM_Q = pltpu.VMEM((U, D, 2 * T), F32)
SUM_KV = pltpu.VMEM((U, 2 * T, D), F32)


def shape(*dims, dtype=BF16):
    return jax.ShapeDtypeStruct(dims, dtype)


def exchanged(message):
    return lax.all_to_all(message, ULY, 0, 0, tiled=True)


def moved(block, distance):
    count = lax.axis_size("blk")
    return lax.ppermute(block, "blk", [(i, (i + distance) % count) for i in range(count)])


def stages(query, key, value, forward_out, out_grad, lse_parts, ids):
    ids = ids.reshape(1, T)
    kv_msg = call(pack_kv_kernel, shape(U, KROWS, D), flops=1 << 20, limit=56)(key, value, ids)
    prev_raw = moved(kv_msg, 1)
    message = call(pack_all_kernel, shape(U, QROWS + KROWS, D), flops=1 << 20, limit=56)(
        query, out_grad, forward_out, lse_parts.transpose(1, 2, 0), ids, kv_msg
    )
    rows = exchanged(message)
    later_rows = moved(rows[:, :QROWS], -1)
    prev = exchanged(prev_raw)
    tall, wide = shape(U, 2 * T, D, dtype=F32), shape(U, D, 2 * T, dtype=F32)
    dq, down = call(own_kernel, (wide, tall), KEYS, flops=4 << 30)(rows)
    dq, dprev = call(prev_kernel, (tall, tall), (SUM_Q,) + KEYS, flops=4 << 30)(rows, prev, dq)
    half = shape(U, 2 * T, D)
    dq_msg, dkv_msg = call(far_kernel, (half, half), (SUM_Q, SUM_KV) + KEYS, flops=1 << 30)(later_rows, prev, dprev)
    total = call(total_kernel, shape(U, 4 * T, D), flops=1 << 20)(dq, moved(dq_msg, 1), down, moved(dkv_msg, -1))
    return call(unpack_kernel, (shape(T, 2 * U * D), shape(T, U * D), shape(T, U * D)), flops=1 << 20)(exchanged(total))


def solution(mesh):
    torus = Mesh(mesh.devices.reshape(4, 2, mesh.shape["blk"]), ("uly_0", "uly_1", "blk"))
    flat, cube, line = P(BLK_ULY, None), P(BLK_ULY, None, None), P(BLK_ULY)
    return jax.shard_map(
        stages,
        mesh=torus,
        in_specs=(flat, flat, flat, flat, flat, cube, line),
        out_specs=(flat, flat, flat),
        check_vma=False,
    )
```

time: 130 us -> 114 us (0.88); the launches traced: 128 us -> 113 us
  waiting for transfers between devices: 58.2 us -> 37.9 us
  blocking collectives: 0 us -> 20 us
  Pallas kernels: 28 us -> 16 us
  starting transfers between devices: 36.6 us -> 35.2 us
    ppermute x4, waiting for transfers between devices: 41 us -> 14.9 us  [moved(): lax.ppermute(block, 'blk', [(i, (i + distance) % count) for i in range(co...]
    all_to_all x0 -> x1, blocking collectives: none -> 20 us  [exchanged(): return lax.all_to_all(message, ULY, 0, 0, tiled=True)]
    pallas_call x8 -> x7, Pallas kernels: 28 us -> 16 us  [the longest x1 5.35 us: stages(): dq, down = call(own_kernel, (wide, tall), KEYS, flops=4 << 30)(rows)]
    all_to_all x4 -> x2, starting transfers between devices: 25.4 us -> 15.2 us  [exchanged(): return lax.all_to_all(message, ULY, 0, 0, tiled=True)]
    ppermute x4, starting transfers between devices: 11.2 us -> 20.1 us  [moved(): lax.ppermute(block, 'blk', [(i, (i + distance) % count) for i in range(co...]
    all_to_all x4 -> x2, waiting for transfers between devices: 17.1 us -> 22.9 us  [exchanged(): return lax.all_to_all(message, ULY, 0, 0, tiled=True)]
    unnamed x16 -> x6, local copies, waits for them, and re-layouts: 4.21 us -> 2.18 us
  transfers between devices with their start and end apart: 8 -> 6, of which waited for: 7 -> 5; matrix products, arithmetic and copies ran while one was open for 0% -> 1% of each run, Pallas kernels for 13% -> 6%
where the time goes in v2:
time: 114 us; the launch traced here: 113 us
  waiting for transfers between devices  37.9 us (33%)
  starting transfers between devices  35.2 us (31%)
  blocking collectives  20 us (18%)
  Pallas kernels  16 us (14%)
  local copies, waits for them, and re-layouts  3.24 us (3%)
    all_to_all x2, waiting for transfers between devices, exchanged(): return lax.all_to_all(message, ULY, 0, 0, tiled=True)  22.9 us
    ppermute x4, starting transfers between devices, moved(): lax.ppermute(block, 'blk', [(i, (i + distance) % count) for i in range(co...  20.1 us
    all_to_all x1, blocking collectives, exchanged(): return lax.all_to_all(message, ULY, 0, 0, tiled=True)  20 us
    all_to_all x2, starting transfers between devices, exchanged(): return lax.all_to_all(message, ULY, 0, 0, tiled=True)  15.2 us
    ppermute x4, waiting for transfers between devices, moved(): lax.ppermute(block, 'blk', [(i, (i + distance) % count) for i in range(co...  14.9 us
    pallas_call x1, Pallas kernels, stages(): dq, down = call(own_kernel, (wide, tall), KEYS, flops=4 << 30)(rows)  5.35 us
    pallas_call x1, Pallas kernels, stages(): call(pack_all_kernel, shape(U, QROWS + KROWS, D), flops=1 << 20, limit=56)  3.31 us
    pallas_call x1, Pallas kernels, stages(): call(far_kernel, (half, half), (SUM_Q, SUM_KV) + KEYS, flops=1 << 30)  2.65 us
  transfers between devices with their start and end apart: 6, of which 5 were waited for; matrix products, arithmetic and copies ran while one was open for 1% of the time, Pallas kernels for 6%

profile of v2, /device:TPU:1, one launch (start us, length us, event | category | flops | bytes accessed | tf_op | source)
XLA Modules:
  0.0 113.1 jit_solution(17207694553903358899)
XLA Ops:
  0.6 2.0 %shard_map.94.kv_ref = bf16[8,272,128]{2,1,0:T(8,128)(2,1)} custom-call(bf16[128,1024]{1,0:T(8,128)(2,1)} %k_ref.1, bf16[128,1024]{1,0:T(8,128)(2,1)} %v_ref.1, s32[1,128]{1,0:T(1,128)} %bitcast.3), custom_call_target="tpu_custom_call" | custom-call | flops 1048576 | bytes 1048576 | tf_op jit(solution)/shard_map/pallas_call | solution.py:238
  2.6 3.3 %shard_map.95 = bf16[8,800,128]{2,1,0:T(8,128)(2,1)} custom-call(bf16[128,2048]{1,0:T(8,128)(2,1)} %q_ref.1, bf16[128,2048]{1,0:T(8,128)(2,1)} %g_ref.1, bf16[128,2048]{1,0:T(8,128)(2,1)} %o_ref.1, f32[16,2,128]{2,1,0:T(2,128)} %bitcast.2, s32[1,128]{1,0:T(1,128)} %bitcast.4, bf16[8,272,128]{2,1,0:T(8,128)(2,1)} %shard_map.94.kv_ref), custom_call_target="tpu_custom_call" | custom-call | flops 1048576 | bytes 1048576 | tf_op jit(solution)/shard_map/pallas_call | solution.py:240
  5.9 0.0 copy-start.2
  5.9 10.5 %all-to-all-start = ((bf16[8,800,128]{2,1,0:T(8,128)(2,1)}), bf16[8,800,128]{2,1,0:T(8,128)(2,1)S(1)}, u32[]{:S(2)}, u32[]{:S(2)}) async-start(bf16[8,800,128]{2,1,0:T(8,128)(2,1)} %shard_map.95), calls=%async_computation | async-start | bytes 3276800 | tf_op jit(solution)/shard_map/all_to_all | solution.py:228
  16.4 0.0 copy-done.2
  16.4 1.9 %collective-permute-start = (bf16[8,272,128]{2,1,0:T(8,128)(2,1)S(1)}, bf16[8,272,128]{2,1,0:T(8,128)(2,1)}, u32[]{:S(2)}, u32[]{:S(2)}) collective-permute-start(bf16[8,272,128]{2,1,0:T(8,128)(2,1)S(1)} %copy-done.2), channel_id=1, source_target_pairs={{0,1},{1,2},{2,3},{3,4},{4,5},{5,6},{6,7},{7,8},{8,9},{9,10},{10,1... | collective-permute-start | bytes 1671176 | tf_op jit(solution)/shard_map/ppermute | solution.py:233
  18.3 19.5 %all-to-all-done.all_ref = bf16[8,800,128]{2,1,0:T(8,128)(2,1)S(1)} async-done(((bf16[8,800,128]{2,1,0:T(8,128)(2,1)}), bf16[8,800,128]{2,1,0:T(8,128)(2,1)S(1)}, u32[]{:S(2)}, u32[]{:S(2)}) %all-to-all-start) | async-done | bytes 1638432 | tf_op jit(solution)/shard_map/all_to_all | solution.py:228
  37.8 1.1 slice.4
  38.8 8.8 %collective-permute-start.1 = (bf16[8,528,128]{2,1,0:T(8,128)(2,1)}, bf16[8,528,128]{2,1,0:T(8,128)(2,1)}, u32[]{:S(2)}, u32[]{:S(2)}) collective-permute-start(bf16[8,528,128]{2,1,0:T(8,128)(2,1)} %slice.4), channel_id=1, source_target_pairs={{0,63},{1,0},{2,1},{3,2},{4,3},{5,4},{6,5},{7,6},{8,7},{9,8},{10,9... | collective-permute-start | bytes 3244040 | tf_op jit(solution)/shard_map/ppermute | solution.py:233
  47.7 0.0 collective-permute-done
  47.7 4.7 %all-to-all-start.1 = ((bf16[8,272,128]{2,1,0:T(8,128)(2,1)}), bf16[8,272,128]{2,1,0:T(8,128)(2,1)S(1)}, u32[]{:S(2)}, u32[]{:S(2)}) async-start(bf16[8,272,128]{2,1,0:T(8,128)(2,1)} %collective-permute-done), calls=%async_computation.1 | async-start | bytes 1114112 | tf_op jit(solution)/shard_map/all_to_all | solution.py:228
  52.4 5.4 %shard_map.96 = (f32[8,128,256]{2,1,0:T(8,128)S(1)}, f32[8,256,128]{2,1,0:T(8,128)S(1)}) custom-call(bf16[8,800,128]{2,1,0:T(8,128)(2,1)S(1)} %all-to-all-done.all_ref), custom_call_target="tpu_custom_call" | custom-call | flops 4294967296 | bytes 1048576 | tf_op jit(solution)/shard_map/pallas_call | solution.py:247
  57.7 0.0 copy-start
  57.7 1.0 copy-done
  58.7 3.4 %all-to-all-done.1.prev_ref = bf16[8,272,128]{2,1,0:T(8,128)(2,1)S(1)} async-done(((bf16[8,272,128]{2,1,0:T(8,128)(2,1)}), bf16[8,272,128]{2,1,0:T(8,128)(2,1)S(1)}, u32[]{:S(2)}, u32[]{:S(2)}) %all-to-all-start.1) | async-done | bytes 557088 | tf_op jit(solution)/shard_map/all_to_all | solution.py:228
  62.1 0.0 copy-start.1
  62.1 1.2 %copy-done.1 = f32[8,128,256]{2,1,0:T(8,128)S(1)} copy-done((f32[8,128,256]{2,1,0:T(8,128)S(1)}, f32[8,128,256]{2,1,0:T(8,128)}, u32[]{:S(2)}) %copy-start.1) | copy-done | bytes 1048600
  63.3 1.4 %shard_map.97 = (f32[8,256,128]{2,1,0:T(8,128)S(1)}, f32[8,256,128]{2,1,0:T(8,128)S(1)}) custom-call(bf16[8,800,128]{2,1,0:T(8,128)(2,1)S(1)} %all-to-all-done.all_ref, bf16[8,272,128]{2,1,0:T(8,128)(2,1)S(1)} %all-to-all-done.1.prev_ref, f32[8,128,256]{2,1,0:T(8,128)S(1)} %copy-done.1), custom_call_target="tpu_custom_call" | custom-call | flops 4294967296 | bytes 1048576 | tf_op jit(solution)/shard_map/pallas_call | solution.py:248
  64.7 5.5 %collective-permute-done.1.q_ref = bf16[8,528,128]{2,1,0:T(8,128)(2,1)} collective-permute-done((bf16[8,528,128]{2,1,0:T(8,128)(2,1)}, bf16[8,528,128]{2,1,0:T(8,128)(2,1)}, u32[]{:S(2)}, u32[]{:S(2)}) %collective-permute-start.1) | collective-permute-done | bytes 1081376 | tf_op jit(solution)/shard_map/ppermute | solution.py:233
  70.2 2.7 %shard_map.98 = (bf16[8,256,128]{2,1,0:T(8,128)(2,1)S(1)}, bf16[8,256,128]{2,1,0:T(8,128)(2,1)S(1)}) custom-call(bf16[8,528,128]{2,1,0:T(8,128)(2,1)} %collective-permute-done.1.q_ref, bf16[8,272,128]{2,1,0:T(8,128)(2,1)S(1)} %all-to-all-done.1.prev_ref, f32[8,256,128]{2,1,0:T(8,128)S(1)} %get-tuple-element.11.sum_ref), custom_call_target="tpu_custom_call" | custom-call | flops 1073741824 | bytes 1048576 | tf_op jit(solution)/shard_map/pallas_call | solution.py:250
  72.9 1.9 %collective-permute-start.2 = (bf16[8,256,128]{2,1,0:T(8,128)(2,1)S(1)}, bf16[8,256,128]{2,1,0:T(8,128)(2,1)S(1)}, u32[]{:S(2)}, u32[]{:S(2)}) collective-permute-start(bf16[8,256,128]{2,1,0:T(8,128)(2,1)S(1)} %get-tuple-element.12), channel_id=1, source_target_pairs={{0,1},{1,2},{2,3},{3,4},{4,5},{5,6},{6,7},{7,8},{8,9},{9,10},{10,1... | collective-permute-start | bytes 1572872 | tf_op jit(solution)/shard_map/ppermute | solution.py:233
  74.8 7.4 %collective-permute-start.3 = (bf16[8,256,128]{2,1,0:T(8,128)(2,1)S(1)}, bf16[8,256,128]{2,1,0:T(8,128)(2,1)S(1)}, u32[]{:S(2)}, u32[]{:S(2)}) collective-permute-start(bf16[8,256,128]{2,1,0:T(8,128)(2,1)S(1)} %get-tuple-element.14), channel_id=1, source_target_pairs={{0,63},{1,0},{2,1},{3,2},{4,3},{5,4},{6,5},{7,6},{8,7},{9,8},{10,9... | collective-permute-start | bytes 1572872 | tf_op jit(solution)/shard_map/ppermute | solution.py:233
  82.2 8.5 %collective-permute-done.2.more_q_ref = bf16[8,256,128]{2,1,0:T(8,128)(2,1)S(1)} collective-permute-done((bf16[8,256,128]{2,1,0:T(8,128)(2,1)S(1)}, bf16[8,256,128]{2,1,0:T(8,128)(2,1)S(1)}, u32[]{:S(2)}, u32[]{:S(2)}) %collective-permute-start.2) | collective-permute-done | bytes 524320 | tf_op jit(solution)/shard_map/ppermute | solution.py:233
  90.8 0.9 collective-permute-done.3.more_kv_ref
  91.7 0.2 shard_map.99
  91.8 20.0 %all_to_all.15.in_ref = bf16[8,512,128]{2,1,0:T(8,128)(2,1)S(1)} all-to-all(bf16[8,512,128]{2,1,0:T(8,128)(2,1)S(1)} %shard_map.99), channel_id=1, replica_groups=mesh['uly_0'=4,'uly_1'=2,'blk'=64] {'uly_0','uly_1'}, dimensions={0} | all-to-all | bytes 2097152 | tf_op jit(solution)/shard_map/all_to_all | solution.py:228
  111.9 1.2 %shard_map.100 = (bf16[128,2048]{1,0:T(8,128)(2,1)}, bf16[128,1024]{1,0:T(8,128)(2,1)}, bf16[128,1024]{1,0:T(8,128)(2,1)}) custom-call(bf16[8,512,128]{2,1,0:T(8,128)(2,1)S(1)} %all_to_all.15.in_ref), custom_call_target="tpu_custom_call" | custom-call | flops 1048576 | bytes 1048576 | tf_op jit(solution)/shard_map/pallas_call | solution.py:252
Async XLA Ops:
  5.9 10.5 %copy-start.2 = (bf16[8,272,128]{2,1,0:T(8,128)(2,1)S(1)}, bf16[8,272,128]{2,1,0:T(8,128)(2,1)}, u32[]{:S(2)}) copy-start(bf16[8,272,128]{2,1,0:T(8,128)(2,1)} %shard_map.94.kv_ref) | copy-start | bytes 1671172
  5.9 31.9 %all-to-all-start = ((bf16[8,800,128]{2,1,0:T(8,128)(2,1)}), bf16[8,800,128]{2,1,0:T(8,128)(2,1)S(1)}, u32[]{:S(2)}, u32[]{:S(2)}) async-start(bf16[8,800,128]{2,1,0:T(8,128)(2,1)} %shard_map.95), calls=%async_computation | async-start | bytes 3276800 | tf_op jit(solution)/shard_map/all_to_all | solution.py:228
  16.4 31.3 %collective-permute-start = (bf16[8,272,128]{2,1,0:T(8,128)(2,1)S(1)}, bf16[8,272,128]{2,1,0:T(8,128)(2,1)}, u32[]{:S(2)}, u32[]{:S(2)}) collective-permute-start(bf16[8,272,128]{2,1,0:T(8,128)(2,1)S(1)} %copy-done.2), channel_id=1, source_target_pairs={{0,1},{1,2},{2,3},{3,4},{4,5},{5,6},{6,7},{7,8},{8,9},{9,10},{10,1... | collective-permute-start | bytes 1671176 | tf_op jit(solution)/shard_map/ppermute | solution.py:233
  38.8 31.4 %collective-permute-start.1 = (bf16[8,528,128]{2,1,0:T(8,128)(2,1)}, bf16[8,528,128]{2,1,0:T(8,128)(2,1)}, u32[]{:S(2)}, u32[]{:S(2)}) collective-permute-start(bf16[8,528,128]{2,1,0:T(8,128)(2,1)} %slice.4), channel_id=1, source_target_pairs={{0,63},{1,0},{2,1},{3,2},{4,3},{5,4},{6,5},{7,6},{8,7},{9,8},{10,9... | collective-permute-start | bytes 3244040 | tf_op jit(solution)/shard_map/ppermute | solution.py:233
  47.7 14.4 %all-to-all-start.1 = ((bf16[8,272,128]{2,1,0:T(8,128)(2,1)}), bf16[8,272,128]{2,1,0:T(8,128)(2,1)S(1)}, u32[]{:S(2)}, u32[]{:S(2)}) async-start(bf16[8,272,128]{2,1,0:T(8,128)(2,1)} %collective-permute-done), calls=%async_computation.1 | async-start | bytes 1114112 | tf_op jit(solution)/shard_map/all_to_all | solution.py:228
  57.7 1.0 copy-start
  62.1 1.2 %copy-start.1 = (f32[8,128,256]{2,1,0:T(8,128)S(1)}, f32[8,128,256]{2,1,0:T(8,128)}, u32[]{:S(2)}) copy-start(f32[8,128,256]{2,1,0:T(8,128)} %copy-done) | copy-start | bytes 3145732
  72.9 17.9 %collective-permute-start.2 = (bf16[8,256,128]{2,1,0:T(8,128)(2,1)S(1)}, bf16[8,256,128]{2,1,0:T(8,128)(2,1)S(1)}, u32[]{:S(2)}, u32[]{:S(2)}) collective-permute-start(bf16[8,256,128]{2,1,0:T(8,128)(2,1)S(1)} %get-tuple-element.12), channel_id=1, source_target_pairs={{0,1},{1,2},{2,3},{3,4},{4,5},{5,6},{6,7},{7,8},{8,9},{9,10},{10,1... | collective-permute-start | bytes 1572872 | tf_op jit(solution)/shard_map/ppermute | solution.py:233
  74.8 16.9 %collective-permute-start.3 = (bf16[8,256,128]{2,1,0:T(8,128)(2,1)S(1)}, bf16[8,256,128]{2,1,0:T(8,128)(2,1)S(1)}, u32[]{:S(2)}, u32[]{:S(2)}) collective-permute-start(bf16[8,256,128]{2,1,0:T(8,128)(2,1)S(1)} %get-tuple-element.14), channel_id=1, source_target_pairs={{0,63},{1,0},{2,1},{3,2},{4,3},{5,4},{6,5},{7,6},{8,7},{9,8},{10,9... | collective-permute-start | bytes 1572872 | tf_op jit(solution)/shard_map/ppermute | solution.py:233

commit v3 on v2

--- a/solution.py
+++ b/solution.py
@@ -45,7 +45,7 @@
     return hi, mid, (rest - mid).astype(BF16).astype(F32)
 
 
-def pack_all_kernel(q_ref, g_ref, o_ref, lse_ref, id_ref, kv_ref, out_ref):
+def pack_q_kernel(q_ref, g_ref, o_ref, lse_ref, id_ref, out_ref):
     first, second = lse_ref[:, 0, :], lse_ref[:, 1, :]
     top = jnp.maximum(first, second)
     lse = top + jnp.log(jnp.exp(first - top) + jnp.exp(second - top))
@@ -63,7 +63,6 @@
     for j in range(U):
         rows = [p[2 * j : 2 * j + 2, :] for p in parts] + [ids]
         out_ref[j, 4 * T : QROWS, :] = jnp.concatenate(rows, axis=0).astype(BF16)
-        out_ref[j, QROWS:, :] = kv_ref[j]
 
 
 def fill_rows(q_ref, lse_s, del_s, qid_s):
@@ -141,7 +140,6 @@
 
 
 def walk(q_ref, kv_ref, first, causal, dq_s, dkv_s, k_s, v_s, kid_s, lse_s, del_s, qid_s):
-    fill_rows(q_ref, lse_s, del_s, qid_s)
     fill_keys(kv_ref, first, k_s, v_s, kid_s)
     for qb in range(U // QP):
         head = qid_s[qb * QP, 0:1, 0:1]
@@ -154,18 +152,14 @@
             tile(q_ref, k_s, v_s, kid_s, lse_s, del_s, qid_s, dq_s, dkv_s, qb, kb, causal)
 
 
-def own_kernel(all_ref, dq_ref, dkv_ref, *scratch):
-    start_sums(dq_ref, dkv_ref)
-    walk(all_ref, all_ref, QROWS, True, dq_ref, dkv_ref, *scratch)
-    for u in range(U):
-        dkv_ref[u, 0:T, :] = dkv_ref[u, 0:T, :] * SCALE
-
-
-def prev_kernel(all_ref, prev_ref, sum_ref, dq_ref, dkv_ref, dq_s, *scratch):
-    dq_s[...] = sum_ref[...]
-    dkv_ref[...] = jnp.zeros_like(dkv_ref)
-    walk(all_ref, prev_ref, 0, False, dq_s, dkv_ref, *scratch)
-    for u in range(U):
+def near_kernel(q_ref, kv_ref, dq_ref, dprev_ref, down_ref, dq_s, *scratch):
+    start_sums(dq_s, dprev_ref)
+    down_ref[...] = jnp.zeros_like(down_ref)
+    fill_rows(q_ref, *scratch[3:])
+    walk(q_ref, kv_ref, KROWS, True, dq_s, down_ref, *scratch)
+    walk(q_ref, kv_ref, 0, False, dq_s, dprev_ref, *scratch)
+    for u in range(U):
+        down_ref[u, 0:T, :] = down_ref[u, 0:T, :] * SCALE
         for h in range(2):
             dq_ref[u, h * T : (h + 1) * T, :] = turned(dq_s, u, h)
 
@@ -173,6 +167,7 @@
 def far_kernel(q_ref, prev_ref, sum_ref, dq_ref, dkv_ref, dq_s, dkv_s, *scratch):
     dq_s[...] = jnp.zeros_like(dq_s)
     dkv_s[...] = sum_ref[...]
+    fill_rows(q_ref, *scratch[3:])
     walk(q_ref, prev_ref, 0, False, dq_s, dkv_s, *scratch)
     for u in range(U):
         dkv_ref[u, 0:T, :] = (dkv_s[u, 0:T, :] * SCALE).astype(BF16)
@@ -233,23 +228,34 @@
     return lax.ppermute(block, "blk", [(i, (i + distance) % count) for i in range(count)])
 
 
+def join_kernel(first_ref, second_ref, out_ref):
+    out_ref[:, 0:KROWS, :] = first_ref[...]
+    out_ref[:, KROWS:, :] = second_ref[...]
+
+
 def stages(query, key, value, forward_out, out_grad, lse_parts, ids):
     ids = ids.reshape(1, T)
     kv_msg = call(pack_kv_kernel, shape(U, KROWS, D), flops=1 << 20, limit=56)(key, value, ids)
     prev_raw = moved(kv_msg, 1)
-    message = call(pack_all_kernel, shape(U, QROWS + KROWS, D), flops=1 << 20, limit=56)(
-        query, out_grad, forward_out, lse_parts.transpose(1, 2, 0), ids, kv_msg
+    message = call(pack_q_kernel, shape(U, QROWS, D), flops=1 << 20, limit=56)(
+        query, out_grad, forward_out, lse_parts.transpose(1, 2, 0), ids
     )
     rows = exchanged(message)
-    later_rows = moved(rows[:, :QROWS], -1)
-    prev = exchanged(prev_raw)
-    tall, wide = shape(U, 2 * T, D, dtype=F32), shape(U, D, 2 * T, dtype=F32)
-    dq, down = call(own_kernel, (wide, tall), KEYS, flops=4 << 30)(rows)
-    dq, dprev = call(prev_kernel, (tall, tall), (SUM_Q,) + KEYS, flops=4 << 30)(rows, prev, dq)
+    both = call(join_kernel, shape(U, 2 * KROWS, D), flops=1 << 20)(prev_raw, kv_msg)
+    keys = exchanged(both)
+    later_rows = moved(rows, -1)
+    tall = shape(U, 2 * T, D, dtype=F32)
+    dq, dprev, down = call(near_kernel, (tall, tall, tall), (SUM_Q,) + KEYS, flops=8 << 30)(rows, keys)
     half = shape(U, 2 * T, D)
-    dq_msg, dkv_msg = call(far_kernel, (half, half), (SUM_Q, SUM_KV) + KEYS, flops=1 << 30)(later_rows, prev, dprev)
-    total = call(total_kernel, shape(U, 4 * T, D), flops=1 << 20)(dq, moved(dq_msg, 1), down, moved(dkv_msg, -1))
-    return call(unpack_kernel, (shape(T, 2 * U * D), shape(T, U * D), shape(T, U * D)), flops=1 << 20)(exchanged(total))
+    dq_msg, dkv_msg = call(far_kernel, (half, half), (SUM_Q, SUM_KV) + KEYS, flops=1 << 30)(
+        later_rows, keys, dprev
+    )
+    total = call(total_kernel, shape(U, 4 * T, D), flops=1 << 20)(
+        dq, moved(dq_msg, 1), down, moved(dkv_msg, -1)
+    )
+    return call(
+        unpack_kernel, (shape(T, 2 * U * D), shape(T, U * D), shape(T, U * D)), flops=1 << 20
+    )(exchanged(total))
 
 
 def solution(mesh):

time: 114 us -> 115 us (level)
  waiting for transfers between devices: 37.9 us -> 47.7 us
  starting transfers between devices: 35.2 us -> 29.2 us
  local copies, waits for them, and re-layouts: 3.24 us -> 1.05 us
    ppermute x4, waiting for transfers between devices: 14.9 us -> 35.4 us  [moved(): lax.ppermute(block, 'blk', [(i, (i + distance) % count) for i in range(co...]
    all_to_all x2, waiting for transfers between devices: 22.9 us -> 12.3 us  [exchanged(): return lax.all_to_all(message, ULY, 0, 0, tiled=True)]
    ppermute x4, starting transfers between devices: 20.1 us -> 13.9 us  [moved(): lax.ppermute(block, 'blk', [(i, (i + distance) % count) for i in range(co...]
    pallas_call x1, Pallas kernels: 2.65 us -> 1.36 us  [stages(): call(far_kernel, (half, half), (SUM_Q, SUM_KV) + KEYS, flops=1 << 30)]
  transfers between devices with their start and end apart: 6 -> 6, of which waited for: 5 -> 5; matrix products, arithmetic and copies ran while one was open for 1% -> 0% of each run, Pallas kernels for 6% -> 8%
where the time goes in v3:
time: 115 us
  waiting for transfers between devices  47.7 us (41%)
  starting transfers between devices  29.2 us (25%)
  blocking collectives  20.8 us (18%)
  Pallas kernels  15.3 us (13%)
    ppermute x4, waiting for transfers between devices, moved(): lax.ppermute(block, 'blk', [(i, (i + distance) % count) for i in range(co...  35.4 us
    all_to_all x1, blocking collectives, exchanged(): return lax.all_to_all(message, ULY, 0, 0, tiled=True)  20.8 us
    all_to_all x2, starting transfers between devices, exchanged(): return lax.all_to_all(message, ULY, 0, 0, tiled=True)  15.3 us
    ppermute x4, starting transfers between devices, moved(): lax.ppermute(block, 'blk', [(i, (i + distance) % count) for i in range(co...  13.9 us
    all_to_all x2, waiting for transfers between devices, exchanged(): return lax.all_to_all(message, ULY, 0, 0, tiled=True)  12.3 us
    pallas_call x1, Pallas kernels, stages(): call(near_kernel, (tall, tall, tall), (SUM_Q,) + KEYS, flops=8 << 30)  6.63 us
    pallas_call x1, Pallas kernels, stages(): call(pack_q_kernel, shape(U, QROWS, D), flops=1 << 20, limit=56)  2.89 us
  transfers between devices with their start and end apart: 6, of which 5 were waited for; matrix products, arithmetic and copies ran while one was open for 0% of the time, Pallas kernels for 8%

profile of v3, /device:TPU:1, one launch (start us, length us, event | category | flops | bytes accessed | tf_op | source)
XLA Modules:
  0.0 114.6 jit_solution(9433075790372890638)
XLA Ops:
  0.6 2.9 %shard_map.94 = bf16[8,528,128]{2,1,0:T(8,128)(2,1)} custom-call(bf16[128,2048]{1,0:T(8,128)(2,1)} %q_ref.1, bf16[128,2048]{1,0:T(8,128)(2,1)} %g_ref.1, bf16[128,2048]{1,0:T(8,128)(2,1)} %o_ref.1, f32[16,2,128]{2,1,0:T(2,128)} %bitcast.2, s32[1,128]{1,0:T(1,128)} %bitcast.3), custom_call_target="tpu_custom_call" | custom-call | flops 1048576 | bytes 1048576 | tf_op jit(solution)/shard_map/pallas_call | solution.py:240
  3.5 10.3 %all-to-all-start = ((bf16[8,528,128]{2,1,0:T(8,128)(2,1)}), bf16[8,528,128]{2,1,0:T(8,128)(2,1)S(1)}, u32[]{:S(2)}, u32[]{:S(2)}) async-start(bf16[8,528,128]{2,1,0:T(8,128)(2,1)} %shard_map.94), calls=%async_computation | async-start | bytes 2162688 | tf_op jit(solution)/shard_map/all_to_all | solution.py:223
  13.8 1.9 %shard_map.95.second_ref = bf16[8,272,128]{2,1,0:T(8,128)(2,1)} custom-call(bf16[128,1024]{1,0:T(8,128)(2,1)} %k_ref.1, bf16[128,1024]{1,0:T(8,128)(2,1)} %v_ref.1, s32[1,128]{1,0:T(1,128)} %bitcast.4), custom_call_target="tpu_custom_call" | custom-call | flops 1048576 | bytes 1048576 | tf_op jit(solution)/shard_map/pallas_call | solution.py:238
  15.8 1.9 %collective-permute-start = (bf16[8,272,128]{2,1,0:T(8,128)(2,1)}, bf16[8,272,128]{2,1,0:T(8,128)(2,1)S(1)}, u32[]{:S(2)}, u32[]{:S(2)}) collective-permute-start(bf16[8,272,128]{2,1,0:T(8,128)(2,1)} %shard_map.95.second_ref), channel_id=1, source_target_pairs={{0,1},{1,2},{2,3},{3,4},{4,5},{5,6},{6,7},{7,8},{8,9},{9,10},{10,1... | collective-permute-start | bytes 1671176 | tf_op jit(solution)/shard_map/ppermute | solution.py:228
  17.7 20.3 %collective-permute-done.first_ref = bf16[8,272,128]{2,1,0:T(8,128)(2,1)S(1)} collective-permute-done((bf16[8,272,128]{2,1,0:T(8,128)(2,1)}, bf16[8,272,128]{2,1,0:T(8,128)(2,1)S(1)}, u32[]{:S(2)}, u32[]{:S(2)}) %collective-permute-start) | collective-permute-done | bytes 557088 | tf_op jit(solution)/shard_map/ppermute | solution.py:228
  37.9 0.0 copy-start
  37.9 1.1 copy-done
  39.0 1.1 shard_map.96
  40.1 0.0 all-to-all-done.q_ref
  40.1 5.0 %all-to-all-start.1 = ((bf16[8,544,128]{2,1,0:T(8,128)(2,1)}), bf16[8,544,128]{2,1,0:T(8,128)(2,1)S(1)}, u32[]{:S(2)}, u32[]{:S(2)}) async-start(bf16[8,544,128]{2,1,0:T(8,128)(2,1)} %shard_map.96), calls=%async_computation.1 | async-start | bytes 2228224 | tf_op jit(solution)/shard_map/all_to_all | solution.py:223
  45.1 3.4 %collective-permute-start.1 = (bf16[8,528,128]{2,1,0:T(8,128)(2,1)S(1)}, bf16[8,528,128]{2,1,0:T(8,128)(2,1)S(1)}, u32[]{:S(2)}, u32[]{:S(2)}) collective-permute-start(bf16[8,528,128]{2,1,0:T(8,128)(2,1)S(1)} %all-to-all-done.q_ref), channel_id=1, source_target_pairs={{0,63},{1,0},{2,1},{3,2},{4,3},{5,4},{6,5},{7,6},{8,7},{9,8},{10,9... | collective-permute-start | bytes 3244040 | tf_op jit(solution)/shard_map/ppermute | solution.py:228
  48.4 12.3 %all-to-all-done.1.kv_ref.prev_ref = bf16[8,544,128]{2,1,0:T(8,128)(2,1)S(1)} async-done(((bf16[8,544,128]{2,1,0:T(8,128)(2,1)}), bf16[8,544,128]{2,1,0:T(8,128)(2,1)S(1)}, u32[]{:S(2)}, u32[]{:S(2)}) %all-to-all-start.1) | async-done | bytes 1114144 | tf_op jit(solution)/shard_map/all_to_all | solution.py:223
  60.7 6.6 %shard_map.97 = (f32[8,256,128]{2,1,0:T(8,128)S(1)}, f32[8,256,128]{2,1,0:T(8,128)S(1)}, f32[8,256,128]{2,1,0:T(8,128)S(1)}) custom-call(bf16[8,528,128]{2,1,0:T(8,128)(2,1)S(1)} %all-to-all-done.q_ref, bf16[8,544,128]{2,1,0:T(8,128)(2,1)S(1)} %all-to-all-done.1.kv_ref.prev_ref), custom_call_target="tpu_custom_call" | custom-call | flops 8589934592 | bytes 1048576 | tf_op jit(solution)/shard_map/pallas_call | solution.py:248
  67.4 5.0 %collective-permute-done.1.q_ref = bf16[8,528,128]{2,1,0:T(8,128)(2,1)S(1)} collective-permute-done((bf16[8,528,128]{2,1,0:T(8,128)(2,1)S(1)}, bf16[8,528,128]{2,1,0:T(8,128)(2,1)S(1)}, u32[]{:S(2)}, u32[]{:S(2)}) %collective-permute-start.1) | collective-permute-done | bytes 1081376 | tf_op jit(solution)/shard_map/ppermute | solution.py:228
  72.3 1.4 %shard_map.98 = (bf16[8,256,128]{2,1,0:T(8,128)(2,1)S(1)}, bf16[8,256,128]{2,1,0:T(8,128)(2,1)S(1)}) custom-call(bf16[8,528,128]{2,1,0:T(8,128)(2,1)S(1)} %collective-permute-done.1.q_ref, bf16[8,544,128]{2,1,0:T(8,128)(2,1)S(1)} %all-to-all-done.1.kv_ref.prev_ref, f32[8,256,128]{2,1,0:T(8,128)S(1)} %get-tuple-element.9.sum_ref), custom_call_target="tpu_custom_call" | custom-call | flops 1073741824 | bytes 1048576 | tf_op jit(solution)/shard_map/pallas_call | solution.py:250
  73.7 1.9 %collective-permute-start.2 = (bf16[8,256,128]{2,1,0:T(8,128)(2,1)S(1)}, bf16[8,256,128]{2,1,0:T(8,128)(2,1)S(1)}, u32[]{:S(2)}, u32[]{:S(2)}) collective-permute-start(bf16[8,256,128]{2,1,0:T(8,128)(2,1)S(1)} %get-tuple-element.10), channel_id=1, source_target_pairs={{0,1},{1,2},{2,3},{3,4},{4,5},{5,6},{6,7},{7,8},{8,9},{9,10},{10,1... | collective-permute-start | bytes 1572872 | tf_op jit(solution)/shard_map/ppermute | solution.py:228
  75.6 6.7 %collective-permute-start.3 = (bf16[8,256,128]{2,1,0:T(8,128)(2,1)S(1)}, bf16[8,256,128]{2,1,0:T(8,128)(2,1)S(1)}, u32[]{:S(2)}, u32[]{:S(2)}) collective-permute-start(bf16[8,256,128]{2,1,0:T(8,128)(2,1)S(1)} %get-tuple-element.12), channel_id=1, source_target_pairs={{0,63},{1,0},{2,1},{3,2},{4,3},{5,4},{6,5},{7,6},{8,7},{9,8},{10,9... | collective-permute-start | bytes 1572872 | tf_op jit(solution)/shard_map/ppermute | solution.py:228
  82.3 9.2 %collective-permute-done.2.more_q_ref = bf16[8,256,128]{2,1,0:T(8,128)(2,1)S(1)} collective-permute-done((bf16[8,256,128]{2,1,0:T(8,128)(2,1)S(1)}, bf16[8,256,128]{2,1,0:T(8,128)(2,1)S(1)}, u32[]{:S(2)}, u32[]{:S(2)}) %collective-permute-start.2) | collective-permute-done | bytes 524320 | tf_op jit(solution)/shard_map/ppermute | solution.py:228
  91.6 0.9 collective-permute-done.3.more_kv_ref
  92.5 0.2 shard_map.99
  92.6 20.8 %all_to_all.15.in_ref = bf16[8,512,128]{2,1,0:T(8,128)(2,1)S(1)} all-to-all(bf16[8,512,128]{2,1,0:T(8,128)(2,1)S(1)} %shard_map.99), channel_id=1, replica_groups=mesh['uly_0'=4,'uly_1'=2,'blk'=64] {'uly_0','uly_1'}, dimensions={0} | all-to-all | bytes 2097152 | tf_op jit(solution)/shard_map/all_to_all | solution.py:223
  113.4 1.2 %shard_map.100 = (bf16[128,2048]{1,0:T(8,128)(2,1)}, bf16[128,1024]{1,0:T(8,128)(2,1)}, bf16[128,1024]{1,0:T(8,128)(2,1)}) custom-call(bf16[8,512,128]{2,1,0:T(8,128)(2,1)S(1)} %all_to_all.15.in_ref), custom_call_target="tpu_custom_call" | custom-call | flops 1048576 | bytes 1048576 | tf_op jit(solution)/shard_map/pallas_call | solution.py:256
Async XLA Ops:
  3.5 36.5 %all-to-all-start = ((bf16[8,528,128]{2,1,0:T(8,128)(2,1)}), bf16[8,528,128]{2,1,0:T(8,128)(2,1)S(1)}, u32[]{:S(2)}, u32[]{:S(2)}) async-start(bf16[8,528,128]{2,1,0:T(8,128)(2,1)} %shard_map.94), calls=%async_computation | async-start | bytes 2162688 | tf_op jit(solution)/shard_map/all_to_all | solution.py:223
  15.8 22.2 %collective-permute-start = (bf16[8,272,128]{2,1,0:T(8,128)(2,1)}, bf16[8,272,128]{2,1,0:T(8,128)(2,1)S(1)}, u32[]{:S(2)}, u32[]{:S(2)}) collective-permute-start(bf16[8,272,128]{2,1,0:T(8,128)(2,1)} %shard_map.95.second_ref), channel_id=1, source_target_pairs={{0,1},{1,2},{2,3},{3,4},{4,5},{5,6},{6,7},{7,8},{8,9},{9,10},{10,1... | collective-permute-start | bytes 1671176 | tf_op jit(solution)/shard_map/ppermute | solution.py:228
  37.9 1.1 copy-start
  40.1 20.7 %all-to-all-start.1 = ((bf16[8,544,128]{2,1,0:T(8,128)(2,1)}), bf16[8,544,128]{2,1,0:T(8,128)(2,1)S(1)}, u32[]{:S(2)}, u32[]{:S(2)}) async-start(bf16[8,544,128]{2,1,0:T(8,128)(2,1)} %shard_map.96), calls=%async_computation.1 | async-start | bytes 2228224 | tf_op jit(solution)/shard_map/all_to_all | solution.py:223
  45.1 27.3 %collective-permute-start.1 = (bf16[8,528,128]{2,1,0:T(8,128)(2,1)S(1)}, bf16[8,528,128]{2,1,0:T(8,128)(2,1)S(1)}, u32[]{:S(2)}, u32[]{:S(2)}) collective-permute-start(bf16[8,528,128]{2,1,0:T(8,128)(2,1)S(1)} %all-to-all-done.q_ref), channel_id=1, source_target_pairs={{0,63},{1,0},{2,1},{3,2},{4,3},{5,4},{6,5},{7,6},{8,7},{9,8},{10,9... | collective-permute-start | bytes 3244040 | tf_op jit(solution)/shard_map/ppermute | solution.py:228
  73.7 17.8 %collective-permute-start.2 = (bf16[8,256,128]{2,1,0:T(8,128)(2,1)S(1)}, bf16[8,256,128]{2,1,0:T(8,128)(2,1)S(1)}, u32[]{:S(2)}, u32[]{:S(2)}) collective-permute-start(bf16[8,256,128]{2,1,0:T(8,128)(2,1)S(1)} %get-tuple-element.10), channel_id=1, source_target_pairs={{0,1},{1,2},{2,3},{3,4},{4,5},{5,6},{6,7},{7,8},{8,9},{9,10},{10,1... | collective-permute-start | bytes 1572872 | tf_op jit(solution)/shard_map/ppermute | solution.py:228
  75.6 16.8 %collective-permute-start.3 = (bf16[8,256,128]{2,1,0:T(8,128)(2,1)S(1)}, bf16[8,256,128]{2,1,0:T(8,128)(2,1)S(1)}, u32[]{:S(2)}, u32[]{:S(2)}) collective-permute-start(bf16[8,256,128]{2,1,0:T(8,128)(2,1)S(1)} %get-tuple-element.12), channel_id=1, source_target_pairs={{0,63},{1,0},{2,1},{3,2},{4,3},{5,4},{6,5},{7,6},{8,7},{9,8},{10,9... | collective-permute-start | bytes 1572872 | tf_op jit(solution)/shard_map/ppermute | solution.py:228

commit v4 on v3

--- a/solution.py
+++ b/solution.py
@@ -152,14 +152,19 @@
             tile(q_ref, k_s, v_s, kid_s, lse_s, del_s, qid_s, dq_s, dkv_s, qb, kb, causal)
 
 
-def near_kernel(q_ref, kv_ref, dq_ref, dprev_ref, down_ref, dq_s, *scratch):
-    start_sums(dq_s, dprev_ref)
-    down_ref[...] = jnp.zeros_like(down_ref)
+def prev_kernel(q_ref, kv_ref, dq_ref, dkv_ref, *scratch):
+    start_sums(dq_ref, dkv_ref)
     fill_rows(q_ref, *scratch[3:])
-    walk(q_ref, kv_ref, KROWS, True, dq_s, down_ref, *scratch)
-    walk(q_ref, kv_ref, 0, False, dq_s, dprev_ref, *scratch)
-    for u in range(U):
-        down_ref[u, 0:T, :] = down_ref[u, 0:T, :] * SCALE
+    walk(q_ref, kv_ref, 0, False, dq_ref, dkv_ref, *scratch)
+
+
+def own_kernel(q_ref, kv_ref, sum_ref, dq_ref, dkv_ref, dq_s, *scratch):
+    dq_s[...] = sum_ref[...]
+    dkv_ref[...] = jnp.zeros_like(dkv_ref)
+    fill_rows(q_ref, *scratch[3:])
+    walk(q_ref, kv_ref, KROWS, True, dq_s, dkv_ref, *scratch)
+    for u in range(U):
+        dkv_ref[u, 0:T, :] = dkv_ref[u, 0:T, :] * SCALE
         for h in range(2):
             dq_ref[u, h * T : (h + 1) * T, :] = turned(dq_s, u, h)
 
@@ -235,27 +240,23 @@
 
 def stages(query, key, value, forward_out, out_grad, lse_parts, ids):
     ids = ids.reshape(1, T)
-    kv_msg = call(pack_kv_kernel, shape(U, KROWS, D), flops=1 << 20, limit=56)(key, value, ids)
-    prev_raw = moved(kv_msg, 1)
     message = call(pack_q_kernel, shape(U, QROWS, D), flops=1 << 20, limit=56)(
         query, out_grad, forward_out, lse_parts.transpose(1, 2, 0), ids
     )
     rows = exchanged(message)
+    kv_msg = call(pack_kv_kernel, shape(U, KROWS, D), flops=1 << 20)(key, value, ids)
+    prev_raw = moved(kv_msg, 1)
+    later_rows = moved(rows, -1)
     both = call(join_kernel, shape(U, 2 * KROWS, D), flops=1 << 20)(prev_raw, kv_msg)
     keys = exchanged(both)
-    later_rows = moved(rows, -1)
-    tall = shape(U, 2 * T, D, dtype=F32)
-    dq, dprev, down = call(near_kernel, (tall, tall, tall), (SUM_Q,) + KEYS, flops=8 << 30)(rows, keys)
-    half = shape(U, 2 * T, D)
-    dq_msg, dkv_msg = call(far_kernel, (half, half), (SUM_Q, SUM_KV) + KEYS, flops=1 << 30)(
-        later_rows, keys, dprev
-    )
-    total = call(total_kernel, shape(U, 4 * T, D), flops=1 << 20)(
-        dq, moved(dq_msg, 1), down, moved(dkv_msg, -1)
-    )
-    return call(
-        unpack_kernel, (shape(T, 2 * U * D), shape(T, U * D), shape(T, U * D)), flops=1 << 20
-    )(exchanged(total))
+    tall, wide, half = shape(U, 2 * T, D, dtype=F32), shape(U, D, 2 * T, dtype=F32), shape(U, 2 * T, D)
+    dq, dprev = call(prev_kernel, (wide, tall), KEYS, flops=4 << 30)(rows, keys)
+    dq_msg, dkv_msg = call(far_kernel, (half, half), (SUM_Q, SUM_KV) + KEYS, flops=1 << 30)(later_rows, keys, dprev)
+    dkv_back = moved(dkv_msg, -1)
+    dq_back = moved(dq_msg, 1)
+    dq, down = call(own_kernel, (tall, tall), (SUM_Q,) + KEYS, flops=4 << 30)(rows, keys, dq)
+    total = call(total_kernel, shape(U, 4 * T, D), flops=1 << 20)(dq, dq_back, down, dkv_back)
+    return call(unpack_kernel, (shape(T, 2 * U * D), shape(T, U * D), shape(T, U * D)), flops=1 << 20)(exchanged(total))
 
 
 def solution(mesh):

time: 115 us -> 112 us (0.974)
  Pallas kernels: 15.3 us -> 13.5 us
    pallas_call x2 -> x3, Pallas kernels: 8.57 us -> 6.75 us  [the longest x1 5.6 us: stages(): call(own_kernel, (tall, tall), (SUM_Q,) + KEYS, flops=4 << 30)]
  transfers between devices with their start and end apart: 6 -> 6, of which waited for: 5 -> 5; matrix products, arithmetic and copies ran while one was open for 0% -> 0% of each run, Pallas kernels for 8% -> 7%
where the time goes in v4:
time: 112 us
  waiting for transfers between devices  47.4 us (42%)
  starting transfers between devices  29.3 us (26%)
  blocking collectives  20.8 us (19%)
  Pallas kernels  13.5 us (12%)
    ppermute x4, waiting for transfers between devices, moved(): lax.ppermute(block, 'blk', [(i, (i + distance) % count) for i in range(co...  35.1 us
    all_to_all x1, blocking collectives, exchanged(): return lax.all_to_all(message, ULY, 0, 0, tiled=True)  20.8 us
    all_to_all x2, starting transfers between devices, exchanged(): return lax.all_to_all(message, ULY, 0, 0, tiled=True)  15.4 us
    ppermute x4, starting transfers between devices, moved(): lax.ppermute(block, 'blk', [(i, (i + distance) % count) for i in range(co...  13.9 us
    all_to_all x2, waiting for transfers between devices, exchanged(): return lax.all_to_all(message, ULY, 0, 0, tiled=True)  12.3 us
    pallas_call x1, Pallas kernels, stages(): call(own_kernel, (tall, tall), (SUM_Q,) + KEYS, flops=4 << 30)  5.6 us
    pallas_call x1, Pallas kernels, stages(): call(pack_q_kernel, shape(U, QROWS, D), flops=1 << 20, limit=56)  2.9 us
  transfers between devices with their start and end apart: 6, of which 5 were waited for; matrix products, arithmetic and copies ran while one was open for 0% of the time, Pallas kernels for 7%

profile of v4, /device:TPU:1, one launch (start us, length us, event | category | flops | bytes accessed | tf_op | source)
XLA Modules:
  0.0 111.7 jit_solution(16294375047786069364)
XLA Ops:
  0.6 2.9 %shard_map.94 = bf16[8,528,128]{2,1,0:T(8,128)(2,1)} custom-call(bf16[128,2048]{1,0:T(8,128)(2,1)} %q_ref.1, bf16[128,2048]{1,0:T(8,128)(2,1)} %g_ref.1, bf16[128,2048]{1,0:T(8,128)(2,1)} %o_ref.1, f32[16,2,128]{2,1,0:T(2,128)} %bitcast.4, s32[1,128]{1,0:T(1,128)} %bitcast.2), custom_call_target="tpu_custom_call" | custom-call | flops 1048576 | bytes 1048576 | tf_op jit(solution)/shard_map/pallas_call | solution.py:243
  3.5 0.0 copy-start
  3.5 0.0 copy-start.1
  3.5 0.0 copy-start.2
  3.5 10.4 %all-to-all-start = ((bf16[8,528,128]{2,1,0:T(8,128)(2,1)}), bf16[8,528,128]{2,1,0:T(8,128)(2,1)S(1)}, u32[]{:S(2)}, u32[]{:S(2)}) async-start(bf16[8,528,128]{2,1,0:T(8,128)(2,1)} %shard_map.94), calls=%async_computation | async-start | bytes 2162688 | tf_op jit(solution)/shard_map/all_to_all | solution.py:228
  14.0 0.0 copy-done
  14.0 0.0 copy-done.1
  14.0 0.0 copy-done.2
  14.0 0.1 shard_map.95.second_ref
  14.1 1.9 %collective-permute-start = (bf16[8,272,128]{2,1,0:T(8,128)(2,1)S(1)}, bf16[8,272,128]{2,1,0:T(8,128)(2,1)S(1)}, u32[]{:S(2)}, u32[]{:S(2)}) collective-permute-start(bf16[8,272,128]{2,1,0:T(8,128)(2,1)S(1)} %shard_map.95.second_ref), channel_id=1, source_target_pairs={{0,1},{1,2},{2,3},{3,4},{4,5},{5,6},{6,7},{7,8},{8,9},{9,10},{10,1... | collective-permute-start | bytes 1671176 | tf_op jit(solution)/shard_map/ppermute | solution.py:233
  16.0 20.0 %collective-permute-done.first_ref = bf16[8,272,128]{2,1,0:T(8,128)(2,1)S(1)} collective-permute-done((bf16[8,272,128]{2,1,0:T(8,128)(2,1)S(1)}, bf16[8,272,128]{2,1,0:T(8,128)(2,1)S(1)}, u32[]{:S(2)}, u32[]{:S(2)}) %collective-permute-start) | collective-permute-done | bytes 557088 | tf_op jit(solution)/shard_map/ppermute | solution.py:233
  36.1 1.1 shard_map.96
  37.1 0.0 all-to-all-done.q_ref
  37.1 5.0 %all-to-all-start.1 = ((bf16[8,544,128]{2,1,0:T(8,128)(2,1)}), bf16[8,544,128]{2,1,0:T(8,128)(2,1)S(1)}, u32[]{:S(2)}, u32[]{:S(2)}) async-start(bf16[8,544,128]{2,1,0:T(8,128)(2,1)} %shard_map.96), calls=%async_computation.1 | async-start | bytes 2228224 | tf_op jit(solution)/shard_map/all_to_all | solution.py:228
  42.1 3.4 %collective-permute-start.1 = (bf16[8,528,128]{2,1,0:T(8,128)(2,1)S(1)}, bf16[8,528,128]{2,1,0:T(8,128)(2,1)S(1)}, u32[]{:S(2)}, u32[]{:S(2)}) collective-permute-start(bf16[8,528,128]{2,1,0:T(8,128)(2,1)S(1)} %all-to-all-done.q_ref), channel_id=1, source_target_pairs={{0,63},{1,0},{2,1},{3,2},{4,3},{5,4},{6,5},{7,6},{8,7},{9,8},{10,9... | collective-permute-start | bytes 3244040 | tf_op jit(solution)/shard_map/ppermute | solution.py:233
  45.5 12.3 %all-to-all-done.1.kv_ref.prev_ref = bf16[8,544,128]{2,1,0:T(8,128)(2,1)S(1)} async-done(((bf16[8,544,128]{2,1,0:T(8,128)(2,1)}), bf16[8,544,128]{2,1,0:T(8,128)(2,1)S(1)}, u32[]{:S(2)}, u32[]{:S(2)}) %all-to-all-start.1) | async-done | bytes 1114144 | tf_op jit(solution)/shard_map/all_to_all | solution.py:228
  57.8 1.0 shard_map.97
  58.9 10.6 %collective-permute-done.1.q_ref = bf16[8,528,128]{2,1,0:T(8,128)(2,1)S(1)} collective-permute-done((bf16[8,528,128]{2,1,0:T(8,128)(2,1)S(1)}, bf16[8,528,128]{2,1,0:T(8,128)(2,1)S(1)}, u32[]{:S(2)}, u32[]{:S(2)}) %collective-permute-start.1) | collective-permute-done | bytes 1081376 | tf_op jit(solution)/shard_map/ppermute | solution.py:233
  69.4 1.4 %shard_map.99 = (bf16[8,256,128]{2,1,0:T(8,128)(2,1)S(1)}, bf16[8,256,128]{2,1,0:T(8,128)(2,1)S(1)}) custom-call(bf16[8,528,128]{2,1,0:T(8,128)(2,1)S(1)} %collective-permute-done.1.q_ref, bf16[8,544,128]{2,1,0:T(8,128)(2,1)S(1)} %all-to-all-done.1.kv_ref.prev_ref, f32[8,256,128]{2,1,0:T(8,128)S(1)} %get-tuple-element.11.sum_ref), custom_call_target="tpu_custom_call" | custom-call | flops 1073741824 | bytes 1048576 | tf_op jit(solution)/shard_map/pallas_call | solution.py:254
  70.8 1.9 %collective-permute-start.2 = (bf16[8,256,128]{2,1,0:T(8,128)(2,1)S(1)}, bf16[8,256,128]{2,1,0:T(8,128)(2,1)S(1)}, u32[]{:S(2)}, u32[]{:S(2)}) collective-permute-start(bf16[8,256,128]{2,1,0:T(8,128)(2,1)S(1)} %get-tuple-element.12), channel_id=1, source_target_pairs={{0,1},{1,2},{2,3},{3,4},{4,5},{5,6},{6,7},{7,8},{8,9},{9,10},{10,1... | collective-permute-start | bytes 1572872 | tf_op jit(solution)/shard_map/ppermute | solution.py:233
  72.7 6.7 %collective-permute-start.3 = (bf16[8,256,128]{2,1,0:T(8,128)(2,1)S(1)}, bf16[8,256,128]{2,1,0:T(8,128)(2,1)S(1)}, u32[]{:S(2)}, u32[]{:S(2)}) collective-permute-start(bf16[8,256,128]{2,1,0:T(8,128)(2,1)S(1)} %get-tuple-element.14), channel_id=1, source_target_pairs={{0,63},{1,0},{2,1},{3,2},{4,3},{5,4},{6,5},{7,6},{8,7},{9,8},{10,9... | collective-permute-start | bytes 1572872 | tf_op jit(solution)/shard_map/ppermute | solution.py:233
  79.4 5.6 %shard_map.98 = (f32[8,256,128]{2,1,0:T(8,128)S(1)}, f32[8,256,128]{2,1,0:T(8,128)S(1)}) custom-call(bf16[8,528,128]{2,1,0:T(8,128)(2,1)S(1)} %all-to-all-done.q_ref, bf16[8,544,128]{2,1,0:T(8,128)(2,1)S(1)} %all-to-all-done.1.kv_ref.prev_ref, f32[8,128,256]{2,1,0:T(8,128)S(1)} %get-tuple-element.9.sum_ref), custom_call_target="tpu_custom_call" | custom-call | flops 4294967296 | bytes 1048576 | tf_op jit(solution)/shard_map/pallas_call | solution.py:257
  85.0 3.6 %collective-permute-done.2.more_q_ref = bf16[8,256,128]{2,1,0:T(8,128)(2,1)S(1)} collective-permute-done((bf16[8,256,128]{2,1,0:T(8,128)(2,1)S(1)}, bf16[8,256,128]{2,1,0:T(8,128)(2,1)S(1)}, u32[]{:S(2)}, u32[]{:S(2)}) %collective-permute-start.2) | collective-permute-done | bytes 524320 | tf_op jit(solution)/shard_map/ppermute | solution.py:233
  88.6 0.9 collective-permute-done.3.more_kv_ref
  89.5 0.2 shard_map.100
  89.7 20.8 %all_to_all.15.in_ref = bf16[8,512,128]{2,1,0:T(8,128)(2,1)S(1)} all-to-all(bf16[8,512,128]{2,1,0:T(8,128)(2,1)S(1)} %shard_map.100), channel_id=1, replica_groups=mesh['uly_0'=4,'uly_1'=2,'blk'=64] {'uly_0','uly_1'}, dimensions={0} | all-to-all | bytes 2097152 | tf_op jit(solution)/shard_map/all_to_all | solution.py:228
  110.5 1.2 %shard_map.101 = (bf16[128,2048]{1,0:T(8,128)(2,1)}, bf16[128,1024]{1,0:T(8,128)(2,1)}, bf16[128,1024]{1,0:T(8,128)(2,1)}) custom-call(bf16[8,512,128]{2,1,0:T(8,128)(2,1)S(1)} %all_to_all.15.in_ref), custom_call_target="tpu_custom_call" | custom-call | flops 1048576 | bytes 1048576 | tf_op jit(solution)/shard_map/pallas_call | solution.py:259
Async XLA Ops:
  3.5 10.4 %copy-start = (bf16[128,1024]{1,0:T(8,128)(2,1)S(1)}, bf16[128,1024]{1,0:T(8,128)(2,1)}, u32[]{:S(2)}) copy-start(bf16[128,1024]{1,0:T(8,128)(2,1)} %k_ref.1) | copy-start | bytes 786436
  3.5 10.4 %copy-start.1 = (bf16[128,1024]{1,0:T(8,128)(2,1)S(1)}, bf16[128,1024]{1,0:T(8,128)(2,1)}, u32[]{:S(2)}) copy-start(bf16[128,1024]{1,0:T(8,128)(2,1)} %v_ref.1) | copy-start | bytes 786436
  3.5 10.5 %copy-start.2 = (s32[128]{0:T(128)S(1)}, s32[128]{0:T(128)}, u32[]{:S(2)}) copy-start(s32[128]{0:T(128)} %param.13) | copy-start | bytes 1540
  3.5 33.6 %all-to-all-start = ((bf16[8,528,128]{2,1,0:T(8,128)(2,1)}), bf16[8,528,128]{2,1,0:T(8,128)(2,1)S(1)}, u32[]{:S(2)}, u32[]{:S(2)}) async-start(bf16[8,528,128]{2,1,0:T(8,128)(2,1)} %shard_map.94), calls=%async_computation | async-start | bytes 2162688 | tf_op jit(solution)/shard_map/all_to_all | solution.py:228
  14.1 22.0 %collective-permute-start = (bf16[8,272,128]{2,1,0:T(8,128)(2,1)S(1)}, bf16[8,272,128]{2,1,0:T(8,128)(2,1)S(1)}, u32[]{:S(2)}, u32[]{:S(2)}) collective-permute-start(bf16[8,272,128]{2,1,0:T(8,128)(2,1)S(1)} %shard_map.95.second_ref), channel_id=1, source_target_pairs={{0,1},{1,2},{2,3},{3,4},{4,5},{5,6},{6,7},{7,8},{8,9},{9,10},{10,1... | collective-permute-start | bytes 1671176 | tf_op jit(solution)/shard_map/ppermute | solution.py:233
  37.1 20.7 %all-to-all-start.1 = ((bf16[8,544,128]{2,1,0:T(8,128)(2,1)}), bf16[8,544,128]{2,1,0:T(8,128)(2,1)S(1)}, u32[]{:S(2)}, u32[]{:S(2)}) async-start(bf16[8,544,128]{2,1,0:T(8,128)(2,1)} %shard_map.96), calls=%async_computation.1 | async-start | bytes 2228224 | tf_op jit(solution)/shard_map/all_to_all | solution.py:228
  42.1 27.3 %collective-permute-start.1 = (bf16[8,528,128]{2,1,0:T(8,128)(2,1)S(1)}, bf16[8,528,128]{2,1,0:T(8,128)(2,1)S(1)}, u32[]{:S(2)}, u32[]{:S(2)}) collective-permute-start(bf16[8,528,128]{2,1,0:T(8,128)(2,1)S(1)} %all-to-all-done.q_ref), channel_id=1, source_target_pairs={{0,63},{1,0},{2,1},{3,2},{4,3},{5,4},{6,5},{7,6},{8,7},{9,8},{10,9... | collective-permute-start | bytes 3244040 | tf_op jit(solution)/shard_map/ppermute | solution.py:233
  70.8 17.8 %collective-permute-start.2 = (bf16[8,256,128]{2,1,0:T(8,128)(2,1)S(1)}, bf16[8,256,128]{2,1,0:T(8,128)(2,1)S(1)}, u32[]{:S(2)}, u32[]{:S(2)}) collective-permute-start(bf16[8,256,128]{2,1,0:T(8,128)(2,1)S(1)} %get-tuple-element.12), channel_id=1, source_target_pairs={{0,1},{1,2},{2,3},{3,4},{4,5},{5,6},{6,7},{7,8},{8,9},{9,10},{10,1... | collective-permute-start | bytes 1572872 | tf_op jit(solution)/shard_map/ppermute | solution.py:233
  72.7 16.8 %collective-permute-start.3 = (bf16[8,256,128]{2,1,0:T(8,128)(2,1)S(1)}, bf16[8,256,128]{2,1,0:T(8,128)(2,1)S(1)}, u32[]{:S(2)}, u32[]{:S(2)}) collective-permute-start(bf16[8,256,128]{2,1,0:T(8,128)(2,1)S(1)} %get-tuple-element.14), channel_id=1, source_target_pairs={{0,63},{1,0},{2,1},{3,2},{4,3},{5,4},{6,5},{7,6},{8,7},{9,8},{10,9... | collective-permute-start | bytes 1572872 | tf_op jit(solution)/shard_map/ppermute | solution.py:233

commit v5 on v4

--- a/solution.py
+++ b/solution.py
@@ -13,7 +13,7 @@
 T = 128
 U = 8
 KB = 256
-QP = 2
+QP = 4
 STAT = 16
 KROWS = 2 * T + STAT
 QROWS = 4 * T + STAT
@@ -24,6 +24,7 @@
 F32 = jnp.float32
 BF16 = jnp.bfloat16
 VM = pl.BlockSpec(memory_space=pltpu.VMEM)
+FAR = pl.BlockSpec(memory_space=pl.ANY)
 
 
 def dot(a, b, ca, cb):
@@ -45,24 +46,48 @@
     return hi, mid, (rest - mid).astype(BF16).astype(F32)
 
 
-def pack_q_kernel(q_ref, g_ref, o_ref, lse_ref, id_ref, out_ref):
-    first, second = lse_ref[:, 0, :], lse_ref[:, 1, :]
+def pack_q_kernel(q_ref, g_ref, o_ref, lse_ref, id_ref, out_ref, o_s, lse_s, id_s, sems, more_sems):
+    def piece(ref, h, row, kind):
+        j, g = divmod(h, 2)
+        rows = pl.ds((row + g) * T, T)
+        return pltpu.make_async_copy(ref.at[:, pl.ds(h * D, D)], out_ref.at[j, rows, :], sems.at[kind, h])
+
+    grads = [piece(g_ref, h, 2, 0) for h in range(2 * U)]
+    queries = [piece(q_ref, h, 0, 1) for h in range(2 * U)]
+    outputs = [
+        pltpu.make_async_copy(o_ref.at[:, pl.ds(h * D, D)], o_s.at[h], sems.at[2, h]) for h in range(2 * U)
+    ]
+    small = [
+        pltpu.make_async_copy(lse_ref, lse_s, more_sems.at[0]),
+        pltpu.make_async_copy(id_ref, id_s, more_sems.at[1]),
+    ]
+    for copy in small:
+        copy.start()
+    for h in range(2 * U):
+        grads[h].start()
+        outputs[h].start()
+    for h in range(2 * U):
+        queries[h].start()
+    for copy in small:
+        copy.wait()
+    first, second = lse_s[:, 0, :], lse_s[:, 1, :]
     top = jnp.maximum(first, second)
     lse = top + jnp.log(jnp.exp(first - top) + jnp.exp(second - top))
     lane = lax.broadcasted_iota(jnp.int32, (T, D), 1)
     deltas = jnp.zeros((T, D), F32)
     for h in range(2 * U):
-        cols = slice(h * D, (h + 1) * D)
-        prod = g_ref[:, cols].astype(F32) * o_ref[:, cols].astype(F32)
+        j, g = divmod(h, 2)
+        grads[h].wait()
+        outputs[h].wait()
+        prod = out_ref[j, (2 + g) * T : (3 + g) * T, :].astype(F32) * o_s[h].astype(F32)
         deltas = jnp.where(lane == h, jnp.sum(prod, axis=1, keepdims=True), deltas)
-        j, g = divmod(h, 2)
-        out_ref[j, g * T : (g + 1) * T, :] = q_ref[:, cols]
-        out_ref[j, (2 + g) * T : (3 + g) * T, :] = g_ref[:, cols]
     parts = three(lse) + three(deltas.T)
-    ids = jnp.broadcast_to(id_ref[...].astype(F32), (4, T))
+    ids = jnp.broadcast_to(id_s[...].astype(F32), (4, T))
     for j in range(U):
         rows = [p[2 * j : 2 * j + 2, :] for p in parts] + [ids]
         out_ref[j, 4 * T : QROWS, :] = jnp.concatenate(rows, axis=0).astype(BF16)
+    for copy in queries:
+        copy.wait()
 
 
 def fill_rows(q_ref, lse_s, del_s, qid_s):
@@ -76,21 +101,23 @@
         qid_s[u, 0:1, :] = st[12:13]
 
 
-def fill_keys(kv_ref, first, k_s, v_s, kid_s):
-    pick = (lax.broadcasted_iota(jnp.int32, (STAT, D), 0) == 0).astype(F32).astype(BF16)
+def fill_keys(kv_ref, first, ids, k_s, v_s, kid_s):
+    id_ref, start, row = ids
+    pick = (lax.broadcasted_iota(jnp.int32, (STAT, D), 0) == row).astype(F32).astype(BF16)
     for u in range(U):
         b, r = divmod(u, KB // T)
         rows = slice(r * T, (r + 1) * T)
         k_s[b, rows, :] = kv_ref[u, first : first + T, :]
         v_s[b, rows, :] = kv_ref[u, first + T : first + 2 * T, :]
-        kid_s[b, rows, :] = dot(kv_ref[u, first + 2 * T : first + KROWS, :], pick, 0, 0)
-
-
-def matching(kv_ref, first, qid, upto):
+        kid_s[b, rows, :] = dot(id_ref[u, start : start + STAT, :], pick, 0, 0)
+
+
+def matching(ids, qid, upto):
+    id_ref, start, row = ids
     total = jnp.zeros((1, T), F32)
     for u in range(upto):
-        ids = kv_ref[u, first + 2 * T : first + 2 * T + 1, :].astype(F32)
-        total = total + jnp.where(ids == qid, 1.0, 0.0)
+        here = id_ref[u, start : start + STAT, :].astype(F32)[row : row + 1]
+        total = total + jnp.where(here == qid, 1.0, 0.0)
     return jnp.sum(total).astype(jnp.int32)
 
 
@@ -139,13 +166,13 @@
     dkv_s[...] = jnp.zeros_like(dkv_s)
 
 
-def walk(q_ref, kv_ref, first, causal, dq_s, dkv_s, k_s, v_s, kid_s, lse_s, del_s, qid_s):
-    fill_keys(kv_ref, first, k_s, v_s, kid_s)
+def walk(q_ref, kv_ref, first, ids, causal, dq_s, dkv_s, k_s, v_s, kid_s, lse_s, del_s, qid_s):
+    fill_keys(kv_ref, first, ids, k_s, v_s, kid_s)
     for qb in range(U // QP):
         head = qid_s[qb * QP, 0:1, 0:1]
         before = qb * QP if causal else U
         upto = (qb + 1) * QP if causal else U
-        live = matching(kv_ref, first, head, before)
+        live = matching(ids, head, before)
 
         @pl.loop((before * T - live) // KB, upto * T // KB)
         def _(kb, qb=qb):
@@ -155,14 +182,14 @@
 def prev_kernel(q_ref, kv_ref, dq_ref, dkv_ref, *scratch):
     start_sums(dq_ref, dkv_ref)
     fill_rows(q_ref, *scratch[3:])
-    walk(q_ref, kv_ref, 0, False, dq_ref, dkv_ref, *scratch)
+    walk(q_ref, kv_ref, 0, (kv_ref, 2 * T, 0), False, dq_ref, dkv_ref, *scratch)
 
 
 def own_kernel(q_ref, kv_ref, sum_ref, dq_ref, dkv_ref, dq_s, *scratch):
     dq_s[...] = sum_ref[...]
     dkv_ref[...] = jnp.zeros_like(dkv_ref)
     fill_rows(q_ref, *scratch[3:])
-    walk(q_ref, kv_ref, KROWS, True, dq_s, dkv_ref, *scratch)
+    walk(q_ref, kv_ref, KROWS, (q_ref, 4 * T, 12), True, dq_s, dkv_ref, *scratch)
     for u in range(U):
         dkv_ref[u, 0:T, :] = dkv_ref[u, 0:T, :] * SCALE
         for h in range(2):
@@ -170,15 +197,30 @@
 
 
 def far_kernel(q_ref, prev_ref, sum_ref, dq_ref, dkv_ref, dq_s, dkv_s, *scratch):
-    dq_s[...] = jnp.zeros_like(dq_s)
-    dkv_s[...] = sum_ref[...]
-    fill_rows(q_ref, *scratch[3:])
-    walk(q_ref, prev_ref, 0, False, dq_s, dkv_s, *scratch)
-    for u in range(U):
-        dkv_ref[u, 0:T, :] = (dkv_s[u, 0:T, :] * SCALE).astype(BF16)
-        dkv_ref[u, T : 2 * T, :] = dkv_s[u, T : 2 * T, :].astype(BF16)
-        for h in range(2):
-            dq_ref[u, h * T : (h + 1) * T, :] = turned(dq_s, u, h).astype(BF16)
+    ids = (prev_ref, 2 * T, 0)
+    head = q_ref[0, 4 * T : QROWS, :].astype(F32)[12:13, 0:1]
+    some = matching(ids, head, U) > 0
+
+    def leave(sums):
+        for u in range(U):
+            dkv_ref[u, 0:T, :] = (sums[u, 0:T, :] * SCALE).astype(BF16)
+            dkv_ref[u, T : 2 * T, :] = sums[u, T : 2 * T, :].astype(BF16)
+
+    @pl.when(some)
+    def _():
+        dq_s[...] = jnp.zeros_like(dq_s)
+        dkv_s[...] = sum_ref[...]
+        fill_rows(q_ref, *scratch[3:])
+        walk(q_ref, prev_ref, 0, ids, False, dq_s, dkv_s, *scratch)
+        leave(dkv_s)
+        for u in range(U):
+            for h in range(2):
+                dq_ref[u, h * T : (h + 1) * T, :] = turned(dq_s, u, h).astype(BF16)
+
+    @pl.when(jnp.logical_not(some))
+    def _():
+        leave(sum_ref)
+        dq_ref[...] = jnp.zeros_like(dq_ref)
 
 
 def total_kernel(dq_ref, more_q_ref, dkv_ref, more_kv_ref, out_ref):
@@ -187,21 +229,28 @@
         out_ref[u, 2 * T :, :] = (dkv_ref[u] + more_kv_ref[u].astype(F32)).astype(BF16)
 
 
-def unpack_kernel(in_ref, q_ref, k_ref, v_ref):
+def unpack_kernel(in_ref, q_ref, k_ref, v_ref, sems):
+    copies = []
     for j in range(U):
-        for g in range(2):
-            h = 2 * j + g
-            q_ref[:, h * D : (h + 1) * D] = in_ref[j, g * T : (g + 1) * T, :]
-        k_ref[:, j * D : (j + 1) * D] = in_ref[j, 2 * T : 3 * T, :]
-        v_ref[:, j * D : (j + 1) * D] = in_ref[j, 3 * T : 4 * T, :]
-
-
-def call(kernel, outs, scratch=(), flops=0, limit=16):
+        for part, (ref, block) in enumerate(((q_ref, 2 * j), (q_ref, 2 * j + 1), (k_ref, j), (v_ref, j))):
+            source = in_ref.at[j, pl.ds(part * T, T), :]
+            target = ref.at[:, pl.ds(block * D, D)]
+            copies.append(pltpu.make_async_copy(source, target, sems.at[part, j]))
+    for copy in copies:
+        copy.start()
+    for copy in copies:
+        copy.wait()
+
+
+def call(kernel, outs, scratch=(), flops=0, limit=16, far_in=(), far_out=False):
     many = isinstance(outs, tuple)
+    spec = FAR if far_out else VM
+    more = {"in_specs": [FAR if way else VM for way in far_in]} if far_in else {}
     return pl.pallas_call(
         kernel,
         out_shape=outs,
-        out_specs=(VM,) * len(outs) if many else VM,
+        out_specs=(spec,) * len(outs) if many else spec,
+        **more,
         scratch_shapes=scratch,
         cost_estimate=pl.CostEstimate(flops=flops, bytes_accessed=1 << 20, transcendentals=0),
         compiler_params=pltpu.CompilerParams(vmem_limit_bytes=limit << 20),
@@ -235,19 +284,33 @@
 
 def join_kernel(first_ref, second_ref, out_ref):
     out_ref[:, 0:KROWS, :] = first_ref[...]
-    out_ref[:, KROWS:, :] = second_ref[...]
+    out_ref[:, KROWS:, :] = second_ref[:, 0 : 2 * T, :]
+
+
+def in_hbm(x):
+    return pltpu.with_memory_space_constraint(x, pltpu.HBM)
 
 
 def stages(query, key, value, forward_out, out_grad, lse_parts, ids):
     ids = ids.reshape(1, T)
-    message = call(pack_q_kernel, shape(U, QROWS, D), flops=1 << 20, limit=56)(
-        query, out_grad, forward_out, lse_parts.transpose(1, 2, 0), ids
-    )
+    message = call(
+        pack_q_kernel,
+        shape(U, QROWS, D),
+        [
+            pltpu.VMEM((2 * U, T, D), BF16),
+            pltpu.VMEM((2 * U, 2, T), F32),
+            pltpu.VMEM((1, T), jnp.int32),
+            pltpu.SemaphoreType.DMA((3, 2 * U)),
+            pltpu.SemaphoreType.DMA((2,)),
+        ],
+        flops=1 << 20,
+        far_in=(True,) * 5,
+    )(*map(in_hbm, (query, out_grad, forward_out, lse_parts.transpose(1, 2, 0), ids)))
     rows = exchanged(message)
     kv_msg = call(pack_kv_kernel, shape(U, KROWS, D), flops=1 << 20)(key, value, ids)
     prev_raw = moved(kv_msg, 1)
     later_rows = moved(rows, -1)
-    both = call(join_kernel, shape(U, 2 * KROWS, D), flops=1 << 20)(prev_raw, kv_msg)
+    both = call(join_kernel, shape(U, KROWS + 2 * T, D), flops=1 << 20)(prev_raw, kv_msg)
     keys = exchanged(both)
     tall, wide, half = shape(U, 2 * T, D, dtype=F32), shape(U, D, 2 * T, dtype=F32), shape(U, 2 * T, D)
     dq, dprev = call(prev_kernel, (wide, tall), KEYS, flops=4 << 30)(rows, keys)
@@ -256,7 +319,14 @@
     dq_back = moved(dq_msg, 1)
     dq, down = call(own_kernel, (tall, tall), (SUM_Q,) + KEYS, flops=4 << 30)(rows, keys, dq)
     total = call(total_kernel, shape(U, 4 * T, D), flops=1 << 20)(dq, dq_back, down, dkv_back)
-    return call(unpack_kernel, (shape(T, 2 * U * D), shape(T, U * D), shape(T, U * D)), flops=1 << 20)(exchanged(total))
+    return call(
+        unpack_kernel,
+        (shape(T, 2 * U * D), shape(T, U * D), shape(T, U * D)),
+        [pltpu.SemaphoreType.DMA((4, U))],
+        flops=1 << 20,
+        far_in=(False,),
+        far_out=True,
+    )(exchanged(total))
 
 
 def solution(mesh):

time: 112 us -> 113 us (level)
    pallas_call x2, Pallas kernels: 3.98 us -> 5.48 us  [the longest x1 4.4 us: stages(): call(pack_q_kernel, shape(U, QROWS, D), [pltpu.VMEM((2 * U, T, D), BF16),...]
where the time goes in v5:
time: 113 us; the launch traced here: 112 us
  waiting for transfers between devices  46.9 us (42%)
  starting transfers between devices  29.3 us (26%)
  blocking collectives  20.8 us (18%)
  Pallas kernels  14.4 us (13%)
    ppermute x4, waiting for transfers between devices, moved(): lax.ppermute(block, 'blk', [(i, (i + distance) % count) for i in range(co...  35 us
    all_to_all x1, blocking collectives, exchanged(): return lax.all_to_all(message, ULY, 0, 0, tiled=True)  20.8 us
    all_to_all x2, starting transfers between devices, exchanged(): return lax.all_to_all(message, ULY, 0, 0, tiled=True)  15.4 us
    ppermute x4, starting transfers between devices, moved(): lax.ppermute(block, 'blk', [(i, (i + distance) % count) for i in range(co...  13.9 us
    all_to_all x2, waiting for transfers between devices, exchanged(): return lax.all_to_all(message, ULY, 0, 0, tiled=True)  12 us
    pallas_call x1, Pallas kernels, stages(): call(own_kernel, (tall, tall), (SUM_Q,) + KEYS, flops=4 << 30)  6.51 us
    pallas_call x1, Pallas kernels, stages(): call(pack_q_kernel, shape(U, QROWS, D), [pltpu.VMEM((2 * U, T, D), BF16),...  4.4 us
  transfers between devices with their start and end apart: 6, of which 5 were waited for; matrix products, arithmetic and copies ran while one was open for 0% of the time, Pallas kernels for 7%

profile of v5, /device:TPU:1, one launch (start us, length us, event | category | flops | bytes accessed | tf_op | source)
XLA Modules:
  0.0 112.2 jit_solution(15448760922914784553)
XLA Ops:
  0.6 4.4 %shard_map.94 = bf16[8,528,128]{2,1,0:T(8,128)(2,1)} custom-call(bf16[128,2048]{1,0:T(8,128)(2,1)} %q_ref.1, bf16[128,2048]{1,0:T(8,128)(2,1)} %g_ref.1, bf16[128,2048]{1,0:T(8,128)(2,1)} %o_ref.1, f32[16,2,128]{2,1,0:T(2,128)} %bitcast.4, s32[1,128]{1,0:T(1,128)} %bitcast.2), custom_call_target="tpu_custom_call" | custom-call | flops 1048576 | bytes 1048576 | tf_op jit(solution)/shard_map/pallas_call | solution.py:296
  5.0 0.0 copy-start
  5.1 0.0 copy-start.1
  5.1 0.0 copy-start.2
  5.1 10.4 %all-to-all-start = ((bf16[8,528,128]{2,1,0:T(8,128)(2,1)}), bf16[8,528,128]{2,1,0:T(8,128)(2,1)S(1)}, u32[]{:S(2)}, u32[]{:S(2)}) async-start(bf16[8,528,128]{2,1,0:T(8,128)(2,1)} %shard_map.94), calls=%async_computation | async-start | bytes 2162688 | tf_op jit(solution)/shard_map/all_to_all | solution.py:277
  15.5 0.0 copy-done
  15.5 0.0 copy-done.1
  15.5 0.0 copy-done.2
  15.5 0.1 shard_map.95.second_ref
  15.6 1.9 %collective-permute-start = (bf16[8,272,128]{2,1,0:T(8,128)(2,1)S(1)}, bf16[8,272,128]{2,1,0:T(8,128)(2,1)S(1)}, u32[]{:S(2)}, u32[]{:S(2)}) collective-permute-start(bf16[8,272,128]{2,1,0:T(8,128)(2,1)S(1)} %shard_map.95.second_ref), channel_id=1, source_target_pairs={{0,1},{1,2},{2,3},{3,4},{4,5},{5,6},{6,7},{7,8},{8,9},{9,10},{10,1... | collective-permute-start | bytes 1671176 | tf_op jit(solution)/shard_map/ppermute | solution.py:282
  17.6 20.0 %collective-permute-done.first_ref = bf16[8,272,128]{2,1,0:T(8,128)(2,1)S(1)} collective-permute-done((bf16[8,272,128]{2,1,0:T(8,128)(2,1)S(1)}, bf16[8,272,128]{2,1,0:T(8,128)(2,1)S(1)}, u32[]{:S(2)}, u32[]{:S(2)}) %collective-permute-start) | collective-permute-done | bytes 557088 | tf_op jit(solution)/shard_map/ppermute | solution.py:282
  37.6 1.1 shard_map.96
  38.7 0.0 all-to-all-done.q_ref
  38.7 5.0 %all-to-all-start.1 = ((bf16[8,528,128]{2,1,0:T(8,128)(2,1)}), bf16[8,528,128]{2,1,0:T(8,128)(2,1)S(1)}, u32[]{:S(2)}, u32[]{:S(2)}) async-start(bf16[8,528,128]{2,1,0:T(8,128)(2,1)} %shard_map.96), calls=%async_computation.1 | async-start | bytes 2162688 | tf_op jit(solution)/shard_map/all_to_all | solution.py:277
  43.7 3.4 %collective-permute-start.1 = (bf16[8,528,128]{2,1,0:T(8,128)(2,1)S(1)}, bf16[8,528,128]{2,1,0:T(8,128)(2,1)S(1)}, u32[]{:S(2)}, u32[]{:S(2)}) collective-permute-start(bf16[8,528,128]{2,1,0:T(8,128)(2,1)S(1)} %all-to-all-done.q_ref), channel_id=1, source_target_pairs={{0,63},{1,0},{2,1},{3,2},{4,3},{5,4},{6,5},{7,6},{8,7},{9,8},{10,9... | collective-permute-start | bytes 3244040 | tf_op jit(solution)/shard_map/ppermute | solution.py:282
  47.0 12.0 %all-to-all-done.1.kv_ref.prev_ref = bf16[8,528,128]{2,1,0:T(8,128)(2,1)S(1)} async-done(((bf16[8,528,128]{2,1,0:T(8,128)(2,1)}), bf16[8,528,128]{2,1,0:T(8,128)(2,1)S(1)}, u32[]{:S(2)}, u32[]{:S(2)}) %all-to-all-start.1) | async-done | bytes 1081376 | tf_op jit(solution)/shard_map/all_to_all | solution.py:277
  59.0 0.6 shard_map.97
  59.7 11.3 %collective-permute-done.1.q_ref = bf16[8,528,128]{2,1,0:T(8,128)(2,1)S(1)} collective-permute-done((bf16[8,528,128]{2,1,0:T(8,128)(2,1)S(1)}, bf16[8,528,128]{2,1,0:T(8,128)(2,1)S(1)}, u32[]{:S(2)}, u32[]{:S(2)}) %collective-permute-start.1) | collective-permute-done | bytes 1081376 | tf_op jit(solution)/shard_map/ppermute | solution.py:282
  71.0 0.3 shard_map.99
  71.3 1.9 %collective-permute-start.2 = (bf16[8,256,128]{2,1,0:T(8,128)(2,1)S(1)}, bf16[8,256,128]{2,1,0:T(8,128)(2,1)S(1)}, u32[]{:S(2)}, u32[]{:S(2)}) collective-permute-start(bf16[8,256,128]{2,1,0:T(8,128)(2,1)S(1)} %get-tuple-element.12), channel_id=1, source_target_pairs={{0,1},{1,2},{2,3},{3,4},{4,5},{5,6},{6,7},{7,8},{8,9},{9,10},{10,1... | collective-permute-start | bytes 1572872 | tf_op jit(solution)/shard_map/ppermute | solution.py:282
  73.2 6.7 %collective-permute-start.3 = (bf16[8,256,128]{2,1,0:T(8,128)(2,1)S(1)}, bf16[8,256,128]{2,1,0:T(8,128)(2,1)S(1)}, u32[]{:S(2)}, u32[]{:S(2)}) collective-permute-start(bf16[8,256,128]{2,1,0:T(8,128)(2,1)S(1)} %get-tuple-element.14), channel_id=1, source_target_pairs={{0,63},{1,0},{2,1},{3,2},{4,3},{5,4},{6,5},{7,6},{8,7},{9,8},{10,9... | collective-permute-start | bytes 1572872 | tf_op jit(solution)/shard_map/ppermute | solution.py:282
  79.9 6.5 %shard_map.98 = (f32[8,256,128]{2,1,0:T(8,128)S(1)}, f32[8,256,128]{2,1,0:T(8,128)S(1)}) custom-call(bf16[8,528,128]{2,1,0:T(8,128)(2,1)S(1)} %all-to-all-done.q_ref, bf16[8,528,128]{2,1,0:T(8,128)(2,1)S(1)} %all-to-all-done.1.kv_ref.prev_ref, f32[8,128,256]{2,1,0:T(8,128)S(1)} %get-tuple-element.9.sum_ref), custom_call_target="tpu_custom_call" | custom-call | flops 4294967296 | bytes 1048576 | tf_op jit(solution)/shard_map/pallas_call | solution.py:320
  86.4 2.7 %collective-permute-done.2.more_q_ref = bf16[8,256,128]{2,1,0:T(8,128)(2,1)S(1)} collective-permute-done((bf16[8,256,128]{2,1,0:T(8,128)(2,1)S(1)}, bf16[8,256,128]{2,1,0:T(8,128)(2,1)S(1)}, u32[]{:S(2)}, u32[]{:S(2)}) %collective-permute-start.2) | collective-permute-done | bytes 524320 | tf_op jit(solution)/shard_map/ppermute | solution.py:282
  89.2 0.9 collective-permute-done.3.more_kv_ref
  90.1 0.2 shard_map.100
  90.2 20.8 %all_to_all.15.in_ref = bf16[8,512,128]{2,1,0:T(8,128)(2,1)S(1)} all-to-all(bf16[8,512,128]{2,1,0:T(8,128)(2,1)S(1)} %shard_map.100), channel_id=1, replica_groups=mesh['uly_0'=4,'uly_1'=2,'blk'=64] {'uly_0','uly_1'}, dimensions={0} | all-to-all | bytes 2097152 | tf_op jit(solution)/shard_map/all_to_all | solution.py:277
  111.0 1.2 %shard_map.101 = (bf16[128,2048]{1,0:T(8,128)(2,1)}, bf16[128,1024]{1,0:T(8,128)(2,1)}, bf16[128,1024]{1,0:T(8,128)(2,1)}) custom-call(bf16[8,512,128]{2,1,0:T(8,128)(2,1)S(1)} %all_to_all.15.in_ref), custom_call_target="tpu_custom_call" | custom-call | flops 1048576 | bytes 1048576 | tf_op jit(solution)/shard_map/pallas_call | solution.py:322
Async XLA Ops:
  5.0 10.5 %copy-start = (bf16[128,1024]{1,0:T(8,128)(2,1)S(1)}, bf16[128,1024]{1,0:T(8,128)(2,1)}, u32[]{:S(2)}) copy-start(bf16[128,1024]{1,0:T(8,128)(2,1)} %k_ref.1) | copy-start | bytes 786436
  5.1 10.5 %copy-start.1 = (bf16[128,1024]{1,0:T(8,128)(2,1)S(1)}, bf16[128,1024]{1,0:T(8,128)(2,1)}, u32[]{:S(2)}) copy-start(bf16[128,1024]{1,0:T(8,128)(2,1)} %v_ref.1) | copy-start | bytes 786436
  5.1 10.5 %copy-start.2 = (s32[128]{0:T(128)S(1)}, s32[128]{0:T(128)}, u32[]{:S(2)}) copy-start(s32[128]{0:T(128)} %param.13) | copy-start | bytes 1540
  5.1 33.6 %all-to-all-start = ((bf16[8,528,128]{2,1,0:T(8,128)(2,1)}), bf16[8,528,128]{2,1,0:T(8,128)(2,1)S(1)}, u32[]{:S(2)}, u32[]{:S(2)}) async-start(bf16[8,528,128]{2,1,0:T(8,128)(2,1)} %shard_map.94), calls=%async_computation | async-start | bytes 2162688 | tf_op jit(solution)/shard_map/all_to_all | solution.py:277
  15.6 22.0 %collective-permute-start = (bf16[8,272,128]{2,1,0:T(8,128)(2,1)S(1)}, bf16[8,272,128]{2,1,0:T(8,128)(2,1)S(1)}, u32[]{:S(2)}, u32[]{:S(2)}) collective-permute-start(bf16[8,272,128]{2,1,0:T(8,128)(2,1)S(1)} %shard_map.95.second_ref), channel_id=1, source_target_pairs={{0,1},{1,2},{2,3},{3,4},{4,5},{5,6},{6,7},{7,8},{8,9},{9,10},{10,1... | collective-permute-start | bytes 1671176 | tf_op jit(solution)/shard_map/ppermute | solution.py:282
  38.7 20.3 %all-to-all-start.1 = ((bf16[8,528,128]{2,1,0:T(8,128)(2,1)}), bf16[8,528,128]{2,1,0:T(8,128)(2,1)S(1)}, u32[]{:S(2)}, u32[]{:S(2)}) async-start(bf16[8,528,128]{2,1,0:T(8,128)(2,1)} %shard_map.96), calls=%async_computation.1 | async-start | bytes 2162688 | tf_op jit(solution)/shard_map/all_to_all | solution.py:277
  43.7 27.3 %collective-permute-start.1 = (bf16[8,528,128]{2,1,0:T(8,128)(2,1)S(1)}, bf16[8,528,128]{2,1,0:T(8,128)(2,1)S(1)}, u32[]{:S(2)}, u32[]{:S(2)}) collective-permute-start(bf16[8,528,128]{2,1,0:T(8,128)(2,1)S(1)} %all-to-all-done.q_ref), channel_id=1, source_target_pairs={{0,63},{1,0},{2,1},{3,2},{4,3},{5,4},{6,5},{7,6},{8,7},{9,8},{10,9... | collective-permute-start | bytes 3244040 | tf_op jit(solution)/shard_map/ppermute | solution.py:282
  71.3 17.8 %collective-permute-start.2 = (bf16[8,256,128]{2,1,0:T(8,128)(2,1)S(1)}, bf16[8,256,128]{2,1,0:T(8,128)(2,1)S(1)}, u32[]{:S(2)}, u32[]{:S(2)}) collective-permute-start(bf16[8,256,128]{2,1,0:T(8,128)(2,1)S(1)} %get-tuple-element.12), channel_id=1, source_target_pairs={{0,1},{1,2},{2,3},{3,4},{4,5},{5,6},{6,7},{7,8},{8,9},{9,10},{10,1... | collective-permute-start | bytes 1572872 | tf_op jit(solution)/shard_map/ppermute | solution.py:282
  73.2 16.8 %collective-permute-start.3 = (bf16[8,256,128]{2,1,0:T(8,128)(2,1)S(1)}, bf16[8,256,128]{2,1,0:T(8,128)(2,1)S(1)}, u32[]{:S(2)}, u32[]{:S(2)}) collective-permute-start(bf16[8,256,128]{2,1,0:T(8,128)(2,1)S(1)} %get-tuple-element.14), channel_id=1, source_target_pairs={{0,63},{1,0},{2,1},{3,2},{4,3},{5,4},{6,5},{7,6},{8,7},{9,8},{10,9... | collective-permute-start | bytes 1572872 | tf_op jit(solution)/shard_map/ppermute | solution.py:282

commit v6 on v4

--- a/solution.py
+++ b/solution.py
@@ -13,7 +13,8 @@
 T = 128
 U = 8
 KB = 256
-QP = 2
+QP = 4
+FAR_QP = 2
 STAT = 16
 KROWS = 2 * T + STAT
 QROWS = 4 * T + STAT
@@ -76,27 +77,29 @@
         qid_s[u, 0:1, :] = st[12:13]
 
 
-def fill_keys(kv_ref, first, k_s, v_s, kid_s):
-    pick = (lax.broadcasted_iota(jnp.int32, (STAT, D), 0) == 0).astype(F32).astype(BF16)
+def fill_keys(kv_ref, first, ids, k_s, v_s, kid_s):
+    id_ref, start, row = ids
+    pick = (lax.broadcasted_iota(jnp.int32, (STAT, D), 0) == row).astype(F32).astype(BF16)
     for u in range(U):
         b, r = divmod(u, KB // T)
         rows = slice(r * T, (r + 1) * T)
         k_s[b, rows, :] = kv_ref[u, first : first + T, :]
         v_s[b, rows, :] = kv_ref[u, first + T : first + 2 * T, :]
-        kid_s[b, rows, :] = dot(kv_ref[u, first + 2 * T : first + KROWS, :], pick, 0, 0)
-
-
-def matching(kv_ref, first, qid, upto):
+        kid_s[b, rows, :] = dot(id_ref[u, start : start + STAT, :], pick, 0, 0)
+
+
+def matching(ids, qid, upto):
+    id_ref, start, row = ids
     total = jnp.zeros((1, T), F32)
     for u in range(upto):
-        ids = kv_ref[u, first + 2 * T : first + 2 * T + 1, :].astype(F32)
-        total = total + jnp.where(ids == qid, 1.0, 0.0)
+        here = id_ref[u, start : start + STAT, :].astype(F32)[row : row + 1]
+        total = total + jnp.where(here == qid, 1.0, 0.0)
     return jnp.sum(total).astype(jnp.int32)
 
 
-def tile(q_ref, k_s, v_s, kid_s, lse_s, del_s, qid_s, dq_s, dkv_ref, qb, kb, causal):
+def tile(q_ref, k_s, v_s, kid_s, lse_s, del_s, qid_s, dq_s, dkv_ref, qb, kb, causal, qp):
     k, v = k_s[kb], v_s[kb]
-    us = [qb * QP + i for i in range(QP)]
+    us = [qb * qp + i for i in range(qp)]
     q = jnp.concatenate([q_ref[u, 0 : 2 * T, :] for u in us], axis=0)
     g = jnp.concatenate([q_ref[u, 2 * T : 4 * T, :] for u in us], axis=0)
     st = dot(k, q, 1, 1)
@@ -139,30 +142,30 @@
     dkv_s[...] = jnp.zeros_like(dkv_s)
 
 
-def walk(q_ref, kv_ref, first, causal, dq_s, dkv_s, k_s, v_s, kid_s, lse_s, del_s, qid_s):
-    fill_keys(kv_ref, first, k_s, v_s, kid_s)
-    for qb in range(U // QP):
-        head = qid_s[qb * QP, 0:1, 0:1]
-        before = qb * QP if causal else U
-        upto = (qb + 1) * QP if causal else U
-        live = matching(kv_ref, first, head, before)
+def walk(qp, q_ref, kv_ref, first, ids, causal, dq_s, dkv_s, k_s, v_s, kid_s, lse_s, del_s, qid_s):
+    fill_keys(kv_ref, first, ids, k_s, v_s, kid_s)
+    for qb in range(U // qp):
+        head = qid_s[qb * qp, 0:1, 0:1]
+        before = qb * qp if causal else U
+        upto = (qb + 1) * qp if causal else U
+        live = matching(ids, head, before)
 
         @pl.loop((before * T - live) // KB, upto * T // KB)
         def _(kb, qb=qb):
-            tile(q_ref, k_s, v_s, kid_s, lse_s, del_s, qid_s, dq_s, dkv_s, qb, kb, causal)
+            tile(q_ref, k_s, v_s, kid_s, lse_s, del_s, qid_s, dq_s, dkv_s, qb, kb, causal, qp)
 
 
 def prev_kernel(q_ref, kv_ref, dq_ref, dkv_ref, *scratch):
     start_sums(dq_ref, dkv_ref)
     fill_rows(q_ref, *scratch[3:])
-    walk(q_ref, kv_ref, 0, False, dq_ref, dkv_ref, *scratch)
+    walk(QP, q_ref, kv_ref, 0, (kv_ref, 2 * T, 0), False, dq_ref, dkv_ref, *scratch)
 
 
 def own_kernel(q_ref, kv_ref, sum_ref, dq_ref, dkv_ref, dq_s, *scratch):
     dq_s[...] = sum_ref[...]
     dkv_ref[...] = jnp.zeros_like(dkv_ref)
     fill_rows(q_ref, *scratch[3:])
-    walk(q_ref, kv_ref, KROWS, True, dq_s, dkv_ref, *scratch)
+    walk(QP, q_ref, kv_ref, KROWS, (q_ref, 4 * T, 12), True, dq_s, dkv_ref, *scratch)
     for u in range(U):
         dkv_ref[u, 0:T, :] = dkv_ref[u, 0:T, :] * SCALE
         for h in range(2):
@@ -170,15 +173,30 @@
 
 
 def far_kernel(q_ref, prev_ref, sum_ref, dq_ref, dkv_ref, dq_s, dkv_s, *scratch):
-    dq_s[...] = jnp.zeros_like(dq_s)
-    dkv_s[...] = sum_ref[...]
-    fill_rows(q_ref, *scratch[3:])
-    walk(q_ref, prev_ref, 0, False, dq_s, dkv_s, *scratch)
-    for u in range(U):
-        dkv_ref[u, 0:T, :] = (dkv_s[u, 0:T, :] * SCALE).astype(BF16)
-        dkv_ref[u, T : 2 * T, :] = dkv_s[u, T : 2 * T, :].astype(BF16)
-        for h in range(2):
-            dq_ref[u, h * T : (h + 1) * T, :] = turned(dq_s, u, h).astype(BF16)
+    ids = (prev_ref, 2 * T, 0)
+    head = q_ref[0, 4 * T : QROWS, :].astype(F32)[12:13, 0:1]
+    some = matching(ids, head, U) > 0
+
+    def leave(sums):
+        for u in range(U):
+            dkv_ref[u, 0:T, :] = (sums[u, 0:T, :] * SCALE).astype(BF16)
+            dkv_ref[u, T : 2 * T, :] = sums[u, T : 2 * T, :].astype(BF16)
+
+    @pl.when(some)
+    def _():
+        dq_s[...] = jnp.zeros_like(dq_s)
+        dkv_s[...] = sum_ref[...]
+        fill_rows(q_ref, *scratch[3:])
+        walk(FAR_QP, q_ref, prev_ref, 0, ids, False, dq_s, dkv_s, *scratch)
+        leave(dkv_s)
+        for u in range(U):
+            for h in range(2):
+                dq_ref[u, h * T : (h + 1) * T, :] = turned(dq_s, u, h).astype(BF16)
+
+    @pl.when(jnp.logical_not(some))
+    def _():
+        leave(sum_ref)
+        dq_ref[...] = jnp.zeros_like(dq_ref)
 
 
 def total_kernel(dq_ref, more_q_ref, dkv_ref, more_kv_ref, out_ref):
@@ -235,19 +253,23 @@
 
 def join_kernel(first_ref, second_ref, out_ref):
     out_ref[:, 0:KROWS, :] = first_ref[...]
-    out_ref[:, KROWS:, :] = second_ref[...]
+    out_ref[:, KROWS:, :] = second_ref[:, 0 : 2 * T, :]
+
+
+def in_hbm(x):
+    return pltpu.with_memory_space_constraint(x, pltpu.HBM)
 
 
 def stages(query, key, value, forward_out, out_grad, lse_parts, ids):
     ids = ids.reshape(1, T)
-    message = call(pack_q_kernel, shape(U, QROWS, D), flops=1 << 20, limit=56)(
-        query, out_grad, forward_out, lse_parts.transpose(1, 2, 0), ids
+    message = call(pack_q_kernel, shape(U, QROWS, D), flops=1 << 20)(
+        *map(in_hbm, (query, out_grad, forward_out, lse_parts.transpose(1, 2, 0), ids))
     )
     rows = exchanged(message)
     kv_msg = call(pack_kv_kernel, shape(U, KROWS, D), flops=1 << 20)(key, value, ids)
     prev_raw = moved(kv_msg, 1)
     later_rows = moved(rows, -1)
-    both = call(join_kernel, shape(U, 2 * KROWS, D), flops=1 << 20)(prev_raw, kv_msg)
+    both = call(join_kernel, shape(U, KROWS + 2 * T, D), flops=1 << 20)(prev_raw, kv_msg)
     keys = exchanged(both)
     tall, wide, half = shape(U, 2 * T, D, dtype=F32), shape(U, D, 2 * T, dtype=F32), shape(U, 2 * T, D)
     dq, dprev = call(prev_kernel, (wide, tall), KEYS, flops=4 << 30)(rows, keys)

time: 112 us -> 111 us (level)
  the two profiles are of different devices: /device:TPU:1 before, /device:TPU:2 now
where the time goes in v6:
time: 111 us
  waiting for transfers between devices  43.4 us (39%)
  starting transfers between devices  24.4 us (22%)
  Pallas kernels  22.6 us (20%)
  blocking collectives  19.8 us (18%)
    ppermute x4, waiting for transfers between devices, moved(): lax.ppermute(block, 'blk', [(i, (i + distance) % count) for i in range(co...  30.7 us
    all_to_all x1, blocking collectives, exchanged(): return lax.all_to_all(message, ULY, 0, 0, tiled=True)  19.8 us
    ppermute x4, starting transfers between devices, moved(): lax.ppermute(block, 'blk', [(i, (i + distance) % count) for i in range(co...  15.4 us
    all_to_all x2, waiting for transfers between devices, exchanged(): return lax.all_to_all(message, ULY, 0, 0, tiled=True)  12.6 us
    all_to_all x2, starting transfers between devices, exchanged(): return lax.all_to_all(message, ULY, 0, 0, tiled=True)  9.02 us
    pallas_call x1, Pallas kernels, stages(): call(own_kernel, (tall, tall), (SUM_Q,) + KEYS, flops=4 << 30)  6.51 us
    pallas_call x1, Pallas kernels, stages(): dq, dprev = call(prev_kernel, (wide, tall), KEYS, flops=4 << 30)(rows, keys)  6.12 us
    pallas_call x1, Pallas kernels, stages(): call(far_kernel, (half, half), (SUM_Q, SUM_KV) + KEYS, flops=1 << 30)  4.52 us
  transfers between devices with their start and end apart: 6, of which 5 were waited for; matrix products, arithmetic and copies ran while one was open for 0% of the time, Pallas kernels for 12%

profile of v6, /device:TPU:2, one launch (start us, length us, event | category | flops | bytes accessed | tf_op | source)
XLA Modules:
  0.0 111.0 jit_solution(2409823288157253665)
XLA Ops:
  0.6 2.9 %shard_map.94 = bf16[8,528,128]{2,1,0:T(8,128)(2,1)} custom-call(bf16[128,2048]{1,0:T(8,128)(2,1)} %q_ref.1, bf16[128,2048]{1,0:T(8,128)(2,1)} %g_ref.1, bf16[128,2048]{1,0:T(8,128)(2,1)} %o_ref.1, f32[16,2,128]{2,1,0:T(2,128)} %bitcast.4, s32[1,128]{1,0:T(1,128)} %bitcast.2), custom_call_target="tpu_custom_call" | custom-call | flops 1048576 | bytes 1048576 | tf_op jit(solution)/shard_map/pallas_call | solution.py:265
  3.5 0.0 copy-start
  3.5 0.0 copy-start.1
  3.5 0.0 copy-start.2
  3.5 4.6 %all-to-all-start = ((bf16[8,528,128]{2,1,0:T(8,128)(2,1)}), bf16[8,528,128]{2,1,0:T(8,128)(2,1)S(1)}, u32[]{:S(2)}, u32[]{:S(2)}) async-start(bf16[8,528,128]{2,1,0:T(8,128)(2,1)} %shard_map.94), calls=%async_computation | async-start | bytes 2162688 | tf_op jit(solution)/shard_map/all_to_all | solution.py:246
  8.1 0.0 copy-done
  8.1 0.0 copy-done.1
  8.1 0.0 copy-done.2
  8.2 0.1 shard_map.95.second_ref
  8.3 3.8 %collective-permute-start = (bf16[8,272,128]{2,1,0:T(8,128)(2,1)S(1)}, bf16[8,272,128]{2,1,0:T(8,128)(2,1)S(1)}, u32[]{:S(2)}, u32[]{:S(2)}) collective-permute-start(bf16[8,272,128]{2,1,0:T(8,128)(2,1)S(1)} %shard_map.95.second_ref), channel_id=1, source_target_pairs={{0,1},{1,2},{2,3},{3,4},{4,5},{5,6},{6,7},{7,8},{8,9},{9,10},{10,1... | collective-permute-start | bytes 1671176 | tf_op jit(solution)/shard_map/ppermute | solution.py:251
  12.1 20.8 %collective-permute-done.first_ref = bf16[8,272,128]{2,1,0:T(8,128)(2,1)S(1)} collective-permute-done((bf16[8,272,128]{2,1,0:T(8,128)(2,1)S(1)}, bf16[8,272,128]{2,1,0:T(8,128)(2,1)S(1)}, u32[]{:S(2)}, u32[]{:S(2)}) %collective-permute-start) | collective-permute-done | bytes 557088 | tf_op jit(solution)/shard_map/ppermute | solution.py:251
  32.9 1.1 shard_map.96
  34.0 0.0 all-to-all-done.q_ref
  34.0 4.4 %all-to-all-start.1 = ((bf16[8,528,128]{2,1,0:T(8,128)(2,1)}), bf16[8,528,128]{2,1,0:T(8,128)(2,1)S(1)}, u32[]{:S(2)}, u32[]{:S(2)}) async-start(bf16[8,528,128]{2,1,0:T(8,128)(2,1)} %shard_map.96), calls=%async_computation.1 | async-start | bytes 2162688 | tf_op jit(solution)/shard_map/all_to_all | solution.py:246
  38.4 3.6 %collective-permute-start.1 = (bf16[8,528,128]{2,1,0:T(8,128)(2,1)S(1)}, bf16[8,528,128]{2,1,0:T(8,128)(2,1)S(1)}, u32[]{:S(2)}, u32[]{:S(2)}) collective-permute-start(bf16[8,528,128]{2,1,0:T(8,128)(2,1)S(1)} %all-to-all-done.q_ref), channel_id=1, source_target_pairs={{0,63},{1,0},{2,1},{3,2},{4,3},{5,4},{6,5},{7,6},{8,7},{9,8},{10,9... | collective-permute-start | bytes 3244040 | tf_op jit(solution)/shard_map/ppermute | solution.py:251
  42.1 12.6 %all-to-all-done.1.kv_ref.prev_ref = bf16[8,528,128]{2,1,0:T(8,128)(2,1)S(1)} async-done(((bf16[8,528,128]{2,1,0:T(8,128)(2,1)}), bf16[8,528,128]{2,1,0:T(8,128)(2,1)S(1)}, u32[]{:S(2)}, u32[]{:S(2)}) %all-to-all-start.1) | async-done | bytes 1081376 | tf_op jit(solution)/shard_map/all_to_all | solution.py:246
  54.7 6.1 %shard_map.97 = (f32[8,128,256]{2,1,0:T(8,128)S(1)}, f32[8,256,128]{2,1,0:T(8,128)S(1)}) custom-call(bf16[8,528,128]{2,1,0:T(8,128)(2,1)S(1)} %all-to-all-done.q_ref, bf16[8,528,128]{2,1,0:T(8,128)(2,1)S(1)} %all-to-all-done.1.kv_ref.prev_ref), custom_call_target="tpu_custom_call" | custom-call | flops 4294967296 | bytes 1048576 | tf_op jit(solution)/shard_map/pallas_call | solution.py:275
  60.8 5.7 %collective-permute-done.1.q_ref = bf16[8,528,128]{2,1,0:T(8,128)(2,1)S(1)} collective-permute-done((bf16[8,528,128]{2,1,0:T(8,128)(2,1)S(1)}, bf16[8,528,128]{2,1,0:T(8,128)(2,1)S(1)}, u32[]{:S(2)}, u32[]{:S(2)}) %collective-permute-start.1) | collective-permute-done | bytes 1081376 | tf_op jit(solution)/shard_map/ppermute | solution.py:251
  66.6 4.5 %shard_map.99 = (bf16[8,256,128]{2,1,0:T(8,128)(2,1)S(1)}, bf16[8,256,128]{2,1,0:T(8,128)(2,1)S(1)}) custom-call(bf16[8,528,128]{2,1,0:T(8,128)(2,1)S(1)} %collective-permute-done.1.q_ref, bf16[8,528,128]{2,1,0:T(8,128)(2,1)S(1)} %all-to-all-done.1.kv_ref.prev_ref, f32[8,256,128]{2,1,0:T(8,128)S(1)} %get-tuple-element.11.sum_ref), custom_call_target="tpu_custom_call" | custom-call | flops 1073741824 | bytes 1048576 | tf_op jit(solution)/shard_map/pallas_call | solution.py:276
  71.1 1.9 %collective-permute-start.2 = (bf16[8,256,128]{2,1,0:T(8,128)(2,1)S(1)}, bf16[8,256,128]{2,1,0:T(8,128)(2,1)S(1)}, u32[]{:S(2)}, u32[]{:S(2)}) collective-permute-start(bf16[8,256,128]{2,1,0:T(8,128)(2,1)S(1)} %get-tuple-element.12), channel_id=1, source_target_pairs={{0,1},{1,2},{2,3},{3,4},{4,5},{5,6},{6,7},{7,8},{8,9},{9,10},{10,1... | collective-permute-start | bytes 1572872 | tf_op jit(solution)/shard_map/ppermute | solution.py:251
  73.0 6.0 %collective-permute-start.3 = (bf16[8,256,128]{2,1,0:T(8,128)(2,1)S(1)}, bf16[8,256,128]{2,1,0:T(8,128)(2,1)S(1)}, u32[]{:S(2)}, u32[]{:S(2)}) collective-permute-start(bf16[8,256,128]{2,1,0:T(8,128)(2,1)S(1)} %get-tuple-element.14), channel_id=1, source_target_pairs={{0,63},{1,0},{2,1},{3,2},{4,3},{5,4},{6,5},{7,6},{8,7},{9,8},{10,9... | collective-permute-start | bytes 1572872 | tf_op jit(solution)/shard_map/ppermute | solution.py:251
  79.1 6.5 %shard_map.98 = (f32[8,256,128]{2,1,0:T(8,128)S(1)}, f32[8,256,128]{2,1,0:T(8,128)S(1)}) custom-call(bf16[8,528,128]{2,1,0:T(8,128)(2,1)S(1)} %all-to-all-done.q_ref, bf16[8,528,128]{2,1,0:T(8,128)(2,1)S(1)} %all-to-all-done.1.kv_ref.prev_ref, f32[8,128,256]{2,1,0:T(8,128)S(1)} %get-tuple-element.9.sum_ref), custom_call_target="tpu_custom_call" | custom-call | flops 4294967296 | bytes 1048576 | tf_op jit(solution)/shard_map/pallas_call | solution.py:279
  85.6 3.0 %collective-permute-done.2.more_q_ref = bf16[8,256,128]{2,1,0:T(8,128)(2,1)S(1)} collective-permute-done((bf16[8,256,128]{2,1,0:T(8,128)(2,1)S(1)}, bf16[8,256,128]{2,1,0:T(8,128)(2,1)S(1)}, u32[]{:S(2)}, u32[]{:S(2)}) %collective-permute-start.2) | collective-permute-done | bytes 524320 | tf_op jit(solution)/shard_map/ppermute | solution.py:251
  88.6 1.2 %collective-permute-done.3.more_kv_ref = bf16[8,256,128]{2,1,0:T(8,128)(2,1)S(1)} collective-permute-done((bf16[8,256,128]{2,1,0:T(8,128)(2,1)S(1)}, bf16[8,256,128]{2,1,0:T(8,128)(2,1)S(1)}, u32[]{:S(2)}, u32[]{:S(2)}) %collective-permute-start.3) | collective-permute-done | bytes 524320 | tf_op jit(solution)/shard_map/ppermute | solution.py:251
  89.8 0.2 shard_map.100
  90.0 19.8 %all_to_all.15.in_ref = bf16[8,512,128]{2,1,0:T(8,128)(2,1)S(1)} all-to-all(bf16[8,512,128]{2,1,0:T(8,128)(2,1)S(1)} %shard_map.100), channel_id=1, replica_groups=mesh['uly_0'=4,'uly_1'=2,'blk'=64] {'uly_0','uly_1'}, dimensions={0} | all-to-all | bytes 2097152 | tf_op jit(solution)/shard_map/all_to_all | solution.py:246
  109.7 1.2 %shard_map.101 = (bf16[128,2048]{1,0:T(8,128)(2,1)}, bf16[128,1024]{1,0:T(8,128)(2,1)}, bf16[128,1024]{1,0:T(8,128)(2,1)}) custom-call(bf16[8,512,128]{2,1,0:T(8,128)(2,1)S(1)} %all_to_all.15.in_ref), custom_call_target="tpu_custom_call" | custom-call | flops 1048576 | bytes 1048576 | tf_op jit(solution)/shard_map/pallas_call | solution.py:281
Async XLA Ops:
  3.5 4.6 %copy-start = (bf16[128,1024]{1,0:T(8,128)(2,1)S(1)}, bf16[128,1024]{1,0:T(8,128)(2,1)}, u32[]{:S(2)}) copy-start(bf16[128,1024]{1,0:T(8,128)(2,1)} %k_ref.1) | copy-start | bytes 786436
  3.5 4.6 %copy-start.1 = (bf16[128,1024]{1,0:T(8,128)(2,1)S(1)}, bf16[128,1024]{1,0:T(8,128)(2,1)}, u32[]{:S(2)}) copy-start(bf16[128,1024]{1,0:T(8,128)(2,1)} %v_ref.1) | copy-start | bytes 786436
  3.5 4.6 %copy-start.2 = (s32[128]{0:T(128)S(1)}, s32[128]{0:T(128)}, u32[]{:S(2)}) copy-start(s32[128]{0:T(128)} %param.13) | copy-start | bytes 1540
  3.5 30.5 %all-to-all-start = ((bf16[8,528,128]{2,1,0:T(8,128)(2,1)}), bf16[8,528,128]{2,1,0:T(8,128)(2,1)S(1)}, u32[]{:S(2)}, u32[]{:S(2)}) async-start(bf16[8,528,128]{2,1,0:T(8,128)(2,1)} %shard_map.94), calls=%async_computation | async-start | bytes 2162688 | tf_op jit(solution)/shard_map/all_to_all | solution.py:246
  8.3 24.7 %collective-permute-start = (bf16[8,272,128]{2,1,0:T(8,128)(2,1)S(1)}, bf16[8,272,128]{2,1,0:T(8,128)(2,1)S(1)}, u32[]{:S(2)}, u32[]{:S(2)}) collective-permute-start(bf16[8,272,128]{2,1,0:T(8,128)(2,1)S(1)} %shard_map.95.second_ref), channel_id=1, source_target_pairs={{0,1},{1,2},{2,3},{3,4},{4,5},{5,6},{6,7},{7,8},{8,9},{9,10},{10,1... | collective-permute-start | bytes 1671176 | tf_op jit(solution)/shard_map/ppermute | solution.py:251
  34.0 20.7 %all-to-all-start.1 = ((bf16[8,528,128]{2,1,0:T(8,128)(2,1)}), bf16[8,528,128]{2,1,0:T(8,128)(2,1)S(1)}, u32[]{:S(2)}, u32[]{:S(2)}) async-start(bf16[8,528,128]{2,1,0:T(8,128)(2,1)} %shard_map.96), calls=%async_computation.1 | async-start | bytes 2162688 | tf_op jit(solution)/shard_map/all_to_all | solution.py:246
  38.4 28.2 %collective-permute-start.1 = (bf16[8,528,128]{2,1,0:T(8,128)(2,1)S(1)}, bf16[8,528,128]{2,1,0:T(8,128)(2,1)S(1)}, u32[]{:S(2)}, u32[]{:S(2)}) collective-permute-start(bf16[8,528,128]{2,1,0:T(8,128)(2,1)S(1)} %all-to-all-done.q_ref), channel_id=1, source_target_pairs={{0,63},{1,0},{2,1},{3,2},{4,3},{5,4},{6,5},{7,6},{8,7},{9,8},{10,9... | collective-permute-start | bytes 3244040 | tf_op jit(solution)/shard_map/ppermute | solution.py:251
  71.1 17.5 %collective-permute-start.2 = (bf16[8,256,128]{2,1,0:T(8,128)(2,1)S(1)}, bf16[8,256,128]{2,1,0:T(8,128)(2,1)S(1)}, u32[]{:S(2)}, u32[]{:S(2)}) collective-permute-start(bf16[8,256,128]{2,1,0:T(8,128)(2,1)S(1)} %get-tuple-element.12), channel_id=1, source_target_pairs={{0,1},{1,2},{2,3},{3,4},{4,5},{5,6},{6,7},{7,8},{8,9},{9,10},{10,1... | collective-permute-start | bytes 1572872 | tf_op jit(solution)/shard_map/ppermute | solution.py:251
  73.0 16.7 %collective-permute-start.3 = (bf16[8,256,128]{2,1,0:T(8,128)(2,1)S(1)}, bf16[8,256,128]{2,1,0:T(8,128)(2,1)S(1)}, u32[]{:S(2)}, u32[]{:S(2)}) collective-permute-start(bf16[8,256,128]{2,1,0:T(8,128)(2,1)S(1)} %get-tuple-element.14), channel_id=1, source_target_pairs={{0,63},{1,0},{2,1},{3,2},{4,3},{5,4},{6,5},{7,6},{8,7},{9,8},{10,9... | collective-permute-start | bytes 1572872 | tf_op jit(solution)/shard_map/ppermute | solution.py:251

commit v7 on v6

--- a/solution.py
+++ b/solution.py
@@ -1,3 +1,4 @@
+import functools
 import math
 
 import jax
@@ -67,7 +68,7 @@
 
 
 def fill_rows(q_ref, lse_s, del_s, qid_s):
-    for u in range(U):
+    for u in range(q_ref.shape[0]):
         st = q_ref[u, 4 * T : QROWS, :].astype(F32)
         two = st[0:2] + st[2:4] + st[4:6]
         dlt = st[6:8] + st[8:10] + st[10:12]
@@ -144,7 +145,7 @@
 
 def walk(qp, q_ref, kv_ref, first, ids, causal, dq_s, dkv_s, k_s, v_s, kid_s, lse_s, del_s, qid_s):
     fill_keys(kv_ref, first, ids, k_s, v_s, kid_s)
-    for qb in range(U // qp):
+    for qb in range(q_ref.shape[0] // qp):
         head = qid_s[qb * qp, 0:1, 0:1]
         before = qb * qp if causal else U
         upto = (qb + 1) * qp if causal else U
@@ -172,15 +173,18 @@
             dq_ref[u, h * T : (h + 1) * T, :] = turned(dq_s, u, h)
 
 
-def far_kernel(q_ref, prev_ref, sum_ref, dq_ref, dkv_ref, dq_s, dkv_s, *scratch):
+def far_kernel(last, q_ref, prev_ref, sum_ref, dq_ref, dkv_ref, dq_s, dkv_s, *scratch):
     ids = (prev_ref, 2 * T, 0)
     head = q_ref[0, 4 * T : QROWS, :].astype(F32)[12:13, 0:1]
     some = matching(ids, head, U) > 0
 
     def leave(sums):
         for u in range(U):
-            dkv_ref[u, 0:T, :] = (sums[u, 0:T, :] * SCALE).astype(BF16)
-            dkv_ref[u, T : 2 * T, :] = sums[u, T : 2 * T, :].astype(BF16)
+            if last:
+                dkv_ref[u, 0:T, :] = (sums[u, 0:T, :] * SCALE).astype(BF16)
+                dkv_ref[u, T : 2 * T, :] = sums[u, T : 2 * T, :].astype(BF16)
+            else:
+                dkv_ref[u] = sums[u]
 
     @pl.when(some)
     def _():
@@ -189,7 +193,7 @@
         fill_rows(q_ref, *scratch[3:])
         walk(FAR_QP, q_ref, prev_ref, 0, ids, False, dq_s, dkv_s, *scratch)
         leave(dkv_s)
-        for u in range(U):
+        for u in range(U // 2):
             for h in range(2):
                 dq_ref[u, h * T : (h + 1) * T, :] = turned(dq_s, u, h).astype(BF16)
 
@@ -199,9 +203,10 @@
         dq_ref[...] = jnp.zeros_like(dq_ref)
 
 
-def total_kernel(dq_ref, more_q_ref, dkv_ref, more_kv_ref, out_ref):
+def total_kernel(dq_ref, front_ref, back_ref, dkv_ref, more_kv_ref, out_ref):
     for u in range(U):
-        out_ref[u, 0 : 2 * T, :] = (dq_ref[u] + more_q_ref[u].astype(F32)).astype(BF16)
+        more_q = front_ref[u] if u < U // 2 else back_ref[u - U // 2]
+        out_ref[u, 0 : 2 * T, :] = (dq_ref[u] + more_q.astype(F32)).astype(BF16)
         out_ref[u, 2 * T :, :] = (dkv_ref[u] + more_kv_ref[u].astype(F32)).astype(BF16)
 
 
@@ -268,16 +273,21 @@
     rows = exchanged(message)
     kv_msg = call(pack_kv_kernel, shape(U, KROWS, D), flops=1 << 20)(key, value, ids)
     prev_raw = moved(kv_msg, 1)
-    later_rows = moved(rows, -1)
+    front = moved(rows[: U // 2], -1)
+    back = moved(rows[U // 2 :], -1)
     both = call(join_kernel, shape(U, KROWS + 2 * T, D), flops=1 << 20)(prev_raw, kv_msg)
     keys = exchanged(both)
     tall, wide, half = shape(U, 2 * T, D, dtype=F32), shape(U, D, 2 * T, dtype=F32), shape(U, 2 * T, D)
     dq, dprev = call(prev_kernel, (wide, tall), KEYS, flops=4 << 30)(rows, keys)
-    dq_msg, dkv_msg = call(far_kernel, (half, half), (SUM_Q, SUM_KV) + KEYS, flops=1 << 30)(later_rows, keys, dprev)
+    part = shape(U // 2, 2 * T, D)
+    sums = (pltpu.VMEM((U // 2, D, 2 * T), F32), SUM_KV) + KEYS
+    dq_front, dprev = call(functools.partial(far_kernel, False), (part, tall), sums, flops=1 << 30)(front, keys, dprev)
+    dq_front = moved(dq_front, 1)
+    dq_tail, dkv_msg = call(functools.partial(far_kernel, True), (part, half), sums, flops=1 << 30)(back, keys, dprev)
     dkv_back = moved(dkv_msg, -1)
-    dq_back = moved(dq_msg, 1)
+    dq_tail = moved(dq_tail, 1)
     dq, down = call(own_kernel, (tall, tall), (SUM_Q,) + KEYS, flops=4 << 30)(rows, keys, dq)
-    total = call(total_kernel, shape(U, 4 * T, D), flops=1 << 20)(dq, dq_back, down, dkv_back)
+    total = call(total_kernel, shape(U, 4 * T, D), flops=1 << 20)(dq, dq_front, dq_tail, down, dkv_back)
     return call(unpack_kernel, (shape(T, 2 * U * D), shape(T, U * D), shape(T, U * D)), flops=1 << 20)(exchanged(total))
 
 

time: 111 us -> 118 us (1.063)
  the two profiles are of different devices: /device:TPU:2 before, /device:TPU:1 now
where the time goes in v7:
time: 118 us; the launch traced here: 117 us
  waiting for transfers between devices  47.8 us (41%)
  starting transfers between devices  33.9 us (29%)
  blocking collectives  20.8 us (18%)
  Pallas kernels  13.2 us (11%)
    ppermute x6, waiting for transfers between devices, moved(): lax.ppermute(block, 'blk', [(i, (i + distance) % count) for i in range(co...  39.5 us
    all_to_all x1, blocking collectives, exchanged(): return lax.all_to_all(message, ULY, 0, 0, tiled=True)  20.8 us
    ppermute x6, starting transfers between devices, moved(): lax.ppermute(block, 'blk', [(i, (i + distance) % count) for i in range(co...  18.4 us
    all_to_all x2, starting transfers between devices, exchanged(): return lax.all_to_all(message, ULY, 0, 0, tiled=True)  15.4 us
    all_to_all x2, waiting for transfers between devices, exchanged(): return lax.all_to_all(message, ULY, 0, 0, tiled=True)  8.26 us
    pallas_call x1, Pallas kernels, stages(): call(own_kernel, (tall, tall), (SUM_Q,) + KEYS, flops=4 << 30)  6.51 us
    pallas_call x1, Pallas kernels, stages(): call(pack_q_kernel, shape(U, QROWS, D), flops=1 << 20)  2.88 us
  transfers between devices with their start and end apart: 8, of which 6 were waited for; matrix products, arithmetic and copies ran while one was open for 1% of the time, Pallas kernels for 7%

profile of v7, /device:TPU:1, one launch (start us, length us, event | category | flops | bytes accessed | tf_op | source)
XLA Modules:
  0.0 117.4 jit_solution(2055870276292211540)
XLA Ops:
  0.6 2.9 %shard_map.94 = bf16[8,528,128]{2,1,0:T(8,128)(2,1)} custom-call(bf16[128,2048]{1,0:T(8,128)(2,1)} %q_ref.1, bf16[128,2048]{1,0:T(8,128)(2,1)} %g_ref.1, bf16[128,2048]{1,0:T(8,128)(2,1)} %o_ref.1, f32[16,2,128]{2,1,0:T(2,128)} %bitcast.4, s32[1,128]{1,0:T(1,128)} %bitcast.2), custom_call_target="tpu_custom_call" | custom-call | flops 1048576 | bytes 1048576 | tf_op jit(solution)/shard_map/pallas_call | solution.py:270
  3.5 0.0 copy-start
  3.5 0.0 copy-start.1
  3.5 0.0 copy-start.2
  3.5 10.4 %all-to-all-start = ((bf16[8,528,128]{2,1,0:T(8,128)(2,1)}), bf16[8,528,128]{2,1,0:T(8,128)(2,1)S(1)}, u32[]{:S(2)}, u32[]{:S(2)}) async-start(bf16[8,528,128]{2,1,0:T(8,128)(2,1)} %shard_map.94), calls=%async_computation | async-start | bytes 2162688 | tf_op jit(solution)/shard_map/all_to_all | solution.py:251
  14.0 0.0 copy-done
  14.0 0.0 copy-done.1
  14.0 0.0 copy-done.2
  14.0 0.1 shard_map.95.second_ref
  14.1 1.9 %collective-permute-start = (bf16[8,272,128]{2,1,0:T(8,128)(2,1)S(1)}, bf16[8,272,128]{2,1,0:T(8,128)(2,1)S(1)}, u32[]{:S(2)}, u32[]{:S(2)}) collective-permute-start(bf16[8,272,128]{2,1,0:T(8,128)(2,1)S(1)} %shard_map.95.second_ref), channel_id=1, source_target_pairs={{0,1},{1,2},{2,3},{3,4},{4,5},{5,6},{6,7},{7,8},{8,9},{9,10},{10,1... | collective-permute-start | bytes 1671176 | tf_op jit(solution)/shard_map/ppermute | solution.py:256
  16.0 20.0 %collective-permute-done.first_ref = bf16[8,272,128]{2,1,0:T(8,128)(2,1)S(1)} collective-permute-done((bf16[8,272,128]{2,1,0:T(8,128)(2,1)S(1)}, bf16[8,272,128]{2,1,0:T(8,128)(2,1)S(1)}, u32[]{:S(2)}, u32[]{:S(2)}) %collective-permute-start) | collective-permute-done | bytes 557088 | tf_op jit(solution)/shard_map/ppermute | solution.py:256
  36.0 1.1 shard_map.96
  37.1 0.0 all-to-all-done.q_ref
  37.1 5.0 %all-to-all-start.1 = ((bf16[8,528,128]{2,1,0:T(8,128)(2,1)}), bf16[8,528,128]{2,1,0:T(8,128)(2,1)S(1)}, u32[]{:S(2)}, u32[]{:S(2)}) async-start(bf16[8,528,128]{2,1,0:T(8,128)(2,1)} %shard_map.96), calls=%async_computation.1 | async-start | bytes 2162688 | tf_op jit(solution)/shard_map/all_to_all | solution.py:251
  42.1 1.1 fusion
  43.2 3.3 %collective-permute-start.1 = (bf16[4,528,128]{2,1,0:T(8,128)(2,1)}, bf16[4,528,128]{2,1,0:T(8,128)(2,1)S(1)}, u32[]{:S(2)}, u32[]{:S(2)}) collective-permute-start(bf16[4,528,128]{2,1,0:T(8,128)(2,1)} %get-tuple-element.20), channel_id=1, source_target_pairs={{0,63},{1,0},{2,1},{3,2},{4,3},{5,4},{6,5},{7,6},{8,7},{9,8},{10,9... | collective-permute-start | bytes 1622024 | tf_op jit(solution)/shard_map/ppermute | solution.py:256
  46.5 2.6 %collective-permute-start.3 = (bf16[4,528,128]{2,1,0:T(8,128)(2,1)}, bf16[4,528,128]{2,1,0:T(8,128)(2,1)S(1)}, u32[]{:S(2)}, u32[]{:S(2)}) collective-permute-start(bf16[4,528,128]{2,1,0:T(8,128)(2,1)} %get-tuple-element.19), channel_id=1, source_target_pairs={{0,63},{1,0},{2,1},{3,2},{4,3},{5,4},{6,5},{7,6},{8,7},{9,8},{10,9... | collective-permute-start | bytes 1622024 | tf_op jit(solution)/shard_map/ppermute | solution.py:256
  49.2 8.3 %all-to-all-done.1.kv_ref.prev_ref = bf16[8,528,128]{2,1,0:T(8,128)(2,1)S(1)} async-done(((bf16[8,528,128]{2,1,0:T(8,128)(2,1)}), bf16[8,528,128]{2,1,0:T(8,128)(2,1)S(1)}, u32[]{:S(2)}, u32[]{:S(2)}) %all-to-all-start.1) | async-done | bytes 1081376 | tf_op jit(solution)/shard_map/all_to_all | solution.py:251
  57.4 0.6 shard_map.97
  58.1 1.0 collective-permute-done.1.q_ref
  59.1 0.3 shard_map.99
  59.4 11.3 %collective-permute-done.3.q_ref = bf16[4,528,128]{2,1,0:T(8,128)(2,1)S(1)} collective-permute-done((bf16[4,528,128]{2,1,0:T(8,128)(2,1)}, bf16[4,528,128]{2,1,0:T(8,128)(2,1)S(1)}, u32[]{:S(2)}, u32[]{:S(2)}) %collective-permute-start.3) | collective-permute-done | bytes 540704 | tf_op jit(solution)/shard_map/ppermute | solution.py:256
  70.7 0.3 shard_map.100
  71.0 6.7 %collective-permute-start.5 = (bf16[8,256,128]{2,1,0:T(8,128)(2,1)S(1)}, bf16[8,256,128]{2,1,0:T(8,128)(2,1)S(1)}, u32[]{:S(2)}, u32[]{:S(2)}) collective-permute-start(bf16[8,256,128]{2,1,0:T(8,128)(2,1)S(1)} %get-tuple-element.18), channel_id=1, source_target_pairs={{0,63},{1,0},{2,1},{3,2},{4,3},{5,4},{6,5},{7,6},{8,7},{9,8},{10,9... | collective-permute-start | bytes 1572872 | tf_op jit(solution)/shard_map/ppermute | solution.py:256
  77.7 1.9 %collective-permute-start.2 = (bf16[4,256,128]{2,1,0:T(8,128)(2,1)S(1)}, bf16[4,256,128]{2,1,0:T(8,128)(2,1)S(1)}, u32[]{:S(2)}, u32[]{:S(2)}) collective-permute-start(bf16[4,256,128]{2,1,0:T(8,128)(2,1)S(1)} %get-tuple-element.14), channel_id=1, source_target_pairs={{0,1},{1,2},{2,3},{3,4},{4,5},{5,6},{6,7},{7,8},{8,9},{9,10},{10,1... | collective-permute-start | bytes 786440 | tf_op jit(solution)/shard_map/ppermute | solution.py:256
  79.6 1.9 %collective-permute-start.4 = (bf16[4,256,128]{2,1,0:T(8,128)(2,1)S(1)}, bf16[4,256,128]{2,1,0:T(8,128)(2,1)S(1)}, u32[]{:S(2)}, u32[]{:S(2)}) collective-permute-start(bf16[4,256,128]{2,1,0:T(8,128)(2,1)S(1)} %get-tuple-element.16), channel_id=1, source_target_pairs={{0,1},{1,2},{2,3},{3,4},{4,5},{5,6},{6,7},{7,8},{8,9},{9,10},{10,1... | collective-permute-start | bytes 786440 | tf_op jit(solution)/shard_map/ppermute | solution.py:256
  81.5 6.5 %shard_map.98 = (f32[8,256,128]{2,1,0:T(8,128)S(1)}, f32[8,256,128]{2,1,0:T(8,128)S(1)}) custom-call(bf16[8,528,128]{2,1,0:T(8,128)(2,1)S(1)} %all-to-all-done.q_ref, bf16[8,528,128]{2,1,0:T(8,128)(2,1)S(1)} %all-to-all-done.1.kv_ref.prev_ref, f32[8,128,256]{2,1,0:T(8,128)S(1)} %get-tuple-element.11.sum_ref), custom_call_target="tpu_custom_call" | custom-call | flops 4294967296 | bytes 1048576 | tf_op jit(solution)/shard_map/pallas_call | solution.py:289
  88.0 1.6 %collective-permute-done.2.front_ref = bf16[4,256,128]{2,1,0:T(8,128)(2,1)S(1)} collective-permute-done((bf16[4,256,128]{2,1,0:T(8,128)(2,1)S(1)}, bf16[4,256,128]{2,1,0:T(8,128)(2,1)S(1)}, u32[]{:S(2)}, u32[]{:S(2)}) %collective-permute-start.2) | collective-permute-done | bytes 262176 | tf_op jit(solution)/shard_map/ppermute | solution.py:256
  89.6 5.6 %collective-permute-done.4.back_ref = bf16[4,256,128]{2,1,0:T(8,128)(2,1)S(1)} collective-permute-done((bf16[4,256,128]{2,1,0:T(8,128)(2,1)S(1)}, bf16[4,256,128]{2,1,0:T(8,128)(2,1)S(1)}, u32[]{:S(2)}, u32[]{:S(2)}) %collective-permute-start.4) | collective-permute-done | bytes 262176 | tf_op jit(solution)/shard_map/ppermute | solution.py:256
  95.2 0.0 collective-permute-done.5.more_kv_ref
  95.2 0.2 shard_map.101
  95.4 20.8 %all_to_all.15.in_ref = bf16[8,512,128]{2,1,0:T(8,128)(2,1)S(1)} all-to-all(bf16[8,512,128]{2,1,0:T(8,128)(2,1)S(1)} %shard_map.101), channel_id=1, replica_groups=mesh['uly_0'=4,'uly_1'=2,'blk'=64] {'uly_0','uly_1'}, dimensions={0} | all-to-all | bytes 2097152 | tf_op jit(solution)/shard_map/all_to_all | solution.py:251
  116.1 1.2 %shard_map.102 = (bf16[128,2048]{1,0:T(8,128)(2,1)}, bf16[128,1024]{1,0:T(8,128)(2,1)}, bf16[128,1024]{1,0:T(8,128)(2,1)}) custom-call(bf16[8,512,128]{2,1,0:T(8,128)(2,1)S(1)} %all_to_all.15.in_ref), custom_call_target="tpu_custom_call" | custom-call | flops 1048576 | bytes 1048576 | tf_op jit(solution)/shard_map/pallas_call | solution.py:291
Async XLA Ops:
  3.5 10.4 %copy-start = (bf16[128,1024]{1,0:T(8,128)(2,1)S(1)}, bf16[128,1024]{1,0:T(8,128)(2,1)}, u32[]{:S(2)}) copy-start(bf16[128,1024]{1,0:T(8,128)(2,1)} %k_ref.1) | copy-start | bytes 786436
  3.5 10.4 %copy-start.1 = (bf16[128,1024]{1,0:T(8,128)(2,1)S(1)}, bf16[128,1024]{1,0:T(8,128)(2,1)}, u32[]{:S(2)}) copy-start(bf16[128,1024]{1,0:T(8,128)(2,1)} %v_ref.1) | copy-start | bytes 786436
  3.5 10.5 %copy-start.2 = (s32[128]{0:T(128)S(1)}, s32[128]{0:T(128)}, u32[]{:S(2)}) copy-start(s32[128]{0:T(128)} %param.13) | copy-start | bytes 1540
  3.5 33.6 %all-to-all-start = ((bf16[8,528,128]{2,1,0:T(8,128)(2,1)}), bf16[8,528,128]{2,1,0:T(8,128)(2,1)S(1)}, u32[]{:S(2)}, u32[]{:S(2)}) async-start(bf16[8,528,128]{2,1,0:T(8,128)(2,1)} %shard_map.94), calls=%async_computation | async-start | bytes 2162688 | tf_op jit(solution)/shard_map/all_to_all | solution.py:251
  14.1 22.0 %collective-permute-start = (bf16[8,272,128]{2,1,0:T(8,128)(2,1)S(1)}, bf16[8,272,128]{2,1,0:T(8,128)(2,1)S(1)}, u32[]{:S(2)}, u32[]{:S(2)}) collective-permute-start(bf16[8,272,128]{2,1,0:T(8,128)(2,1)S(1)} %shard_map.95.second_ref), channel_id=1, source_target_pairs={{0,1},{1,2},{2,3},{3,4},{4,5},{5,6},{6,7},{7,8},{8,9},{9,10},{10,1... | collective-permute-start | bytes 1671176 | tf_op jit(solution)/shard_map/ppermute | solution.py:256
  37.1 20.3 %all-to-all-start.1 = ((bf16[8,528,128]{2,1,0:T(8,128)(2,1)}), bf16[8,528,128]{2,1,0:T(8,128)(2,1)S(1)}, u32[]{:S(2)}, u32[]{:S(2)}) async-start(bf16[8,528,128]{2,1,0:T(8,128)(2,1)} %shard_map.96), calls=%async_computation.1 | async-start | bytes 2162688 | tf_op jit(solution)/shard_map/all_to_all | solution.py:251
  43.2 15.9 %collective-permute-start.1 = (bf16[4,528,128]{2,1,0:T(8,128)(2,1)}, bf16[4,528,128]{2,1,0:T(8,128)(2,1)S(1)}, u32[]{:S(2)}, u32[]{:S(2)}) collective-permute-start(bf16[4,528,128]{2,1,0:T(8,128)(2,1)} %get-tuple-element.20), channel_id=1, source_target_pairs={{0,63},{1,0},{2,1},{3,2},{4,3},{5,4},{6,5},{7,6},{8,7},{9,8},{10,9... | collective-permute-start | bytes 1622024 | tf_op jit(solution)/shard_map/ppermute | solution.py:256
  46.5 24.1 %collective-permute-start.3 = (bf16[4,528,128]{2,1,0:T(8,128)(2,1)}, bf16[4,528,128]{2,1,0:T(8,128)(2,1)S(1)}, u32[]{:S(2)}, u32[]{:S(2)}) collective-permute-start(bf16[4,528,128]{2,1,0:T(8,128)(2,1)} %get-tuple-element.19), channel_id=1, source_target_pairs={{0,63},{1,0},{2,1},{3,2},{4,3},{5,4},{6,5},{7,6},{8,7},{9,8},{10,9... | collective-permute-start | bytes 1622024 | tf_op jit(solution)/shard_map/ppermute | solution.py:256
  71.0 24.2 %collective-permute-start.5 = (bf16[8,256,128]{2,1,0:T(8,128)(2,1)S(1)}, bf16[8,256,128]{2,1,0:T(8,128)(2,1)S(1)}, u32[]{:S(2)}, u32[]{:S(2)}) collective-permute-start(bf16[8,256,128]{2,1,0:T(8,128)(2,1)S(1)} %get-tuple-element.18), channel_id=1, source_target_pairs={{0,63},{1,0},{2,1},{3,2},{4,3},{5,4},{6,5},{7,6},{8,7},{9,8},{10,9... | collective-permute-start | bytes 1572872 | tf_op jit(solution)/shard_map/ppermute | solution.py:256
  77.7 11.9 %collective-permute-start.2 = (bf16[4,256,128]{2,1,0:T(8,128)(2,1)S(1)}, bf16[4,256,128]{2,1,0:T(8,128)(2,1)S(1)}, u32[]{:S(2)}, u32[]{:S(2)}) collective-permute-start(bf16[4,256,128]{2,1,0:T(8,128)(2,1)S(1)} %get-tuple-element.14), channel_id=1, source_target_pairs={{0,1},{1,2},{2,3},{3,4},{4,5},{5,6},{6,7},{7,8},{8,9},{9,10},{10,1... | collective-permute-start | bytes 786440 | tf_op jit(solution)/shard_map/ppermute | solution.py:256
  79.6 15.6 %collective-permute-start.4 = (bf16[4,256,128]{2,1,0:T(8,128)(2,1)S(1)}, bf16[4,256,128]{2,1,0:T(8,128)(2,1)S(1)}, u32[]{:S(2)}, u32[]{:S(2)}) collective-permute-start(bf16[4,256,128]{2,1,0:T(8,128)(2,1)S(1)} %get-tuple-element.16), channel_id=1, source_target_pairs={{0,1},{1,2},{2,3},{3,4},{4,5},{5,6},{6,7},{7,8},{8,9},{9,10},{10,1... | collective-permute-start | bytes 786440 | tf_op jit(solution)/shard_map/ppermute | solution.py:256

commit v8 on v6

--- a/solution.py
+++ b/solution.py
@@ -32,7 +32,7 @@
 
 
 def pack_kv_kernel(k_ref, v_ref, id_ref, out_ref):
-    ids = jnp.broadcast_to(id_ref[...].astype(F32), (STAT, T)).astype(BF16)
+    ids = jnp.broadcast_to((id_ref[...] + 1).astype(F32), (STAT, T)).astype(BF16)
     for j in range(U):
         out_ref[j, 0:T, :] = k_ref[:, j * D : (j + 1) * D]
         out_ref[j, T : 2 * T, :] = v_ref[:, j * D : (j + 1) * D]
@@ -60,7 +60,7 @@
         out_ref[j, g * T : (g + 1) * T, :] = q_ref[:, cols]
         out_ref[j, (2 + g) * T : (3 + g) * T, :] = g_ref[:, cols]
     parts = three(lse) + three(deltas.T)
-    ids = jnp.broadcast_to(id_ref[...].astype(F32), (4, T))
+    ids = jnp.broadcast_to((id_ref[...] + 1).astype(F32), (4, T))
     for j in range(U):
         rows = [p[2 * j : 2 * j + 2, :] for p in parts] + [ids]
         out_ref[j, 4 * T : QROWS, :] = jnp.concatenate(rows, axis=0).astype(BF16)
@@ -248,7 +248,8 @@
 
 def moved(block, distance):
     count = lax.axis_size("blk")
-    return lax.ppermute(block, "blk", [(i, (i + distance) % count) for i in range(count)])
+    route = [(i, i + distance) for i in range(count) if 0 <= i + distance < count]
+    return lax.ppermute(block, "blk", route)
 
 
 def join_kernel(first_ref, second_ref, out_ref):

time: 111 us -> 111 us (level)
  no operation moved by 1% of the time
where the time goes in v8:
time: 111 us
  waiting for transfers between devices  43.4 us (39%)
  starting transfers between devices  24.4 us (22%)
  Pallas kernels  22.6 us (20%)
  blocking collectives  19.8 us (18%)
    ppermute x4, waiting for transfers between devices, moved(): return lax.ppermute(block, 'blk', route)  30.8 us
    all_to_all x1, blocking collectives, exchanged(): return lax.all_to_all(message, ULY, 0, 0, tiled=True)  19.8 us
    ppermute x4, starting transfers between devices, moved(): return lax.ppermute(block, 'blk', route)  15.4 us
    all_to_all x2, waiting for transfers between devices, exchanged(): return lax.all_to_all(message, ULY, 0, 0, tiled=True)  12.6 us
    all_to_all x2, starting transfers between devices, exchanged(): return lax.all_to_all(message, ULY, 0, 0, tiled=True)  9.02 us
    pallas_call x1, Pallas kernels, stages(): call(own_kernel, (tall, tall), (SUM_Q,) + KEYS, flops=4 << 30)  6.51 us
    pallas_call x1, Pallas kernels, stages(): dq, dprev = call(prev_kernel, (wide, tall), KEYS, flops=4 << 30)(rows, keys)  6.11 us
    pallas_call x1, Pallas kernels, stages(): call(far_kernel, (half, half), (SUM_Q, SUM_KV) + KEYS, flops=1 << 30)  4.52 us
  transfers between devices with their start and end apart: 6, of which 5 were waited for; matrix products, arithmetic and copies ran while one was open for 0% of the time, Pallas kernels for 12%

profile of v8, /device:TPU:2, one launch (start us, length us, event | category | flops | bytes accessed | tf_op | source)
XLA Modules:
  0.0 111.0 jit_solution(9135374637813199104)
XLA Ops:
  0.6 2.9 %shard_map.94 = bf16[8,528,128]{2,1,0:T(8,128)(2,1)} custom-call(bf16[128,2048]{1,0:T(8,128)(2,1)} %q_ref.1, bf16[128,2048]{1,0:T(8,128)(2,1)} %g_ref.1, bf16[128,2048]{1,0:T(8,128)(2,1)} %o_ref.1, f32[16,2,128]{2,1,0:T(2,128)} %bitcast.4, s32[1,128]{1,0:T(1,128)} %bitcast.2), custom_call_target="tpu_custom_call" | custom-call | flops 1048576 | bytes 1048576 | tf_op jit(solution)/shard_map/pallas_call | solution.py:266
  3.5 0.0 copy-start
  3.5 0.0 copy-start.1
  3.5 0.0 copy-start.2
  3.5 4.6 %all-to-all-start = ((bf16[8,528,128]{2,1,0:T(8,128)(2,1)}), bf16[8,528,128]{2,1,0:T(8,128)(2,1)S(1)}, u32[]{:S(2)}, u32[]{:S(2)}) async-start(bf16[8,528,128]{2,1,0:T(8,128)(2,1)} %shard_map.94), calls=%async_computation | async-start | bytes 2162688 | tf_op jit(solution)/shard_map/all_to_all | solution.py:246
  8.1 0.0 copy-done
  8.1 0.0 copy-done.1
  8.1 0.0 copy-done.2
  8.2 0.1 shard_map.95.second_ref
  8.3 3.8 %collective-permute-start = (bf16[8,272,128]{2,1,0:T(8,128)(2,1)S(1)}, bf16[8,272,128]{2,1,0:T(8,128)(2,1)S(1)}, u32[]{:S(2)}, u32[]{:S(2)}) collective-permute-start(bf16[8,272,128]{2,1,0:T(8,128)(2,1)S(1)} %shard_map.95.second_ref), channel_id=1, source_target_pairs={{0,1},{1,2},{2,3},{3,4},{4,5},{5,6},{6,7},{7,8},{8,9},{9,10},{10,1... | collective-permute-start | bytes 1671176 | tf_op jit(solution)/shard_map/ppermute | solution.py:252
  12.1 20.8 %collective-permute-done.first_ref = bf16[8,272,128]{2,1,0:T(8,128)(2,1)S(1)} collective-permute-done((bf16[8,272,128]{2,1,0:T(8,128)(2,1)S(1)}, bf16[8,272,128]{2,1,0:T(8,128)(2,1)S(1)}, u32[]{:S(2)}, u32[]{:S(2)}) %collective-permute-start) | collective-permute-done | bytes 557088 | tf_op jit(solution)/shard_map/ppermute | solution.py:252
  32.9 1.1 shard_map.96
  34.0 0.0 all-to-all-done.q_ref
  34.0 4.4 %all-to-all-start.1 = ((bf16[8,528,128]{2,1,0:T(8,128)(2,1)}), bf16[8,528,128]{2,1,0:T(8,128)(2,1)S(1)}, u32[]{:S(2)}, u32[]{:S(2)}) async-start(bf16[8,528,128]{2,1,0:T(8,128)(2,1)} %shard_map.96), calls=%async_computation.1 | async-start | bytes 2162688 | tf_op jit(solution)/shard_map/all_to_all | solution.py:246
  38.4 3.6 %collective-permute-start.1 = (bf16[8,528,128]{2,1,0:T(8,128)(2,1)S(1)}, bf16[8,528,128]{2,1,0:T(8,128)(2,1)S(1)}, u32[]{:S(2)}, u32[]{:S(2)}) collective-permute-start(bf16[8,528,128]{2,1,0:T(8,128)(2,1)S(1)} %all-to-all-done.q_ref), channel_id=1, source_target_pairs={{1,0},{2,1},{3,2},{4,3},{5,4},{6,5},{7,6},{8,7},{9,8},{10,9},{11,1... | collective-permute-start | bytes 3244040 | tf_op jit(solution)/shard_map/ppermute | solution.py:252
  42.1 12.6 %all-to-all-done.1.kv_ref.prev_ref = bf16[8,528,128]{2,1,0:T(8,128)(2,1)S(1)} async-done(((bf16[8,528,128]{2,1,0:T(8,128)(2,1)}), bf16[8,528,128]{2,1,0:T(8,128)(2,1)S(1)}, u32[]{:S(2)}, u32[]{:S(2)}) %all-to-all-start.1) | async-done | bytes 1081376 | tf_op jit(solution)/shard_map/all_to_all | solution.py:246
  54.7 6.1 %shard_map.97 = (f32[8,128,256]{2,1,0:T(8,128)S(1)}, f32[8,256,128]{2,1,0:T(8,128)S(1)}) custom-call(bf16[8,528,128]{2,1,0:T(8,128)(2,1)S(1)} %all-to-all-done.q_ref, bf16[8,528,128]{2,1,0:T(8,128)(2,1)S(1)} %all-to-all-done.1.kv_ref.prev_ref), custom_call_target="tpu_custom_call" | custom-call | flops 4294967296 | bytes 1048576 | tf_op jit(solution)/shard_map/pallas_call | solution.py:276
  60.8 5.7 %collective-permute-done.1.q_ref = bf16[8,528,128]{2,1,0:T(8,128)(2,1)S(1)} collective-permute-done((bf16[8,528,128]{2,1,0:T(8,128)(2,1)S(1)}, bf16[8,528,128]{2,1,0:T(8,128)(2,1)S(1)}, u32[]{:S(2)}, u32[]{:S(2)}) %collective-permute-start.1) | collective-permute-done | bytes 1081376 | tf_op jit(solution)/shard_map/ppermute | solution.py:252
  66.6 4.5 %shard_map.99 = (bf16[8,256,128]{2,1,0:T(8,128)(2,1)S(1)}, bf16[8,256,128]{2,1,0:T(8,128)(2,1)S(1)}) custom-call(bf16[8,528,128]{2,1,0:T(8,128)(2,1)S(1)} %collective-permute-done.1.q_ref, bf16[8,528,128]{2,1,0:T(8,128)(2,1)S(1)} %all-to-all-done.1.kv_ref.prev_ref, f32[8,256,128]{2,1,0:T(8,128)S(1)} %get-tuple-element.11.sum_ref), custom_call_target="tpu_custom_call" | custom-call | flops 1073741824 | bytes 1048576 | tf_op jit(solution)/shard_map/pallas_call | solution.py:277
  71.1 1.9 %collective-permute-start.2 = (bf16[8,256,128]{2,1,0:T(8,128)(2,1)S(1)}, bf16[8,256,128]{2,1,0:T(8,128)(2,1)S(1)}, u32[]{:S(2)}, u32[]{:S(2)}) collective-permute-start(bf16[8,256,128]{2,1,0:T(8,128)(2,1)S(1)} %get-tuple-element.12), channel_id=1, source_target_pairs={{0,1},{1,2},{2,3},{3,4},{4,5},{5,6},{6,7},{7,8},{8,9},{9,10},{10,1... | collective-permute-start | bytes 1572872 | tf_op jit(solution)/shard_map/ppermute | solution.py:252
  73.0 6.0 %collective-permute-start.3 = (bf16[8,256,128]{2,1,0:T(8,128)(2,1)S(1)}, bf16[8,256,128]{2,1,0:T(8,128)(2,1)S(1)}, u32[]{:S(2)}, u32[]{:S(2)}) collective-permute-start(bf16[8,256,128]{2,1,0:T(8,128)(2,1)S(1)} %get-tuple-element.14), channel_id=1, source_target_pairs={{1,0},{2,1},{3,2},{4,3},{5,4},{6,5},{7,6},{8,7},{9,8},{10,9},{11,1... | collective-permute-start | bytes 1572872 | tf_op jit(solution)/shard_map/ppermute | solution.py:252
  79.1 6.5 %shard_map.98 = (f32[8,256,128]{2,1,0:T(8,128)S(1)}, f32[8,256,128]{2,1,0:T(8,128)S(1)}) custom-call(bf16[8,528,128]{2,1,0:T(8,128)(2,1)S(1)} %all-to-all-done.q_ref, bf16[8,528,128]{2,1,0:T(8,128)(2,1)S(1)} %all-to-all-done.1.kv_ref.prev_ref, f32[8,128,256]{2,1,0:T(8,128)S(1)} %get-tuple-element.9.sum_ref), custom_call_target="tpu_custom_call" | custom-call | flops 4294967296 | bytes 1048576 | tf_op jit(solution)/shard_map/pallas_call | solution.py:280
  85.6 3.0 %collective-permute-done.2.more_q_ref = bf16[8,256,128]{2,1,0:T(8,128)(2,1)S(1)} collective-permute-done((bf16[8,256,128]{2,1,0:T(8,128)(2,1)S(1)}, bf16[8,256,128]{2,1,0:T(8,128)(2,1)S(1)}, u32[]{:S(2)}, u32[]{:S(2)}) %collective-permute-start.2) | collective-permute-done | bytes 524320 | tf_op jit(solution)/shard_map/ppermute | solution.py:252
  88.6 1.2 %collective-permute-done.3.more_kv_ref = bf16[8,256,128]{2,1,0:T(8,128)(2,1)S(1)} collective-permute-done((bf16[8,256,128]{2,1,0:T(8,128)(2,1)S(1)}, bf16[8,256,128]{2,1,0:T(8,128)(2,1)S(1)}, u32[]{:S(2)}, u32[]{:S(2)}) %collective-permute-start.3) | collective-permute-done | bytes 524320 | tf_op jit(solution)/shard_map/ppermute | solution.py:252
  89.8 0.2 shard_map.100
  90.0 19.8 %all_to_all.15.in_ref = bf16[8,512,128]{2,1,0:T(8,128)(2,1)S(1)} all-to-all(bf16[8,512,128]{2,1,0:T(8,128)(2,1)S(1)} %shard_map.100), channel_id=1, replica_groups=mesh['uly_0'=4,'uly_1'=2,'blk'=64] {'uly_0','uly_1'}, dimensions={0} | all-to-all | bytes 2097152 | tf_op jit(solution)/shard_map/all_to_all | solution.py:246
  109.8 1.2 %shard_map.101 = (bf16[128,2048]{1,0:T(8,128)(2,1)}, bf16[128,1024]{1,0:T(8,128)(2,1)}, bf16[128,1024]{1,0:T(8,128)(2,1)}) custom-call(bf16[8,512,128]{2,1,0:T(8,128)(2,1)S(1)} %all_to_all.15.in_ref), custom_call_target="tpu_custom_call" | custom-call | flops 1048576 | bytes 1048576 | tf_op jit(solution)/shard_map/pallas_call | solution.py:282
Async XLA Ops:
  3.5 4.6 %copy-start = (bf16[128,1024]{1,0:T(8,128)(2,1)S(1)}, bf16[128,1024]{1,0:T(8,128)(2,1)}, u32[]{:S(2)}) copy-start(bf16[128,1024]{1,0:T(8,128)(2,1)} %k_ref.1) | copy-start | bytes 786436
  3.5 4.6 %copy-start.1 = (bf16[128,1024]{1,0:T(8,128)(2,1)S(1)}, bf16[128,1024]{1,0:T(8,128)(2,1)}, u32[]{:S(2)}) copy-start(bf16[128,1024]{1,0:T(8,128)(2,1)} %v_ref.1) | copy-start | bytes 786436
  3.5 4.6 %copy-start.2 = (s32[128]{0:T(128)S(1)}, s32[128]{0:T(128)}, u32[]{:S(2)}) copy-start(s32[128]{0:T(128)} %param.13) | copy-start | bytes 1540
  3.5 30.5 %all-to-all-start = ((bf16[8,528,128]{2,1,0:T(8,128)(2,1)}), bf16[8,528,128]{2,1,0:T(8,128)(2,1)S(1)}, u32[]{:S(2)}, u32[]{:S(2)}) async-start(bf16[8,528,128]{2,1,0:T(8,128)(2,1)} %shard_map.94), calls=%async_computation | async-start | bytes 2162688 | tf_op jit(solution)/shard_map/all_to_all | solution.py:246
  8.3 24.7 %collective-permute-start = (bf16[8,272,128]{2,1,0:T(8,128)(2,1)S(1)}, bf16[8,272,128]{2,1,0:T(8,128)(2,1)S(1)}, u32[]{:S(2)}, u32[]{:S(2)}) collective-permute-start(bf16[8,272,128]{2,1,0:T(8,128)(2,1)S(1)} %shard_map.95.second_ref), channel_id=1, source_target_pairs={{0,1},{1,2},{2,3},{3,4},{4,5},{5,6},{6,7},{7,8},{8,9},{9,10},{10,1... | collective-permute-start | bytes 1671176 | tf_op jit(solution)/shard_map/ppermute | solution.py:252
  34.0 20.7 %all-to-all-start.1 = ((bf16[8,528,128]{2,1,0:T(8,128)(2,1)}), bf16[8,528,128]{2,1,0:T(8,128)(2,1)S(1)}, u32[]{:S(2)}, u32[]{:S(2)}) async-start(bf16[8,528,128]{2,1,0:T(8,128)(2,1)} %shard_map.96), calls=%async_computation.1 | async-start | bytes 2162688 | tf_op jit(solution)/shard_map/all_to_all | solution.py:246
  38.4 28.2 %collective-permute-start.1 = (bf16[8,528,128]{2,1,0:T(8,128)(2,1)S(1)}, bf16[8,528,128]{2,1,0:T(8,128)(2,1)S(1)}, u32[]{:S(2)}, u32[]{:S(2)}) collective-permute-start(bf16[8,528,128]{2,1,0:T(8,128)(2,1)S(1)} %all-to-all-done.q_ref), channel_id=1, source_target_pairs={{1,0},{2,1},{3,2},{4,3},{5,4},{6,5},{7,6},{8,7},{9,8},{10,9},{11,1... | collective-permute-start | bytes 3244040 | tf_op jit(solution)/shard_map/ppermute | solution.py:252
  71.1 17.5 %collective-permute-start.2 = (bf16[8,256,128]{2,1,0:T(8,128)(2,1)S(1)}, bf16[8,256,128]{2,1,0:T(8,128)(2,1)S(1)}, u32[]{:S(2)}, u32[]{:S(2)}) collective-permute-start(bf16[8,256,128]{2,1,0:T(8,128)(2,1)S(1)} %get-tuple-element.12), channel_id=1, source_target_pairs={{0,1},{1,2},{2,3},{3,4},{4,5},{5,6},{6,7},{7,8},{8,9},{9,10},{10,1... | collective-permute-start | bytes 1572872 | tf_op jit(solution)/shard_map/ppermute | solution.py:252
  73.0 16.7 %collective-permute-start.3 = (bf16[8,256,128]{2,1,0:T(8,128)(2,1)S(1)}, bf16[8,256,128]{2,1,0:T(8,128)(2,1)S(1)}, u32[]{:S(2)}, u32[]{:S(2)}) collective-permute-start(bf16[8,256,128]{2,1,0:T(8,128)(2,1)S(1)} %get-tuple-element.14), channel_id=1, source_target_pairs={{1,0},{2,1},{3,2},{4,3},{5,4},{6,5},{7,6},{8,7},{9,8},{10,9},{11,1... | collective-permute-start | bytes 1572872 | tf_op jit(solution)/shard_map/ppermute | solution.py:252

commit v9 on v8

--- a/solution.py
+++ b/solution.py
@@ -155,10 +155,27 @@
             tile(q_ref, k_s, v_s, kid_s, lse_s, del_s, qid_s, dq_s, dkv_s, qb, kb, causal, qp)
 
 
+def walk_back(q_ref, kv_ref, first, ids, dq_s, dkv_s, k_s, v_s, kid_s, lse_s, del_s, qid_s):
+    fill_keys(kv_ref, first, ids, k_s, v_s, kid_s)
+    end = U * T // KB
+    for qb in range(U // QP):
+        front = matching(ids, qid_s[qb * QP, 0:1, 0:1], U)
+        back = matching(ids, qid_s[qb * QP + FAR_QP, 0:1, 0:1], U)
+        start = (U * T - front) // KB
+
+        @pl.loop(jnp.where(back > 0, start, end), end)
+        def _(kb, qb=qb):
+            tile(q_ref, k_s, v_s, kid_s, lse_s, del_s, qid_s, dq_s, dkv_s, qb, kb, False, QP)
+
+        @pl.loop(jnp.where(back > 0, end, start), end)
+        def _(kb, qb=qb):
+            tile(q_ref, k_s, v_s, kid_s, lse_s, del_s, qid_s, dq_s, dkv_s, 2 * qb, kb, False, FAR_QP)
+
+
 def prev_kernel(q_ref, kv_ref, dq_ref, dkv_ref, *scratch):
     start_sums(dq_ref, dkv_ref)
     fill_rows(q_ref, *scratch[3:])
-    walk(QP, q_ref, kv_ref, 0, (kv_ref, 2 * T, 0), False, dq_ref, dkv_ref, *scratch)
+    walk_back(q_ref, kv_ref, 0, (kv_ref, 2 * T, 0), dq_ref, dkv_ref, *scratch)
 
 
 def own_kernel(q_ref, kv_ref, sum_ref, dq_ref, dkv_ref, dq_s, *scratch):
@@ -187,7 +204,7 @@
         dq_s[...] = jnp.zeros_like(dq_s)
         dkv_s[...] = sum_ref[...]
         fill_rows(q_ref, *scratch[3:])
-        walk(FAR_QP, q_ref, prev_ref, 0, ids, False, dq_s, dkv_s, *scratch)
+        walk_back(q_ref, prev_ref, 0, ids, dq_s, dkv_s, *scratch)
         leave(dkv_s)
         for u in range(U):
             for h in range(2):

time: 111 us -> 111 us (level)
  transfers between devices with their start and end apart: 6 -> 6, of which waited for: 5 -> 5; matrix products, arithmetic and copies ran while one was open for 0% -> 0% of each run, Pallas kernels for 12% -> 13%
where the time goes in v9:
time: 111 us; the launch traced here: 110 us
  waiting for transfers between devices  43.4 us (39%)
  starting transfers between devices  24.4 us (22%)
  Pallas kernels  22 us (20%)
  blocking collectives  19.8 us (18%)
    ppermute x4, waiting for transfers between devices, moved(): return lax.ppermute(block, 'blk', route)  30.7 us
    all_to_all x1, blocking collectives, exchanged(): return lax.all_to_all(message, ULY, 0, 0, tiled=True)  19.8 us
    ppermute x4, starting transfers between devices, moved(): return lax.ppermute(block, 'blk', route)  15.4 us
    all_to_all x2, waiting for transfers between devices, exchanged(): return lax.all_to_all(message, ULY, 0, 0, tiled=True)  12.6 us
    all_to_all x2, starting transfers between devices, exchanged(): return lax.all_to_all(message, ULY, 0, 0, tiled=True)  9.02 us
    pallas_call x1, Pallas kernels, stages(): call(own_kernel, (tall, tall), (SUM_Q,) + KEYS, flops=4 << 30)  6.51 us
    pallas_call x1, Pallas kernels, stages(): dq, dprev = call(prev_kernel, (wide, tall), KEYS, flops=4 << 30)(rows, keys)  6.13 us
    pallas_call x1, Pallas kernels, stages(): call(far_kernel, (half, half), (SUM_Q, SUM_KV) + KEYS, flops=1 << 30)  3.9 us
  transfers between devices with their start and end apart: 6, of which 5 were waited for; matrix products, arithmetic and copies ran while one was open for 0% of the time, Pallas kernels for 13%

profile of v9, /device:TPU:2, one launch (start us, length us, event | category | flops | bytes accessed | tf_op | source)
XLA Modules:
  0.0 110.3 jit_solution(11035773683072981363)
XLA Ops:
  0.6 2.9 %shard_map.94 = bf16[8,528,128]{2,1,0:T(8,128)(2,1)} custom-call(bf16[128,2048]{1,0:T(8,128)(2,1)} %q_ref.1, bf16[128,2048]{1,0:T(8,128)(2,1)} %g_ref.1, bf16[128,2048]{1,0:T(8,128)(2,1)} %o_ref.1, f32[16,2,128]{2,1,0:T(2,128)} %bitcast.4, s32[1,128]{1,0:T(1,128)} %bitcast.2), custom_call_target="tpu_custom_call" | custom-call | flops 1048576 | bytes 1048576 | tf_op jit(solution)/shard_map/pallas_call | solution.py:283
  3.5 0.0 copy-start
  3.5 0.0 copy-start.1
  3.5 0.0 copy-start.2
  3.5 4.6 %all-to-all-start = ((bf16[8,528,128]{2,1,0:T(8,128)(2,1)}), bf16[8,528,128]{2,1,0:T(8,128)(2,1)S(1)}, u32[]{:S(2)}, u32[]{:S(2)}) async-start(bf16[8,528,128]{2,1,0:T(8,128)(2,1)} %shard_map.94), calls=%async_computation | async-start | bytes 2162688 | tf_op jit(solution)/shard_map/all_to_all | solution.py:263
  8.1 0.0 copy-done
  8.1 0.0 copy-done.1
  8.1 0.0 copy-done.2
  8.2 0.1 shard_map.95.second_ref
  8.3 3.8 %collective-permute-start = (bf16[8,272,128]{2,1,0:T(8,128)(2,1)S(1)}, bf16[8,272,128]{2,1,0:T(8,128)(2,1)S(1)}, u32[]{:S(2)}, u32[]{:S(2)}) collective-permute-start(bf16[8,272,128]{2,1,0:T(8,128)(2,1)S(1)} %shard_map.95.second_ref), channel_id=1, source_target_pairs={{0,1},{1,2},{2,3},{3,4},{4,5},{5,6},{6,7},{7,8},{8,9},{9,10},{10,1... | collective-permute-start | bytes 1671176 | tf_op jit(solution)/shard_map/ppermute | solution.py:269
  12.1 20.8 %collective-permute-done.first_ref = bf16[8,272,128]{2,1,0:T(8,128)(2,1)S(1)} collective-permute-done((bf16[8,272,128]{2,1,0:T(8,128)(2,1)S(1)}, bf16[8,272,128]{2,1,0:T(8,128)(2,1)S(1)}, u32[]{:S(2)}, u32[]{:S(2)}) %collective-permute-start) | collective-permute-done | bytes 557088 | tf_op jit(solution)/shard_map/ppermute | solution.py:269
  32.9 1.1 shard_map.96
  34.0 0.0 all-to-all-done.q_ref
  34.0 4.4 %all-to-all-start.1 = ((bf16[8,528,128]{2,1,0:T(8,128)(2,1)}), bf16[8,528,128]{2,1,0:T(8,128)(2,1)S(1)}, u32[]{:S(2)}, u32[]{:S(2)}) async-start(bf16[8,528,128]{2,1,0:T(8,128)(2,1)} %shard_map.96), calls=%async_computation.1 | async-start | bytes 2162688 | tf_op jit(solution)/shard_map/all_to_all | solution.py:263
  38.4 3.6 %collective-permute-start.1 = (bf16[8,528,128]{2,1,0:T(8,128)(2,1)S(1)}, bf16[8,528,128]{2,1,0:T(8,128)(2,1)S(1)}, u32[]{:S(2)}, u32[]{:S(2)}) collective-permute-start(bf16[8,528,128]{2,1,0:T(8,128)(2,1)S(1)} %all-to-all-done.q_ref), channel_id=1, source_target_pairs={{1,0},{2,1},{3,2},{4,3},{5,4},{6,5},{7,6},{8,7},{9,8},{10,9},{11,1... | collective-permute-start | bytes 3244040 | tf_op jit(solution)/shard_map/ppermute | solution.py:269
  42.1 12.6 %all-to-all-done.1.kv_ref.prev_ref = bf16[8,528,128]{2,1,0:T(8,128)(2,1)S(1)} async-done(((bf16[8,528,128]{2,1,0:T(8,128)(2,1)}), bf16[8,528,128]{2,1,0:T(8,128)(2,1)S(1)}, u32[]{:S(2)}, u32[]{:S(2)}) %all-to-all-start.1) | async-done | bytes 1081376 | tf_op jit(solution)/shard_map/all_to_all | solution.py:263
  54.7 6.1 %shard_map.97 = (f32[8,128,256]{2,1,0:T(8,128)S(1)}, f32[8,256,128]{2,1,0:T(8,128)S(1)}) custom-call(bf16[8,528,128]{2,1,0:T(8,128)(2,1)S(1)} %all-to-all-done.q_ref, bf16[8,528,128]{2,1,0:T(8,128)(2,1)S(1)} %all-to-all-done.1.kv_ref.prev_ref), custom_call_target="tpu_custom_call" | custom-call | flops 4294967296 | bytes 1048576 | tf_op jit(solution)/shard_map/pallas_call | solution.py:293
  60.8 5.7 %collective-permute-done.1.q_ref = bf16[8,528,128]{2,1,0:T(8,128)(2,1)S(1)} collective-permute-done((bf16[8,528,128]{2,1,0:T(8,128)(2,1)S(1)}, bf16[8,528,128]{2,1,0:T(8,128)(2,1)S(1)}, u32[]{:S(2)}, u32[]{:S(2)}) %collective-permute-start.1) | collective-permute-done | bytes 1081376 | tf_op jit(solution)/shard_map/ppermute | solution.py:269
  66.6 3.9 %shard_map.99 = (bf16[8,256,128]{2,1,0:T(8,128)(2,1)S(1)}, bf16[8,256,128]{2,1,0:T(8,128)(2,1)S(1)}) custom-call(bf16[8,528,128]{2,1,0:T(8,128)(2,1)S(1)} %collective-permute-done.1.q_ref, bf16[8,528,128]{2,1,0:T(8,128)(2,1)S(1)} %all-to-all-done.1.kv_ref.prev_ref, f32[8,256,128]{2,1,0:T(8,128)S(1)} %get-tuple-element.11.sum_ref), custom_call_target="tpu_custom_call" | custom-call | flops 1073741824 | bytes 1048576 | tf_op jit(solution)/shard_map/pallas_call | solution.py:294
  70.5 1.9 %collective-permute-start.2 = (bf16[8,256,128]{2,1,0:T(8,128)(2,1)S(1)}, bf16[8,256,128]{2,1,0:T(8,128)(2,1)S(1)}, u32[]{:S(2)}, u32[]{:S(2)}) collective-permute-start(bf16[8,256,128]{2,1,0:T(8,128)(2,1)S(1)} %get-tuple-element.12), channel_id=1, source_target_pairs={{0,1},{1,2},{2,3},{3,4},{4,5},{5,6},{6,7},{7,8},{8,9},{9,10},{10,1... | collective-permute-start | bytes 1572872 | tf_op jit(solution)/shard_map/ppermute | solution.py:269
  72.4 6.0 %collective-permute-start.3 = (bf16[8,256,128]{2,1,0:T(8,128)(2,1)S(1)}, bf16[8,256,128]{2,1,0:T(8,128)(2,1)S(1)}, u32[]{:S(2)}, u32[]{:S(2)}) collective-permute-start(bf16[8,256,128]{2,1,0:T(8,128)(2,1)S(1)} %get-tuple-element.14), channel_id=1, source_target_pairs={{1,0},{2,1},{3,2},{4,3},{5,4},{6,5},{7,6},{8,7},{9,8},{10,9},{11,1... | collective-permute-start | bytes 1572872 | tf_op jit(solution)/shard_map/ppermute | solution.py:269
  78.4 6.5 %shard_map.98 = (f32[8,256,128]{2,1,0:T(8,128)S(1)}, f32[8,256,128]{2,1,0:T(8,128)S(1)}) custom-call(bf16[8,528,128]{2,1,0:T(8,128)(2,1)S(1)} %all-to-all-done.q_ref, bf16[8,528,128]{2,1,0:T(8,128)(2,1)S(1)} %all-to-all-done.1.kv_ref.prev_ref, f32[8,128,256]{2,1,0:T(8,128)S(1)} %get-tuple-element.9.sum_ref), custom_call_target="tpu_custom_call" | custom-call | flops 4294967296 | bytes 1048576 | tf_op jit(solution)/shard_map/pallas_call | solution.py:297
  85.0 3.0 %collective-permute-done.2.more_q_ref = bf16[8,256,128]{2,1,0:T(8,128)(2,1)S(1)} collective-permute-done((bf16[8,256,128]{2,1,0:T(8,128)(2,1)S(1)}, bf16[8,256,128]{2,1,0:T(8,128)(2,1)S(1)}, u32[]{:S(2)}, u32[]{:S(2)}) %collective-permute-start.2) | collective-permute-done | bytes 524320 | tf_op jit(solution)/shard_map/ppermute | solution.py:269
  88.0 1.2 %collective-permute-done.3.more_kv_ref = bf16[8,256,128]{2,1,0:T(8,128)(2,1)S(1)} collective-permute-done((bf16[8,256,128]{2,1,0:T(8,128)(2,1)S(1)}, bf16[8,256,128]{2,1,0:T(8,128)(2,1)S(1)}, u32[]{:S(2)}, u32[]{:S(2)}) %collective-permute-start.3) | collective-permute-done | bytes 524320 | tf_op jit(solution)/shard_map/ppermute | solution.py:269
  89.1 0.2 shard_map.100
  89.3 19.8 %all_to_all.15.in_ref = bf16[8,512,128]{2,1,0:T(8,128)(2,1)S(1)} all-to-all(bf16[8,512,128]{2,1,0:T(8,128)(2,1)S(1)} %shard_map.100), channel_id=1, replica_groups=mesh['uly_0'=4,'uly_1'=2,'blk'=64] {'uly_0','uly_1'}, dimensions={0} | all-to-all | bytes 2097152 | tf_op jit(solution)/shard_map/all_to_all | solution.py:263
  109.1 1.2 %shard_map.101 = (bf16[128,2048]{1,0:T(8,128)(2,1)}, bf16[128,1024]{1,0:T(8,128)(2,1)}, bf16[128,1024]{1,0:T(8,128)(2,1)}) custom-call(bf16[8,512,128]{2,1,0:T(8,128)(2,1)S(1)} %all_to_all.15.in_ref), custom_call_target="tpu_custom_call" | custom-call | flops 1048576 | bytes 1048576 | tf_op jit(solution)/shard_map/pallas_call | solution.py:299
Async XLA Ops:
  3.5 4.6 %copy-start = (bf16[128,1024]{1,0:T(8,128)(2,1)S(1)}, bf16[128,1024]{1,0:T(8,128)(2,1)}, u32[]{:S(2)}) copy-start(bf16[128,1024]{1,0:T(8,128)(2,1)} %k_ref.1) | copy-start | bytes 786436
  3.5 4.6 %copy-start.1 = (bf16[128,1024]{1,0:T(8,128)(2,1)S(1)}, bf16[128,1024]{1,0:T(8,128)(2,1)}, u32[]{:S(2)}) copy-start(bf16[128,1024]{1,0:T(8,128)(2,1)} %v_ref.1) | copy-start | bytes 786436
  3.5 4.6 %copy-start.2 = (s32[128]{0:T(128)S(1)}, s32[128]{0:T(128)}, u32[]{:S(2)}) copy-start(s32[128]{0:T(128)} %param.13) | copy-start | bytes 1540
  3.5 30.5 %all-to-all-start = ((bf16[8,528,128]{2,1,0:T(8,128)(2,1)}), bf16[8,528,128]{2,1,0:T(8,128)(2,1)S(1)}, u32[]{:S(2)}, u32[]{:S(2)}) async-start(bf16[8,528,128]{2,1,0:T(8,128)(2,1)} %shard_map.94), calls=%async_computation | async-start | bytes 2162688 | tf_op jit(solution)/shard_map/all_to_all | solution.py:263
  8.3 24.7 %collective-permute-start = (bf16[8,272,128]{2,1,0:T(8,128)(2,1)S(1)}, bf16[8,272,128]{2,1,0:T(8,128)(2,1)S(1)}, u32[]{:S(2)}, u32[]{:S(2)}) collective-permute-start(bf16[8,272,128]{2,1,0:T(8,128)(2,1)S(1)} %shard_map.95.second_ref), channel_id=1, source_target_pairs={{0,1},{1,2},{2,3},{3,4},{4,5},{5,6},{6,7},{7,8},{8,9},{9,10},{10,1... | collective-permute-start | bytes 1671176 | tf_op jit(solution)/shard_map/ppermute | solution.py:269
  34.0 20.7 %all-to-all-start.1 = ((bf16[8,528,128]{2,1,0:T(8,128)(2,1)}), bf16[8,528,128]{2,1,0:T(8,128)(2,1)S(1)}, u32[]{:S(2)}, u32[]{:S(2)}) async-start(bf16[8,528,128]{2,1,0:T(8,128)(2,1)} %shard_map.96), calls=%async_computation.1 | async-start | bytes 2162688 | tf_op jit(solution)/shard_map/all_to_all | solution.py:263
  38.4 28.2 %collective-permute-start.1 = (bf16[8,528,128]{2,1,0:T(8,128)(2,1)S(1)}, bf16[8,528,128]{2,1,0:T(8,128)(2,1)S(1)}, u32[]{:S(2)}, u32[]{:S(2)}) collective-permute-start(bf16[8,528,128]{2,1,0:T(8,128)(2,1)S(1)} %all-to-all-done.q_ref), channel_id=1, source_target_pairs={{1,0},{2,1},{3,2},{4,3},{5,4},{6,5},{7,6},{8,7},{9,8},{10,9},{11,1... | collective-permute-start | bytes 3244040 | tf_op jit(solution)/shard_map/ppermute | solution.py:269
  70.5 17.5 %collective-permute-start.2 = (bf16[8,256,128]{2,1,0:T(8,128)(2,1)S(1)}, bf16[8,256,128]{2,1,0:T(8,128)(2,1)S(1)}, u32[]{:S(2)}, u32[]{:S(2)}) collective-permute-start(bf16[8,256,128]{2,1,0:T(8,128)(2,1)S(1)} %get-tuple-element.12), channel_id=1, source_target_pairs={{0,1},{1,2},{2,3},{3,4},{4,5},{5,6},{6,7},{7,8},{8,9},{9,10},{10,1... | collective-permute-start | bytes 1572872 | tf_op jit(solution)/shard_map/ppermute | solution.py:269
  72.4 16.7 %collective-permute-start.3 = (bf16[8,256,128]{2,1,0:T(8,128)(2,1)S(1)}, bf16[8,256,128]{2,1,0:T(8,128)(2,1)S(1)}, u32[]{:S(2)}, u32[]{:S(2)}) collective-permute-start(bf16[8,256,128]{2,1,0:T(8,128)(2,1)S(1)} %get-tuple-element.14), channel_id=1, source_target_pairs={{1,0},{2,1},{3,2},{4,3},{5,4},{6,5},{7,6},{8,7},{9,8},{10,9},{11,1... | collective-permute-start | bytes 1572872 | tf_op jit(solution)/shard_map/ppermute | solution.py:269
